TPU v7x, 32 devices: a whole 2x2x4 slice. The times are simulated.
32 devices in a mesh: ka: 16 (over z, x, core), sp: 2 (over y).
Axes of the slice: x: 2, y: 2, z: 4, core: 2. Of those that a mesh axis runs over, the one named last changes fastest.
Arguments:
- bloch_index: int32 [16, 2], P('ka'), may hold values from 0 to 63
- material: int32 [32, 64, 128], P('sp'), may hold values from 0 to 2
- permittivity: float32 [3], replicated, may hold values from 1 to 12
- absorption_peak: float32 [1], replicated, may hold values from 0.25 to 2
- source_sheet: float32 [16, 2, 32, 64], P('ka', None, 'sp'), may hold values from -6 to 6
- waveform: float32 [10], replicated, may hold values from -6 to 6
- electric_in: bfloat16 [16, 6, 32, 64, 128], P('ka', None, 'sp'), may hold values from -12 to 12
- magnetic_in: bfloat16 [16, 6, 32, 64, 128], P('ka', None, 'sp'), may hold values from -12 to 12
Outputs:
- electric_out: float32 [16, 6, 32, 64, 128], P('ka', None, 'sp')
- magnetic_out: float32 [16, 6, 32, 64, 128], P('ka', None, 'sp')
- reflected: float32 [16, 2], P('ka')
- reflected_mean: float32 [2], replicated
All inputs are finite; a program needn't handle non-finite values.
Results may differ from a plain program's by a relative error of at most 0.0003.
Values sent between devices are 32-bit elements; how exact they have to be, the bound alone decides.
No kernel may reach another device: no remote copies, remote signals or barrier semaphores. Data moves between devices by JAX's collectives and lax.ppermute only.
A program may use at most 64 MiB of HBM per device.

v0:
```python
import jax
import jax.numpy as jnp
from jax import lax
from jax.sharding import PartitionSpec as P

PML = 16
INTERVAL = 5
NSNAP = 2
MPHASE = 64
NMAT = 3


TIME_STEP = 0.5


def shifted_2(value, axis, steps):
    count = lax.axis_size(axis)
    pairs = [(source, (source + steps) % count) for source in range(count)]
    return lax.ppermute(value, axis, pairs)


def rotate(couple, cosine, sine):
    return (couple[0] * cosine - couple[1] * sine, couple[0] * sine + couple[1] * cosine)


def subtract(left, right):
    return (left[0] - right[0], left[1] - right[1])


def position(values, along):
    return lax.broadcasted_iota(jnp.int32, values.shape, along)


def roll_couple(couple, amount, along):
    return tuple((jnp.roll(values, amount, axis=along) for values in couple))


def above_cell(couple, beyond, along):
    length = couple[0].shape[along]
    rolled = roll_couple(couple, -1, along)
    last = position(couple[0], along) == length - 1
    return tuple((jnp.where(last, edge, moved) for edge, moved in zip(beyond, rolled)))


def below_cell(couple, beyond, along):
    rolled = roll_couple(couple, 1, along)
    first = position(couple[0], along) == 0
    return tuple((jnp.where(first, edge, moved) for edge, moved in zip(beyond, rolled)))


def forward_wrap(couple, along, cosine, sine):
    length = couple[0].shape[along]
    rolled = roll_couple(couple, -1, along)
    turned = rotate(rolled, cosine, sine)
    last = position(couple[0], along) == length - 1
    shifted = tuple((jnp.where(last, edge, moved) for edge, moved in zip(turned, rolled)))
    return subtract(shifted, couple)


def backward_wrap(couple, along, cosine, sine):
    rolled = roll_couple(couple, 1, along)
    turned = rotate(rolled, cosine, -sine)
    first = position(couple[0], along) == 0
    shifted = tuple((jnp.where(first, edge, moved) for edge, moved in zip(turned, rolled)))
    return subtract(couple, shifted)


def forward_open(couple):
    along = couple[0].ndim - 1
    length = couple[0].shape[along]
    rolled = roll_couple(couple, -1, along)
    last = position(couple[0], along) == length - 1
    shifted = tuple((jnp.where(last, 0.0, moved) for moved in rolled))
    return subtract(shifted, couple)


def backward_open(couple):
    along = couple[0].ndim - 1
    rolled = roll_couple(couple, 1, along)
    first = position(couple[0], along) == 0
    shifted = tuple((jnp.where(first, 0.0, moved) for moved in rolled))
    return subtract(couple, shifted)


def electric_curl(electric, beyond_y, beyond_z, cosine, sine):
    ex_part, ey_part, ez_part = electric
    across = ex_part[0].ndim - 3
    sideways = across + 1
    dx_ey = subtract(above_cell(ey_part, beyond_y, across), ey_part)
    dx_ez = subtract(above_cell(ez_part, beyond_z, across), ez_part)
    return (
        subtract(forward_wrap(ez_part, sideways, cosine, sine), forward_open(ey_part)),
        subtract(forward_open(ex_part), dx_ez),
        subtract(dx_ey, forward_wrap(ex_part, sideways, cosine, sine)),
    )


def magnetic_curl(magnetic, behind_y, behind_z, cosine, sine):
    hx_part, hy_part, hz_part = magnetic
    across = hx_part[0].ndim - 3
    sideways = across + 1
    bx_hy = subtract(hy_part, below_cell(hy_part, behind_y, across))
    bx_hz = subtract(hz_part, below_cell(hz_part, behind_z, across))
    return (
        subtract(backward_wrap(hz_part, sideways, cosine, sine), backward_open(hy_part)),
        subtract(backward_open(hx_part), bx_hz),
        subtract(bx_hy, backward_wrap(hx_part, sideways, cosine, sine)),
    )


def relax(couple, change, retain, factor):
    return (retain * couple[0] + factor * change[0], retain * couple[1] + factor * change[1])


def coefficients(material, permittivity, absorption_peak, depth):
    height = jnp.arange(depth, dtype=jnp.float32)
    low_depth = jnp.maximum(PML - height, 0.0) / PML
    high_depth = jnp.maximum(height - (depth - 1 - PML), 0.0) / PML
    conduct = absorption_peak[0] * (low_depth**3 + high_depth**3)
    half_mag = conduct * (0.5 * TIME_STEP)
    h_retain = (1.0 - half_mag) / (1.0 + half_mag)
    h_factor = -TIME_STEP / (1.0 + half_mag)
    relative = jnp.zeros(material.shape, jnp.float32)
    for level in range(NMAT):
        relative = relative + jnp.where(material == level, permittivity[level], 0.0)
    half_ele = conduct * (0.5 * TIME_STEP) / relative
    e_retain = (1.0 - half_ele) / (1.0 + half_ele)
    e_factor = TIME_STEP / relative / (1.0 + half_ele)
    return (e_retain, e_factor, h_retain, h_factor)


def split_plane(stacked, member):
    return (stacked[:, 2 * member : 2 * member + 1], stacked[:, 2 * member + 1 : 2 * member + 2])


def on_device(
    bloch_index,
    material,
    permittivity,
    absorption_peak,
    source_sheet,
    waveform,
    electric_in,
    magnetic_in,
):
    points = bloch_index.shape[0]
    rows, width, depth = material.shape
    e_retain, e_factor, h_retain, h_factor = coefficients(
        material, permittivity, absorption_peak, depth
    )
    plane = (jnp.arange(depth) == PML + 2).astype(jnp.float32)
    monitor = PML + 6
    angles = 2.0 * jnp.pi * bloch_index.astype(jnp.float32) / MPHASE
    cos_x = jnp.cos(angles[:, 0]).reshape(points, 1, 1, 1)
    sin_x = jnp.sin(angles[:, 0]).reshape(points, 1, 1, 1)
    cos_y = jnp.cos(angles[:, 1]).reshape(points, 1, 1, 1)
    sin_y = jnp.sin(angles[:, 1]).reshape(points, 1, 1, 1)
    slab = lax.axis_index("sp")
    slabs = lax.axis_size("sp")
    at_end = slab == slabs - 1
    at_start = slab == 0
    end_cos = jnp.where(at_end, cos_x, 1.0)
    end_sin = jnp.where(at_end, sin_x, 0.0)
    start_cos = jnp.where(at_start, cos_x, 1.0)
    start_sin = jnp.where(at_start, -sin_x, 0.0)
    sheet = (source_sheet[:, 0][..., None] * plane, source_sheet[:, 1][..., None] * plane)
    total_points = points * lax.axis_size("ka")
    cells_plane = rows * slabs * width

    def advance(fields, drive):
        electric, magnetic = fields
        front_plane = jnp.stack(
            [
                electric[1][0][:, 0],
                electric[1][1][:, 0],
                electric[2][0][:, 0],
                electric[2][1][:, 0],
            ],
            1,
        )
        received = shifted_2(front_plane, "sp", -1)
        beyond_y = rotate(split_plane(received, 0), end_cos, end_sin)
        beyond_z = rotate(split_plane(received, 1), end_cos, end_sin)
        change = electric_curl(electric, beyond_y, beyond_z, cos_y, sin_y)
        magnetic = tuple(
            (
                relax(couple, change_part, h_retain, h_factor)
                for couple, change_part in zip(magnetic, change)
            )
        )
        back_plane = jnp.stack(
            [
                magnetic[1][0][:, rows - 1],
                magnetic[1][1][:, rows - 1],
                magnetic[2][0][:, rows - 1],
                magnetic[2][1][:, rows - 1],
            ],
            1,
        )
        behind = shifted_2(back_plane, "sp", 1)
        behind_y = rotate(split_plane(behind, 0), start_cos, start_sin)
        behind_z = rotate(split_plane(behind, 1), start_cos, start_sin)
        change = magnetic_curl(magnetic, behind_y, behind_z, cos_y, sin_y)
        first_change = (change[0][0] - drive * sheet[0], change[0][1] - drive * sheet[1])
        change = (first_change, change[1], change[2])
        electric = tuple(
            (
                relax(couple, change_part, e_retain, e_factor)
                for couple, change_part in zip(electric, change)
            )
        )
        return (electric, magnetic)

    def snapshot(fields, index):
        fields = lax.fori_loop(
            0,
            INTERVAL,
            lambda inner, held: advance(held, waveform[index * INTERVAL + inner]),
            fields,
        )
        electric = fields[0]
        power = (
            electric[0][0][..., monitor] ** 2
            + electric[0][1][..., monitor] ** 2
            + electric[1][0][..., monitor] ** 2
            + electric[1][1][..., monitor] ** 2
        )
        partial_value = jnp.sum(power, (1, 2)) / cells_plane
        return (fields, partial_value)

    electric_wide = electric_in.astype(jnp.float32)
    magnetic_wide = magnetic_in.astype(jnp.float32)
    start_e = tuple(
        ((electric_wide[:, 2 * member], electric_wide[:, 2 * member + 1]) for member in range(3))
    )
    start_h = tuple(
        ((magnetic_wide[:, 2 * member], magnetic_wide[:, 2 * member + 1]) for member in range(3))
    )
    final, reports = lax.scan(snapshot, (start_e, start_h), jnp.arange(NSNAP))
    reflected = lax.psum(jnp.transpose(reports), "sp")
    reflected_mean = lax.psum(jnp.sum(reflected, 0) / total_points, "ka")
    electric, magnetic = final
    electric_out = jnp.stack([values for couple in electric for values in couple], 1)
    magnetic_out = jnp.stack([values for couple in magnetic for values in couple], 1)
    return (electric_out, magnetic_out, reflected, reflected_mean)


def solution(mesh):
    in_specs = (
        P("ka", None),
        P("sp", None, None),
        P(),
        P(),
        P("ka", None, "sp", None),
        P(),
        P("ka", None, "sp", None, None),
        P("ka", None, "sp", None, None),
    )
    out_specs = (
        P("ka", None, "sp", None, None),
        P("ka", None, "sp", None, None),
        P("ka", None),
        P(),
    )
    return jax.shard_map(
        on_device, mesh=mesh, in_specs=in_specs, out_specs=out_specs, check_vma=False
    )
```

profile of v0, /device:TPU:0, one launch (start us, length us, event | category | flops | bytes accessed | tf_op | source)
XLA Modules:
  0.0 468.7 jit_solution(13137554951830633101)
XLA Ops:
  0.6 1.9 convert_element_type.18
  3.0 1.9 slice_bitcast_fusion
  6.1 3.2 multiply_divide_fusion
  13.5 415.4 %while.90 = (s32[]{:T(128)}, f32[1,16,64,128]{3,2,1,0:T(8,128)S(1)}, f32[1,16,64,128]{3,2,1,0:T(8,128)S(1)}, f32[1,16,64,128]{3,2,1,0:T(8,128)S(1)}, f32[1,16,64...) while((s32[]{:T(128)}, ...), condition=%wide.region_4.5_spmd.clone.clone, body=%wide.region_0.4_spmd.clone.clone.sunk | while | flops 21113380 | bytes 123783040 | solution.py:239
  17.4 196.4 %while.91 = (s32[]{:T(128)}, f32[1,16,64,128]{3,2,1,0:T(8,128)S(1)}, f32[1,16,64,128]{3,2,1,0:T(8,128)S(1)}, f32[1,16,64,128]{3,2,1,0:T(8,128)S(1)}, f32[1,16,64...) while((s32[]{:T(128)}, ...), condition=%wide.region_2.2_spmd, body=%wide.region_1.1_spmd.sunk | while | flops 20840868 | bytes 118443480 | solution.py:215
  19.0 3.1 collective-permute-start
  40.9 2.8 fusion.98
  53.1 2.2 collective-permute-done.1
  79.1 2.8 fusion.98
  88.4 1.8 collective-permute-start.1
  98.1 1.8 collective-permute-start
  118.7 2.8 fusion.98
  131.0 2.0 collective-permute-done.1
  156.8 2.8 fusion.98
  166.1 1.8 collective-permute-start.1
  175.8 1.8 collective-permute-start
  196.4 2.8 fusion.98
  208.8 2.0 collective-permute-done.1
  225.8 194.9 %while.91 = (s32[]{:T(128)}, f32[1,16,64,128]{3,2,1,0:T(8,128)S(1)}, f32[1,16,64,128]{3,2,1,0:T(8,128)S(1)}, f32[1,16,64,128]{3,2,1,0:T(8,128)S(1)}, f32[1,16,64...) while((s32[]{:T(128)}, ...), condition=%wide.region_2.2_spmd, body=%wide.region_1.1_spmd.sunk | while | flops 20840868 | bytes 118443480 | solution.py:215
  246.6 2.8 fusion.98
  266.3 2.5 collective-permute-start
  287.6 2.8 fusion.98
  299.8 2.2 collective-permute-done.1
  325.6 2.8 fusion.98
  334.9 1.9 collective-permute-start.1
  344.6 1.9 collective-permute-start
  365.4 2.8 fusion.98
  377.6 2.1 collective-permute-done.1
  403.4 2.8 fusion.98
  412.7 1.9 collective-permute-start.1
  433.8 4.9 %psum.14 = f32[1,2]{1,0:T(1,128)S(1)} all-reduce(f32[1,2]{1,0:T(1,128)S(1)} %bitcast.218), channel_id=1, replica_groups=mesh['ka'=16,'sp'=2] {'sp'}, use_global_device_ids=true, to_apply=%region_5.6 | all-reduce | flops 2 | bytes 16 | tf_op jit(solution)/shard_map/psum | solution.py:240
  438.7 30.0 %psum.15 = f32[2]{0:T(128)} all-reduce(f32[2]{0:T(128)S(1)} %multiply_bitcast_fusion), channel_id=1, replica_groups=mesh['ka'=16,'sp'=2] {'ka'}, use_global_device_ids=true, to_apply=%region_6.7 | all-reduce | flops 2 | bytes 16 | tf_op jit(solution)/shard_map/psum | solution.py:241
  (1486 shorter events, 355.6 us)
Async XLA Ops:
  17.4 10.5 %copy-start.33 = (f32[128]{0:T(128)}, f32[128]{0:T(128)S(1)}, u32[]{:S(2)}) copy-start(f32[128]{0:T(128)S(1)} %get-tuple-element.1767) | copy-start | bytes 1540 | tf_op jit(solution)/shard_map/while/body/eval_jaxpr/while
  19.0 21.8 %collective-permute-start = (f32[1,4,64,128]{3,2,1,0:T(8,128)S(1)}, f32[1,4,64,128]{3,2,1,0:T(8,128)S(1)}, u32[]{:S(2)}, u32[]{:S(2)}) collective-permute-start(f32[1,4,64,128]{3,2,1,0:T(8,128)S(1)} %pad_maximum_fusion.12), channel_id=1, source_target_pairs={{0,1},{1,0},{2,3},{3,2},{4,5},{5,4},{6,7},{7,6},{8,9},{9,8},{10,11... | collective-permute-start | bytes 393224 | tf_op jit(solution)/shard_map/while/body/eval_jaxpr/while/body/eval_jaxpr/ppermute | solution.py:19
  46.6 11.0 %copy-start.3 = (f32[1,16,64,128]{3,2,1,0:T(8,128)}, f32[1,16,64,128]{3,2,1,0:T(8,128)S(1)}, u32[]{:S(2)}) copy-start(f32[1,16,64,128]{3,2,1,0:T(8,128)S(1)} %fusion.97) | copy-start | bytes 1572868 | tf_op jit(solution)/shard_map/while/body/eval_jaxpr/while
  50.2 5.0 %collective-permute-start.1 = (f32[1,4,64,128]{3,2,1,0:T(8,128)S(1)}, f32[1,4,64,128]{3,2,1,0:T(8,128)S(1)}, u32[]{:S(2)}, u32[]{:S(2)}) collective-permute-start(f32[1,4,64,128]{3,2,1,0:T(8,128)S(1)} %pad_maximum_fusion.13), channel_id=1, source_target_pairs={{0,1},{1,0},{2,3},{3,2},{4,5},{5,4},{6,7},{7,6},{8,9},{9,8},{10,11... | collective-permute-start | bytes 393224 | tf_op jit(solution)/shard_map/while/body/eval_jaxpr/while/body/eval_jaxpr/ppermute | solution.py:19
  59.9 19.1 %collective-permute-start = (f32[1,4,64,128]{3,2,1,0:T(8,128)S(1)}, f32[1,4,64,128]{3,2,1,0:T(8,128)S(1)}, u32[]{:S(2)}, u32[]{:S(2)}) collective-permute-start(f32[1,4,64,128]{3,2,1,0:T(8,128)S(1)} %pad_maximum_fusion.12), channel_id=1, source_target_pairs={{0,1},{1,0},{2,3},{3,2},{4,5},{5,4},{6,7},{7,6},{8,9},{9,8},{10,11... | collective-permute-start | bytes 393224 | tf_op jit(solution)/shard_map/while/body/eval_jaxpr/while/body/eval_jaxpr/ppermute | solution.py:19
  84.7 11.0 %copy-start.3 = (f32[1,16,64,128]{3,2,1,0:T(8,128)}, f32[1,16,64,128]{3,2,1,0:T(8,128)S(1)}, u32[]{:S(2)}) copy-start(f32[1,16,64,128]{3,2,1,0:T(8,128)S(1)} %fusion.97) | copy-start | bytes 1572868 | tf_op jit(solution)/shard_map/while/body/eval_jaxpr/while
  88.4 5.0 %collective-permute-start.1 = (f32[1,4,64,128]{3,2,1,0:T(8,128)S(1)}, f32[1,4,64,128]{3,2,1,0:T(8,128)S(1)}, u32[]{:S(2)}, u32[]{:S(2)}) collective-permute-start(f32[1,4,64,128]{3,2,1,0:T(8,128)S(1)} %pad_maximum_fusion.13), channel_id=1, source_target_pairs={{0,1},{1,0},{2,3},{3,2},{4,5},{5,4},{6,7},{7,6},{8,9},{9,8},{10,11... | collective-permute-start | bytes 393224 | tf_op jit(solution)/shard_map/while/body/eval_jaxpr/while/body/eval_jaxpr/ppermute | solution.py:19
  98.1 20.6 %collective-permute-start = (f32[1,4,64,128]{3,2,1,0:T(8,128)S(1)}, f32[1,4,64,128]{3,2,1,0:T(8,128)S(1)}, u32[]{:S(2)}, u32[]{:S(2)}) collective-permute-start(f32[1,4,64,128]{3,2,1,0:T(8,128)S(1)} %pad_maximum_fusion.12), channel_id=1, source_target_pairs={{0,1},{1,0},{2,3},{3,2},{4,5},{5,4},{6,7},{7,6},{8,9},{9,8},{10,11... | collective-permute-start | bytes 393224 | tf_op jit(solution)/shard_map/while/body/eval_jaxpr/while/body/eval_jaxpr/ppermute | solution.py:19
  124.3 11.0 %copy-start.3 = (f32[1,16,64,128]{3,2,1,0:T(8,128)}, f32[1,16,64,128]{3,2,1,0:T(8,128)S(1)}, u32[]{:S(2)}) copy-start(f32[1,16,64,128]{3,2,1,0:T(8,128)S(1)} %fusion.97) | copy-start | bytes 1572868 | tf_op jit(solution)/shard_map/while/body/eval_jaxpr/while
  128.0 5.0 %collective-permute-start.1 = (f32[1,4,64,128]{3,2,1,0:T(8,128)S(1)}, f32[1,4,64,128]{3,2,1,0:T(8,128)S(1)}, u32[]{:S(2)}, u32[]{:S(2)}) collective-permute-start(f32[1,4,64,128]{3,2,1,0:T(8,128)S(1)} %pad_maximum_fusion.13), channel_id=1, source_target_pairs={{0,1},{1,0},{2,3},{3,2},{4,5},{5,4},{6,7},{7,6},{8,9},{9,8},{10,11... | collective-permute-start | bytes 393224 | tf_op jit(solution)/shard_map/while/body/eval_jaxpr/while/body/eval_jaxpr/ppermute | solution.py:19
  137.7 19.1 %collective-permute-start = (f32[1,4,64,128]{3,2,1,0:T(8,128)S(1)}, f32[1,4,64,128]{3,2,1,0:T(8,128)S(1)}, u32[]{:S(2)}, u32[]{:S(2)}) collective-permute-start(f32[1,4,64,128]{3,2,1,0:T(8,128)S(1)} %pad_maximum_fusion.12), channel_id=1, source_target_pairs={{0,1},{1,0},{2,3},{3,2},{4,5},{5,4},{6,7},{7,6},{8,9},{9,8},{10,11... | collective-permute-start | bytes 393224 | tf_op jit(solution)/shard_map/while/body/eval_jaxpr/while/body/eval_jaxpr/ppermute | solution.py:19
  162.5 11.0 %copy-start.3 = (f32[1,16,64,128]{3,2,1,0:T(8,128)}, f32[1,16,64,128]{3,2,1,0:T(8,128)S(1)}, u32[]{:S(2)}) copy-start(f32[1,16,64,128]{3,2,1,0:T(8,128)S(1)} %fusion.97) | copy-start | bytes 1572868 | tf_op jit(solution)/shard_map/while/body/eval_jaxpr/while
  166.1 5.0 %collective-permute-start.1 = (f32[1,4,64,128]{3,2,1,0:T(8,128)S(1)}, f32[1,4,64,128]{3,2,1,0:T(8,128)S(1)}, u32[]{:S(2)}, u32[]{:S(2)}) collective-permute-start(f32[1,4,64,128]{3,2,1,0:T(8,128)S(1)} %pad_maximum_fusion.13), channel_id=1, source_target_pairs={{0,1},{1,0},{2,3},{3,2},{4,5},{5,4},{6,7},{7,6},{8,9},{9,8},{10,11... | collective-permute-start | bytes 393224 | tf_op jit(solution)/shard_map/while/body/eval_jaxpr/while/body/eval_jaxpr/ppermute | solution.py:19
  175.8 20.6 %collective-permute-start = (f32[1,4,64,128]{3,2,1,0:T(8,128)S(1)}, f32[1,4,64,128]{3,2,1,0:T(8,128)S(1)}, u32[]{:S(2)}, u32[]{:S(2)}) collective-permute-start(f32[1,4,64,128]{3,2,1,0:T(8,128)S(1)} %pad_maximum_fusion.12), channel_id=1, source_target_pairs={{0,1},{1,0},{2,3},{3,2},{4,5},{5,4},{6,7},{7,6},{8,9},{9,8},{10,11... | collective-permute-start | bytes 393224 | tf_op jit(solution)/shard_map/while/body/eval_jaxpr/while/body/eval_jaxpr/ppermute | solution.py:19
  202.1 11.0 %copy-start.3 = (f32[1,16,64,128]{3,2,1,0:T(8,128)}, f32[1,16,64,128]{3,2,1,0:T(8,128)S(1)}, u32[]{:S(2)}) copy-start(f32[1,16,64,128]{3,2,1,0:T(8,128)S(1)} %fusion.97) | copy-start | bytes 1572868 | tf_op jit(solution)/shard_map/while/body/eval_jaxpr/while
  205.7 5.0 %collective-permute-start.1 = (f32[1,4,64,128]{3,2,1,0:T(8,128)S(1)}, f32[1,4,64,128]{3,2,1,0:T(8,128)S(1)}, u32[]{:S(2)}, u32[]{:S(2)}) collective-permute-start(f32[1,4,64,128]{3,2,1,0:T(8,128)S(1)} %pad_maximum_fusion.13), channel_id=1, source_target_pairs={{0,1},{1,0},{2,3},{3,2},{4,5},{5,4},{6,7},{7,6},{8,9},{9,8},{10,11... | collective-permute-start | bytes 393224 | tf_op jit(solution)/shard_map/while/body/eval_jaxpr/while/body/eval_jaxpr/ppermute | solution.py:19
  227.5 19.1 %collective-permute-start = (f32[1,4,64,128]{3,2,1,0:T(8,128)S(1)}, f32[1,4,64,128]{3,2,1,0:T(8,128)S(1)}, u32[]{:S(2)}, u32[]{:S(2)}) collective-permute-start(f32[1,4,64,128]{3,2,1,0:T(8,128)S(1)} %pad_maximum_fusion.12), channel_id=1, source_target_pairs={{0,1},{1,0},{2,3},{3,2},{4,5},{5,4},{6,7},{7,6},{8,9},{9,8},{10,11... | collective-permute-start | bytes 393224 | tf_op jit(solution)/shard_map/while/body/eval_jaxpr/while/body/eval_jaxpr/ppermute | solution.py:19
  252.3 11.7 %copy-start.3 = (f32[1,16,64,128]{3,2,1,0:T(8,128)}, f32[1,16,64,128]{3,2,1,0:T(8,128)S(1)}, u32[]{:S(2)}) copy-start(f32[1,16,64,128]{3,2,1,0:T(8,128)S(1)} %fusion.97) | copy-start | bytes 1572868 | tf_op jit(solution)/shard_map/while/body/eval_jaxpr/while
  255.9 5.7 %collective-permute-start.1 = (f32[1,4,64,128]{3,2,1,0:T(8,128)S(1)}, f32[1,4,64,128]{3,2,1,0:T(8,128)S(1)}, u32[]{:S(2)}, u32[]{:S(2)}) collective-permute-start(f32[1,4,64,128]{3,2,1,0:T(8,128)S(1)} %pad_maximum_fusion.13), channel_id=1, source_target_pairs={{0,1},{1,0},{2,3},{3,2},{4,5},{5,4},{6,7},{7,6},{8,9},{9,8},{10,11... | collective-permute-start | bytes 393224 | tf_op jit(solution)/shard_map/while/body/eval_jaxpr/while/body/eval_jaxpr/ppermute | solution.py:19
  266.3 21.3 %collective-permute-start = (f32[1,4,64,128]{3,2,1,0:T(8,128)S(1)}, f32[1,4,64,128]{3,2,1,0:T(8,128)S(1)}, u32[]{:S(2)}, u32[]{:S(2)}) collective-permute-start(f32[1,4,64,128]{3,2,1,0:T(8,128)S(1)} %pad_maximum_fusion.12), channel_id=1, source_target_pairs={{0,1},{1,0},{2,3},{3,2},{4,5},{5,4},{6,7},{7,6},{8,9},{9,8},{10,11... | collective-permute-start | bytes 393224 | tf_op jit(solution)/shard_map/while/body/eval_jaxpr/while/body/eval_jaxpr/ppermute | solution.py:19
  293.3 11.0 %copy-start.3 = (f32[1,16,64,128]{3,2,1,0:T(8,128)}, f32[1,16,64,128]{3,2,1,0:T(8,128)S(1)}, u32[]{:S(2)}) copy-start(f32[1,16,64,128]{3,2,1,0:T(8,128)S(1)} %fusion.97) | copy-start | bytes 1572868 | tf_op jit(solution)/shard_map/while/body/eval_jaxpr/while
  296.9 5.0 %collective-permute-start.1 = (f32[1,4,64,128]{3,2,1,0:T(8,128)S(1)}, f32[1,4,64,128]{3,2,1,0:T(8,128)S(1)}, u32[]{:S(2)}, u32[]{:S(2)}) collective-permute-start(f32[1,4,64,128]{3,2,1,0:T(8,128)S(1)} %pad_maximum_fusion.13), channel_id=1, source_target_pairs={{0,1},{1,0},{2,3},{3,2},{4,5},{5,4},{6,7},{7,6},{8,9},{9,8},{10,11... | collective-permute-start | bytes 393224 | tf_op jit(solution)/shard_map/while/body/eval_jaxpr/while/body/eval_jaxpr/ppermute | solution.py:19
  306.6 19.0 %collective-permute-start = (f32[1,4,64,128]{3,2,1,0:T(8,128)S(1)}, f32[1,4,64,128]{3,2,1,0:T(8,128)S(1)}, u32[]{:S(2)}, u32[]{:S(2)}) collective-permute-start(f32[1,4,64,128]{3,2,1,0:T(8,128)S(1)} %pad_maximum_fusion.12), channel_id=1, source_target_pairs={{0,1},{1,0},{2,3},{3,2},{4,5},{5,4},{6,7},{7,6},{8,9},{9,8},{10,11... | collective-permute-start | bytes 393224 | tf_op jit(solution)/shard_map/while/body/eval_jaxpr/while/body/eval_jaxpr/ppermute | solution.py:19
  331.3 11.0 %copy-start.3 = (f32[1,16,64,128]{3,2,1,0:T(8,128)}, f32[1,16,64,128]{3,2,1,0:T(8,128)S(1)}, u32[]{:S(2)}) copy-start(f32[1,16,64,128]{3,2,1,0:T(8,128)S(1)} %fusion.97) | copy-start | bytes 1572868 | tf_op jit(solution)/shard_map/while/body/eval_jaxpr/while
  334.9 5.0 %collective-permute-start.1 = (f32[1,4,64,128]{3,2,1,0:T(8,128)S(1)}, f32[1,4,64,128]{3,2,1,0:T(8,128)S(1)}, u32[]{:S(2)}, u32[]{:S(2)}) collective-permute-start(f32[1,4,64,128]{3,2,1,0:T(8,128)S(1)} %pad_maximum_fusion.13), channel_id=1, source_target_pairs={{0,1},{1,0},{2,3},{3,2},{4,5},{5,4},{6,7},{7,6},{8,9},{9,8},{10,11... | collective-permute-start | bytes 393224 | tf_op jit(solution)/shard_map/while/body/eval_jaxpr/while/body/eval_jaxpr/ppermute | solution.py:19
  344.6 20.7 %collective-permute-start = (f32[1,4,64,128]{3,2,1,0:T(8,128)S(1)}, f32[1,4,64,128]{3,2,1,0:T(8,128)S(1)}, u32[]{:S(2)}, u32[]{:S(2)}) collective-permute-start(f32[1,4,64,128]{3,2,1,0:T(8,128)S(1)} %pad_maximum_fusion.12), channel_id=1, source_target_pairs={{0,1},{1,0},{2,3},{3,2},{4,5},{5,4},{6,7},{7,6},{8,9},{9,8},{10,11... | collective-permute-start | bytes 393224 | tf_op jit(solution)/shard_map/while/body/eval_jaxpr/while/body/eval_jaxpr/ppermute | solution.py:19
  371.1 11.0 %copy-start.3 = (f32[1,16,64,128]{3,2,1,0:T(8,128)}, f32[1,16,64,128]{3,2,1,0:T(8,128)S(1)}, u32[]{:S(2)}) copy-start(f32[1,16,64,128]{3,2,1,0:T(8,128)S(1)} %fusion.97) | copy-start | bytes 1572868 | tf_op jit(solution)/shard_map/while/body/eval_jaxpr/while
  374.7 5.0 %collective-permute-start.1 = (f32[1,4,64,128]{3,2,1,0:T(8,128)S(1)}, f32[1,4,64,128]{3,2,1,0:T(8,128)S(1)}, u32[]{:S(2)}, u32[]{:S(2)}) collective-permute-start(f32[1,4,64,128]{3,2,1,0:T(8,128)S(1)} %pad_maximum_fusion.13), channel_id=1, source_target_pairs={{0,1},{1,0},{2,3},{3,2},{4,5},{5,4},{6,7},{7,6},{8,9},{9,8},{10,11... | collective-permute-start | bytes 393224 | tf_op jit(solution)/shard_map/while/body/eval_jaxpr/while/body/eval_jaxpr/ppermute | solution.py:19
  384.4 19.0 %collective-permute-start = (f32[1,4,64,128]{3,2,1,0:T(8,128)S(1)}, f32[1,4,64,128]{3,2,1,0:T(8,128)S(1)}, u32[]{:S(2)}, u32[]{:S(2)}) collective-permute-start(f32[1,4,64,128]{3,2,1,0:T(8,128)S(1)} %pad_maximum_fusion.12), channel_id=1, source_target_pairs={{0,1},{1,0},{2,3},{3,2},{4,5},{5,4},{6,7},{7,6},{8,9},{9,8},{10,11... | collective-permute-start | bytes 393224 | tf_op jit(solution)/shard_map/while/body/eval_jaxpr/while/body/eval_jaxpr/ppermute | solution.py:19
  409.1 11.0 %copy-start.3 = (f32[1,16,64,128]{3,2,1,0:T(8,128)}, f32[1,16,64,128]{3,2,1,0:T(8,128)S(1)}, u32[]{:S(2)}) copy-start(f32[1,16,64,128]{3,2,1,0:T(8,128)S(1)} %fusion.97) | copy-start | bytes 1572868 | tf_op jit(solution)/shard_map/while/body/eval_jaxpr/while
  412.7 5.0 %collective-permute-start.1 = (f32[1,4,64,128]{3,2,1,0:T(8,128)S(1)}, f32[1,4,64,128]{3,2,1,0:T(8,128)S(1)}, u32[]{:S(2)}, u32[]{:S(2)}) collective-permute-start(f32[1,4,64,128]{3,2,1,0:T(8,128)S(1)} %pad_maximum_fusion.13), channel_id=1, source_target_pairs={{0,1},{1,0},{2,3},{3,2},{4,5},{5,4},{6,7},{7,6},{8,9},{9,8},{10,11... | collective-permute-start | bytes 393224 | tf_op jit(solution)/shard_map/while/body/eval_jaxpr/while/body/eval_jaxpr/ppermute | solution.py:19
  438.7 30.0 %copy-start.60 = (f32[1,2]{1,0:T(1,128)}, f32[1,2]{1,0:T(1,128)S(1)}, u32[]{:S(2)}) copy-start(f32[1,2]{1,0:T(1,128)S(1)} %psum.14) | copy-start | bytes 28
  (408 other events, 1731.2 us)
where the time goes:
time: 474 us; the launch traced here: 469 us
  local copies, waits for them, and re-layouts  230 us (49%)
  other arithmetic  153 us (32%)
  blocking collectives  34.9 us (7%)
  starting transfers between devices  23 us (5%)
  waiting for transfers between devices  13.4 us (3%)
  loops' own time  9.35 us (2%)
    slice x280, local copies, waits for them, and re-layouts, roll_couple(): return tuple((jnp.roll(values, amount, axis=along) for values in couple))  160 us
    add x60, other arithmetic, relax(): retain * couple[1] + factor * change[1]  70.4 us
    add x60, other arithmetic, relax(): retain * couple[0] + factor * change[0]  54.8 us
    psum x1, blocking collectives, on_device(): reflected_mean = lax.psum(jnp.sum(reflected, 0) / total_points, 'ka')  30 us
    ppermute x20, starting transfers between devices, shifted_2(): return lax.ppermute(value, axis, pairs)  23 us
    dynamic_slice x10, local copies, waits for them, and re-layouts, snapshot(): waveform[index * INTERVAL + inner]  13.7 us
    ppermute x20, waiting for transfers between devices, shifted_2(): return lax.ppermute(value, axis, pairs)  13.4 us
    while x8, local copies, waits for them, and re-layouts, snapshot(): lax.fori_loop(0, INTERVAL, lambda inner, held: advance(held, waveform[ind...  11.1 us
  transfers between devices with their start and end apart: 20, of which 10 were waited for; matrix products, arithmetic and copies ran while one was open for 45% of the time, Pallas kernels for 0%

commit v1 on v0

v1 whole, which is shorter than its diff:
```python
import functools

import jax
import jax.numpy as jnp
from jax import lax
from jax.experimental import pallas as pl
from jax.experimental.pallas import tpu as pltpu
from jax.sharding import PartitionSpec as P

PML = 16
INTERVAL = 5
NSNAP = 2
MPHASE = 64
NMAT = 3
TIME_STEP = 0.5
SUB = 8

VMEM = pl.BlockSpec(memory_space=pltpu.VMEM)
SMEM = pl.BlockSpec(memory_space=pltpu.SMEM)
HBM = pl.BlockSpec(memory_space=pl.ANY)
F32 = jnp.float32


def load(ref, *where):
    tiles = ref.shape[-2] // SUB
    return [ref[(*where, pl.ds(SUB * j, SUB))].astype(F32) for j in range(tiles)]


def load_couple(ref, member, *where):
    return (load(ref, 2 * member, *where), load(ref, 2 * member + 1, *where))


def store(ref, values, *where):
    for j, tile in enumerate(values):
        ref[(*where, pl.ds(SUB * j, SUB))] = tile


def store_couple(ref, couple, member, *where):
    store(ref, couple[0], 2 * member, *where)
    store(ref, couple[1], 2 * member + 1, *where)


def both(fn, *couples):
    return tuple(
        [fn(*tiles) for tiles in zip(*parts)] for parts in zip(*couples)
    )


def scaled(planes, fn, couple, *others):
    out = []
    for part in range(2):
        parts = [couple[part], *(other[part] for other in others)]
        out.append([fn(*tiles) for tiles in zip(*planes, *parts)])
    return tuple(out)


def turn(couple, cosine, sine):
    return (
        [re * cosine - im * sine for re, im in zip(*couple)],
        [re * sine + im * cosine for re, im in zip(*couple)],
    )


def next_y(couple, cosine, sine):
    rows = lax.broadcasted_iota(jnp.int32, couple[0][0].shape, 0)
    wrapped = turn((couple[0][:1], couple[1][:1]), cosine, sine)
    out = []
    for part, edge in zip(couple, wrapped):
        after = part[1:] + edge
        out.append(
            [
                pltpu.roll(jnp.where(rows == 0, there, here), SUB - 1, 0)
                for here, there in zip(part, after)
            ]
        )
    return tuple(out)


def prior_y(couple, cosine, sine):
    rows = lax.broadcasted_iota(jnp.int32, couple[0][0].shape, 0)
    wrapped = turn((couple[0][-1:], couple[1][-1:]), cosine, -sine)
    out = []
    for part, edge in zip(couple, wrapped):
        before = edge + part[:-1]
        out.append(
            [
                pltpu.roll(jnp.where(rows == SUB - 1, there, here), 1, 0)
                for here, there in zip(part, before)
            ]
        )
    return tuple(out)


def next_z(couple):
    depth = couple[0][0].shape[1]
    lanes = lax.broadcasted_iota(jnp.int32, couple[0][0].shape, 1)
    return both(
        lambda tile: jnp.where(lanes == depth - 1, 0.0, pltpu.roll(tile, depth - 1, 1)),
        couple,
    )


def prior_z(couple):
    lanes = lax.broadcasted_iota(jnp.int32, couple[0][0].shape, 1)
    return both(lambda tile: jnp.where(lanes == 0, 0.0, pltpu.roll(tile, 1, 1)), couple)


def h_coefs(ref):
    return ref[0], ref[1]


def new_hx(ey, ez, hx, keep, gain, cosine, sine):
    return both(
        lambda h, z_up, z, y_up, y: keep * h + gain * ((z_up - z) - (y_up - y)),
        hx,
        next_y(ez, cosine, sine),
        ez,
        next_z(ey),
        ey,
    )


def partial_h(ex, ey, ez, hy, hz, keep, gain, cosine, sine):
    part_y = both(
        lambda h, x_up, x, z: keep * h + gain * ((x_up - x) + z), hy, next_z(ex), ex, ez
    )
    part_z = both(
        lambda h, x_up, x, y: keep * h - gain * ((x_up - x) + y),
        hz,
        next_y(ex, cosine, sine),
        ex,
        ey,
    )
    return part_y, part_z


def close_h(part_y, part_z, ey_above, ez_above, gain):
    return (
        both(lambda h, z: h - gain * z, part_y, ez_above),
        both(lambda h, y: h + gain * y, part_z, ey_above),
    )


def h_row(e_ref, h_ref, x, keep, gain, cosine, sine, with_x=True):
    ex, ey, ez = (load_couple(e_ref, m, x) for m in range(3))
    ey_above, ez_above = (load_couple(e_ref, m, x + 1) for m in (1, 2))
    hx, hy, hz = (load_couple(h_ref, m, x) for m in range(3))
    new_x = new_hx(ey, ez, hx, keep, gain, cosine, sine)
    new_y = both(
        lambda h, x_up, x_, z_up, z: keep * h + gain * ((x_up - x_) - (z_up - z)),
        hy,
        next_z(ex),
        ex,
        ez_above,
        ez,
    )
    new_z = both(
        lambda h, y_up, y, x_up, x_: keep * h + gain * ((y_up - y) - (x_up - x_)),
        hz,
        ey_above,
        ey,
        next_y(ex, cosine, sine),
        ex,
    )
    store_couple(h_ref, new_x, 0, x)
    store_couple(h_ref, new_y, 1, x)
    store_couple(h_ref, new_z, 2, x)


def new_e(e, h, hy_below, hz_below, retain, factor, sheet, drive, cosine, sine):
    ex, ey, ez = e
    hx, hy, hz = h
    drive_x = both(lambda s: drive * s, sheet)
    new_x = scaled(
        (retain, factor),
        lambda r, f, e_, z, z_dn, y, y_dn, s: r * e_ + f * ((z - z_dn) - (y - y_dn) - s),
        ex,
        hz,
        prior_y(hz, cosine, sine),
        hy,
        prior_z(hy),
        drive_x,
    )
    new_y = scaled(
        (retain, factor),
        lambda r, f, e_, x, x_dn, z, z_dn: r * e_ + f * ((x - x_dn) - (z - z_dn)),
        ey,
        hx,
        prior_z(hx),
        hz,
        hz_below,
    )
    new_z = scaled(
        (retain, factor),
        lambda r, f, e_, y, y_dn, x, x_dn: r * e_ + f * ((y - y_dn) - (x - x_dn)),
        ez,
        hy,
        hy_below,
        hx,
        prior_y(hx, cosine, sine),
    )
    return new_x, new_y, new_z


def e_row(e_ref, h_ref, c_ref, sheet_ref, x, drive, cosine, sine, below=None):
    e = [load_couple(e_ref, m, x) for m in range(3)]
    h = [load_couple(h_ref, m, x) for m in range(3)]
    if below is None:
        below = [load_couple(h_ref, m, x - 1) for m in (1, 2)]
    retain, factor = load(c_ref, 0, x), load(c_ref, 1, x)
    sheet = (load(sheet_ref, 0, x), load(sheet_ref, 1, x))
    new = new_e(e, h, *below, retain, factor, sheet, drive, cosine, sine)
    for m in range(3):
        store_couple(e_ref, new[m], m, x)
    return new


def first_kernel(bloch_ref, hc_ref, e_hbm, h_hbm, d_ref, s_ref, low, high, mag, sems):
    rows = e_hbm.shape[1]
    copies = [
        pltpu.make_async_copy(e_hbm.at[pl.ds(2, 4), 0], low, sems.at[0]),
        pltpu.make_async_copy(e_hbm.at[:, rows - 1], high, sems.at[1]),
        pltpu.make_async_copy(h_hbm.at[pl.ds(2, 4), rows - 1], mag, sems.at[2]),
    ]
    for copy in copies:
        copy.start()
    cosine, sine = bloch_ref[0], bloch_ref[1]
    keep, gain = h_coefs(hc_ref)
    copies[0].wait()
    d_ref[...] = low[...].astype(F32)
    copies[1].wait()
    copies[2].wait()
    ex, ey, ez = (load_couple(high, m) for m in range(3))
    hy, hz = (load_couple(mag, m) for m in range(2))
    part_y, part_z = partial_h(ex, ey, ez, hy, hz, keep, gain, cosine, sine)
    store_couple(s_ref, part_y, 0)
    store_couple(s_ref, part_z, 1)


def widen_kernel(peak_ref, perm_ref, mat_ref, ein_ref, hin_ref, e_ref, h_ref, c_ref):
    rows, width, depth = mat_ref.shape
    conduct = conductivity(peak_ref[0], (width, depth))

    def one_row(x, carry):
        for m in range(6):
            e_ref[m, x] = ein_ref[m, x].astype(F32)
            h_ref[m, x] = hin_ref[m, x].astype(F32)
        level = mat_ref[x]
        relative = jnp.zeros((width, depth), F32)
        for index in range(NMAT):
            relative = jnp.where(level == index, perm_ref[index], relative)
        half = conduct * (0.5 * TIME_STEP) / relative
        c_ref[0, x] = (1.0 - half) / (1.0 + half)
        c_ref[1, x] = TIME_STEP / relative / (1.0 + half)
        return carry

    lax.fori_loop(0, rows, one_row, 0)


def conductivity(peak, shape):
    depth = shape[-1]
    height = lax.broadcasted_iota(jnp.int32, shape, len(shape) - 1).astype(F32)
    low = jnp.maximum(PML - height, 0.0) / PML
    high = jnp.maximum(height - (depth - 1 - PML), 0.0) / PML
    return peak * (low * low * low + high * high * high)


def inner_kernel(
    lo, hi, step, bloch_ref, wave_ref, hc_ref, c_ref, sheet_ref, e_in, h_in, e_ref, h_ref
):
    rows = e_ref.shape[1]
    cosine, sine, drive = bloch_ref[0], bloch_ref[1], wave_ref[step]
    keep, gain = h_coefs(hc_ref)
    top = hi == rows - 1

    h_row(e_ref, h_ref, lo, keep, gain, cosine, sine)
    h_row(e_ref, h_ref, lo + 1, keep, gain, cosine, sine)

    def one_row(x, carry):
        h_row(e_ref, h_ref, x + 1, keep, gain, cosine, sine)
        e_row(e_ref, h_ref, c_ref, sheet_ref, x, drive, cosine, sine)
        return carry

    lax.fori_loop(lo + 1, hi - 1, one_row, 0)
    e_row(e_ref, h_ref, c_ref, sheet_ref, hi - 1, drive, cosine, sine)
    if top:
        ey, ez = (load_couple(e_ref, m, rows - 1) for m in (1, 2))
        hx = load_couple(h_ref, 0, rows - 1)
        store_couple(h_ref, new_hx(ey, ez, hx, keep, gain, cosine, sine), 0, rows - 1)
    else:
        e_row(e_ref, h_ref, c_ref, sheet_ref, hi, drive, cosine, sine)


def upper_kernel(
    step, bloch_ref, wave_ref, hc_ref, c_ref, sheet_ref, s_ref, d_ref, e_in, h_in,
    e_ref, h_ref, out_ref,
):
    x = e_ref.shape[1] - 1
    cosine, sine, drive = bloch_ref[0], bloch_ref[1], wave_ref[step]
    keep, gain = h_coefs(hc_ref)
    part_y, part_z = (load_couple(s_ref, m) for m in range(2))
    ey_above, ez_above = (
        turn(load_couple(d_ref, m), bloch_ref[2], bloch_ref[3]) for m in range(2)
    )
    hy, hz = close_h(part_y, part_z, ey_above, ez_above, gain)
    store_couple(h_ref, hy, 1, x)
    store_couple(h_ref, hz, 2, x)
    ex, ey, ez = e_row(e_ref, h_ref, c_ref, sheet_ref, x, drive, cosine, sine)
    part_y, part_z = partial_h(ex, ey, ez, hy, hz, keep, gain, cosine, sine)
    store_couple(out_ref, part_y, 0)
    store_couple(out_ref, part_z, 1)


def lower_kernel(
    step, bloch_ref, wave_ref, hc_ref, c_ref, sheet_ref, s_ref, e_in, h_in,
    e_ref, out_ref,
):
    cosine, sine, drive = bloch_ref[0], bloch_ref[1], wave_ref[step]
    _, gain = h_coefs(hc_ref)
    part_y, part_z = (
        turn(load_couple(s_ref, m), bloch_ref[4], bloch_ref[5]) for m in range(2)
    )
    ey, ez = (load_couple(e_ref, m, 0) for m in (1, 2))
    below = close_h(part_y, part_z, ey, ez, gain)
    _, ey, ez = e_row(e_ref, h_in, c_ref, sheet_ref, 0, drive, cosine, sine, below)
    store_couple(out_ref, ey, 0)
    store_couple(out_ref, ez, 1)


def power_kernel(slot, scale, lo, hi, e_ref, old_ref, out_ref):
    depth = e_ref.shape[-1]

    def one_row(x, total):
        for m in range(4):
            for tile in load(e_ref, m, x):
                total = total + tile * tile
        return total

    total = lax.fori_loop(lo, hi, one_row, jnp.zeros((SUB, depth), F32))
    lanes = lax.broadcasted_iota(jnp.int32, (SUB, depth), 1)
    total = jnp.where(lanes == PML + 6, total, 0.0)
    total = jnp.sum(jnp.sum(total, 0, keepdims=True), 1, keepdims=True) * scale
    out_ref[...] = old_ref[...] + jnp.where(lanes == slot, total, 0.0)


def finish_kernel(e_ref, h_ref, e_out, h_out, sems):
    copies = [
        pltpu.make_async_copy(e_ref, e_out, sems.at[0]),
        pltpu.make_async_copy(h_ref, h_out, sems.at[1]),
    ]
    for copy in copies:
        copy.start()
    for copy in copies:
        copy.wait()


def add_kernel(scale, *refs):
    total = refs[0][...]
    for ref in refs[1:-1]:
        total = total + ref[...]
    refs[-1][...] = total * scale if scale != 1.0 else total


def nbytes(shape):
    size = 4
    for extent in shape:
        size *= extent
    return size


def call(kernel, outs, ins, specs, aliases=None, scratch=(), flops=0, vmem=16):
    return pl.pallas_call(
        kernel,
        out_shape=tuple(pltpu.VMEM(shape, F32) for shape in outs),
        in_specs=specs,
        out_specs=tuple(VMEM for _ in outs),
        input_output_aliases=aliases or {},
        scratch_shapes=scratch,
        cost_estimate=pl.CostEstimate(flops=flops, bytes_accessed=0, transcendentals=0),
        compiler_params=pltpu.CompilerParams(vmem_limit_bytes=vmem * 2**20),
    )(*ins)


def shift(value, axis, steps):
    count = lax.axis_size(axis)
    return lax.ppermute(value, axis, [(i, (i + steps) % count) for i in range(count)])


def total_over(value, axis, scale=1.0):
    count = lax.axis_size(axis)
    shape = value.shape
    if count & (count - 1):
        parts = [value] + [shift(value, axis, step) for step in range(1, count)]
        return call(functools.partial(add_kernel, scale), [shape], parts, [VMEM] * count)[0]
    step = 1
    while step < count:
        other = lax.ppermute(value, axis, [(i, i ^ step) for i in range(count)])
        step *= 2
        last = scale if step >= count else 1.0
        value = call(
            functools.partial(add_kernel, last), [shape], [value, other], [VMEM] * 2
        )[0]
    return value


def on_device(
    bloch_index,
    material,
    permittivity,
    absorption_peak,
    source_sheet,
    waveform,
    electric_in,
    magnetic_in,
):
    points = bloch_index.shape[0]
    rows, width, depth = material.shape
    steps = waveform.shape[0]
    slab = lax.axis_index("sp")
    slabs = lax.axis_size("sp")
    total_points = points * lax.axis_size("ka")
    cells_plane = rows * slabs * width

    angles = 2.0 * jnp.pi * bloch_index.astype(F32) / MPHASE
    at_end = slab == slabs - 1
    at_start = slab == 0
    cosines, sines = jnp.cos(angles), jnp.sin(angles)
    half_mag = conductivity(absorption_peak[0], (SUB, depth)) * (0.5 * TIME_STEP)
    hc = jnp.stack([(1.0 - half_mag) / (1.0 + half_mag), -TIME_STEP / (1.0 + half_mag)])
    plane = (jnp.arange(depth) == PML + 2).astype(F32)
    sheets = source_sheet[..., None] * plane

    results = []
    for point in range(points):
        cos_x, cos_y = cosines[point, 0], cosines[point, 1]
        sin_x, sin_y = sines[point, 0], sines[point, 1]
        bloch = jnp.stack(
            [
                cos_y,
                sin_y,
                jnp.where(at_end, cos_x, 1.0),
                jnp.where(at_end, sin_x, 0.0),
                jnp.where(at_start, cos_x, 1.0),
                jnp.where(at_start, -sin_x, 0.0),
            ]
        )
        results.append(
            one_point(
                bloch, hc, sheets[point], waveform, material, permittivity,
                absorption_peak, electric_in[point], magnetic_in[point],
                steps, 1.0 / cells_plane,
            )
        )
    electric, magnetic, powers = zip(*results)
    sums = [total_over(power, "sp") for power in powers]
    local = sums[0]
    for other in sums[1:]:
        local = local + other
    mean = total_over(local, "ka", 1.0 / total_points)
    return (
        jnp.stack(electric),
        jnp.stack(magnetic),
        jnp.stack([total[0, :NSNAP] for total in sums]),
        mean[0, :NSNAP],
    )


def one_point(
    bloch, hc, sheet, waveform, material, permittivity, peak, electric_in, magnetic_in,
    steps, scale,
):
    rows, width, depth = material.shape
    edge = (4, width, depth)
    full = (6, rows, width, depth)
    middle = rows // 2
    mine_d, mine_s = call(
        first_kernel,
        [edge, edge],
        [bloch, hc, electric_in, magnetic_in],
        [SMEM, VMEM, HBM, HBM],
        scratch=[
            pltpu.VMEM((4, width, depth), electric_in.dtype),
            pltpu.VMEM((6, width, depth), electric_in.dtype),
            pltpu.VMEM((4, width, depth), electric_in.dtype),
            pltpu.SemaphoreType.DMA((3,)),
        ],
    )
    their_d = shift(mine_d, "sp", -1)
    their_s = shift(mine_s, "sp", 1)
    e, h, c = call(
        widen_kernel,
        [full, full, (2, rows, width, depth)],
        [peak, permittivity, material, electric_in, magnetic_in],
        [SMEM, SMEM, VMEM, VMEM, VMEM],
    )
    power = jnp.zeros((SUB, depth), F32)

    def inner(lo, hi, step, e, h):
        return call(
            functools.partial(inner_kernel, lo, hi, step),
            [full, full],
            [bloch, waveform, hc, c, sheet, e, h],
            [SMEM, SMEM] + [VMEM] * 5,
            {5: 0, 6: 1},
        )

    def measured(lo, hi, step, power, e):
        if (step + 1) % INTERVAL:
            return power
        return call(
            functools.partial(power_kernel, step // INTERVAL, scale, lo, hi),
            [(SUB, depth)],
            [e, power],
            [VMEM, VMEM],
        )[0]

    e, h = inner(middle, rows - 1, 0, e, h)
    e, h = inner(0, middle, 0, e, h)
    for step in range(steps):
        e, h, next_s = call(
            functools.partial(upper_kernel, step),
            [full, full, edge],
            [bloch, waveform, hc, c, sheet, mine_s, their_d, e, h],
            [SMEM, SMEM] + [VMEM] * 7,
            {7: 0, 8: 1},
        )
        last = step == steps - 1
        power = measured(middle + 1, rows, step, power, e)
        if not last:
            next_their_s = shift(next_s, "sp", 1)
            e, h = inner(middle, rows - 1, step + 1, e, h)
        e, mine_d = call(
            functools.partial(lower_kernel, step),
            [full, edge],
            [bloch, waveform, hc, c, sheet, their_s, e, h],
            [SMEM, SMEM] + [VMEM] * 6,
            {6: 0},
        )
        if not last:
            their_d = shift(mine_d, "sp", -1)
            mine_s, their_s = next_s, next_their_s
        power = measured(0, middle + 1, step, power, e)
        if not last:
            e, h = inner(0, middle, step + 1, e, h)
    whole = jax.ShapeDtypeStruct(full, F32)
    e, h = pl.pallas_call(
        finish_kernel,
        out_shape=(whole, whole),
        in_specs=[VMEM, VMEM],
        out_specs=(HBM, HBM),
        scratch_shapes=[pltpu.SemaphoreType.DMA((2,))],
        compiler_params=pltpu.CompilerParams(vmem_limit_bytes=2**20),
    )(e, h)
    return e, h, power


def solution(mesh):
    in_specs = (
        P("ka", None),
        P("sp", None, None),
        P(),
        P(),
        P("ka", None, "sp", None),
        P(),
        P("ka", None, "sp", None, None),
        P("ka", None, "sp", None, None),
    )
    out_specs = (
        P("ka", None, "sp", None, None),
        P("ka", None, "sp", None, None),
        P("ka", None),
        P(),
    )
    return jax.shard_map(
        on_device, mesh=mesh, in_specs=in_specs, out_specs=out_specs, check_vma=False
    )
```

time: 474 us -> 117 us (0.25); the launches traced: 469 us -> 117 us
  local copies, waits for them, and re-layouts: 230 us -> 5.85 us
  other arithmetic: 153 us -> 1.05 us
  Pallas kernels: 0 us -> 56.5 us
  blocking collectives: 34.9 us -> 0 us
  loops' own time: 9.35 us -> 0 us
  waiting for transfers between devices: 13.4 us -> 20.3 us
  starting transfers between devices: 23 us -> 28.9 us
    slice x362 -> x2, local copies, waits for them, and re-layouts: 185 us -> 1.11 us  [the longest x1 0.59 us: on_device(): sin_x, sin_y = (sines[point, 0], sines[point, 1])]
    add x120 -> x0, other arithmetic: 125 us -> none  [the longest x60 70.4 us: relax(): retain * couple[1] + factor * change[1]]
    pallas_call x0 -> x52, Pallas kernels: none -> 56.5 us  [the longest x51 53.8 us: call(): pl.pallas_call(kernel, out_shape=tuple((pltpu.VMEM(shape, F32) for shape...]
    psum x2 -> x0, blocking collectives: 34.9 us -> none  [the longest x1 30 us: on_device(): reflected_mean = lax.psum(jnp.sum(reflected, 0) / total_points, 'ka')]
    while x820 -> x0, local copies, waits for them, and re-layouts: 21.8 us -> none  [the longest x8 11.1 us: snapshot(): lax.fori_loop(0, INTERVAL, lambda inner, held: advance(held, waveform[ind...]
    dynamic_slice x12 -> x0, local copies, waits for them, and re-layouts: 16.3 us -> none  [the longest x10 13.7 us: snapshot(): waveform[index * INTERVAL + inner]]
    eq x60 -> x0, other arithmetic: 15.1 us -> none  [the longest x10 5.23 us: below_cell(): first = position(couple[0], along) == 0]
    another operation x3 -> x0, loops' own time: 9.35 us -> none  [the longest x2 6.81 us: snapshot(): lax.fori_loop(0, INTERVAL, lambda inner, held: advance(held, waveform[ind...]
  transfers between devices with their start and end apart: 20 -> 25, of which waited for: 10 -> 17; matrix products, arithmetic and copies ran while one was open for 45% -> 1% of each run, Pallas kernels for 0% -> 41%
where the time goes in v1:
time: 117 us
  Pallas kernels  56.5 us (48%)
  starting transfers between devices  28.9 us (25%)
  waiting for transfers between devices  20.3 us (17%)
  local copies, waits for them, and re-layouts  5.85 us (5%)
  between operations  4.3 us (4%)
    pallas_call x51, Pallas kernels, call(): pl.pallas_call(kernel, out_shape=tuple((pltpu.VMEM(shape, F32) for shape...  53.8 us
    ppermute x20, starting transfers between devices, shift(): lax.ppermute(value, axis, [(i, (i + steps) % count) for i in range(count)])  22 us
    ppermute x20, waiting for transfers between devices, shift(): lax.ppermute(value, axis, [(i, (i + steps) % count) for i in range(count)])  12.6 us
    ppermute x5, waiting for transfers between devices, total_over(): other = lax.ppermute(value, axis, [(i, i ^ step) for i in range(count)])  7.66 us
    ppermute x5, starting transfers between devices, total_over(): other = lax.ppermute(value, axis, [(i, i ^ step) for i in range(count)])  6.92 us
    unnamed x14, local copies, waits for them, and re-layouts  2.84 us
    pallas_call x1, Pallas kernels, one_point(): pl.pallas_call(finish_kernel, out_shape=(whole, whole), in_specs=[VMEM, V...  2.71 us
  transfers between devices with their start and end apart: 25, of which 17 were waited for; matrix products, arithmetic and copies ran while one was open for 1% of the time, Pallas kernels for 41%

profile of v1, /device:TPU:0, one launch (start us, length us, event | category | flops | bytes accessed | tf_op | source)
XLA Modules:
  0.0 116.9 jit_solution(16660829069925116229)
XLA Ops:
  10.2 3.1 %collective-permute-start = (f32[4,64,128]{2,1,0:T(8,128)S(1)}, f32[4,64,128]{2,1,0:T(8,128)S(1)}, u32[]{:S(2)}, u32[]{:S(2)}) collective-permute-start(f32[4,64,128]{2,1,0:T(8,128)S(1)} %get-tuple-element.101), channel_id=1, source_target_pairs={{0,1},{1,0},{2,3},{3,2},{4,5},{5,4},{6,7},{7,6},{8,9},{9,8},{10,11... | collective-permute-start | bytes 393224 | tf_op jit(solution)/shard_map/ppermute | solution.py:386
  14.9 1.7 %shard_map.113 = (f32[6,16,64,128]{3,2,1,0:T(8,128)S(1)}, f32[6,16,64,128]{3,2,1,0:T(8,128)S(1)}) custom-call(f32[6]{0:T(128)S(1)} %stack.30.bloch_ref, f32[10]{0:T(128)S(1)} %copy-done.3, f32[2,8,128]{2,1,0:T(8,128)S(1)} %pad_maximum_fusion.hc_ref, f32[2,16,64,128]{3,2,1,0:T(8,128)S(1)} %get-tuple-element.99.c_ref, ...), custom_call_target="tpu_custom_call", output_to_operand_aliasing={{0}: (5, {}), {1}: (6, {})} | custom-call | tf_op jit(solution)/shard_map/pallas_call | solution.py:372
  16.6 1.9 %shard_map.114 = (f32[6,16,64,128]{3,2,1,0:T(8,128)S(1)}, f32[6,16,64,128]{3,2,1,0:T(8,128)S(1)}) custom-call(f32[6]{0:T(128)S(1)} %stack.30.bloch_ref, f32[10]{0:T(128)S(1)} %copy-done.3, f32[2,8,128]{2,1,0:T(8,128)S(1)} %pad_maximum_fusion.hc_ref, f32[2,16,64,128]{3,2,1,0:T(8,128)S(1)} %get-tuple-element.99.c_ref, ...), custom_call_target="tpu_custom_call", output_to_operand_aliasing={{0}: (5, {}), {1}: (6, {})} | custom-call | tf_op jit(solution)/shard_map/pallas_call | solution.py:372
  19.2 1.7 %shard_map.116 = (f32[6,16,64,128]{3,2,1,0:T(8,128)S(1)}, f32[6,16,64,128]{3,2,1,0:T(8,128)S(1)}) custom-call(f32[6]{0:T(128)S(1)} %stack.30.bloch_ref, f32[10]{0:T(128)S(1)} %copy-done.3, f32[2,8,128]{2,1,0:T(8,128)S(1)} %pad_maximum_fusion.hc_ref, f32[2,16,64,128]{3,2,1,0:T(8,128)S(1)} %get-tuple-element.99.c_ref, ...), custom_call_target="tpu_custom_call", output_to_operand_aliasing={{0}: (5, {}), {1}: (6, {})} | custom-call | tf_op jit(solution)/shard_map/pallas_call | solution.py:372
  21.6 2.0 %collective-permute-start.2 = (f32[4,64,128]{2,1,0:T(8,128)S(1)}, f32[4,64,128]{2,1,0:T(8,128)S(1)}, u32[]{:S(2)}, u32[]{:S(2)}) collective-permute-start(f32[4,64,128]{2,1,0:T(8,128)S(1)} %get-tuple-element.113), channel_id=1, source_target_pairs={{0,1},{1,0},{2,3},{3,2},{4,5},{5,4},{6,7},{7,6},{8,9},{9,8},{10,11... | collective-permute-start | bytes 393224 | tf_op jit(solution)/shard_map/ppermute | solution.py:386
  23.7 1.9 %shard_map.118 = (f32[6,16,64,128]{3,2,1,0:T(8,128)S(1)}, f32[6,16,64,128]{3,2,1,0:T(8,128)S(1)}) custom-call(f32[6]{0:T(128)S(1)} %stack.30.bloch_ref, f32[10]{0:T(128)S(1)} %copy-done.3, f32[2,8,128]{2,1,0:T(8,128)S(1)} %pad_maximum_fusion.hc_ref, f32[2,16,64,128]{3,2,1,0:T(8,128)S(1)} %get-tuple-element.99.c_ref, ...), custom_call_target="tpu_custom_call", output_to_operand_aliasing={{0}: (5, {}), {1}: (6, {})} | custom-call | tf_op jit(solution)/shard_map/pallas_call | solution.py:372
  25.5 2.5 %collective-permute-done.2.d_ref = f32[4,64,128]{2,1,0:T(8,128)S(1)} collective-permute-done((f32[4,64,128]{2,1,0:T(8,128)S(1)}, f32[4,64,128]{2,1,0:T(8,128)S(1)}, u32[]{:S(2)}, u32[]{:S(2)}) %collective-permute-start.2) | collective-permute-done | bytes 131104 | tf_op jit(solution)/shard_map/ppermute | solution.py:386
  28.7 1.7 %shard_map.120 = (f32[6,16,64,128]{3,2,1,0:T(8,128)S(1)}, f32[6,16,64,128]{3,2,1,0:T(8,128)S(1)}) custom-call(f32[6]{0:T(128)S(1)} %stack.30.bloch_ref, f32[10]{0:T(128)S(1)} %copy-done.3, f32[2,8,128]{2,1,0:T(8,128)S(1)} %pad_maximum_fusion.hc_ref, f32[2,16,64,128]{3,2,1,0:T(8,128)S(1)} %get-tuple-element.99.c_ref, ...), custom_call_target="tpu_custom_call", output_to_operand_aliasing={{0}: (5, {}), {1}: (6, {})} | custom-call | tf_op jit(solution)/shard_map/pallas_call | solution.py:372
  31.1 1.7 %collective-permute-start.4 = (f32[4,64,128]{2,1,0:T(8,128)S(1)}, f32[4,64,128]{2,1,0:T(8,128)S(1)}, u32[]{:S(2)}, u32[]{:S(2)}) collective-permute-start(f32[4,64,128]{2,1,0:T(8,128)S(1)} %get-tuple-element.122), channel_id=1, source_target_pairs={{0,1},{1,0},{2,3},{3,2},{4,5},{5,4},{6,7},{7,6},{8,9},{9,8},{10,11... | collective-permute-start | bytes 393224 | tf_op jit(solution)/shard_map/ppermute | solution.py:386
  33.1 1.9 %shard_map.122 = (f32[6,16,64,128]{3,2,1,0:T(8,128)S(1)}, f32[6,16,64,128]{3,2,1,0:T(8,128)S(1)}) custom-call(f32[6]{0:T(128)S(1)} %stack.30.bloch_ref, f32[10]{0:T(128)S(1)} %copy-done.3, f32[2,8,128]{2,1,0:T(8,128)S(1)} %pad_maximum_fusion.hc_ref, f32[2,16,64,128]{3,2,1,0:T(8,128)S(1)} %get-tuple-element.99.c_ref, ...), custom_call_target="tpu_custom_call", output_to_operand_aliasing={{0}: (5, {}), {1}: (6, {})} | custom-call | tf_op jit(solution)/shard_map/pallas_call | solution.py:372
  36.8 1.7 %shard_map.124 = (f32[6,16,64,128]{3,2,1,0:T(8,128)S(1)}, f32[6,16,64,128]{3,2,1,0:T(8,128)S(1)}) custom-call(f32[6]{0:T(128)S(1)} %stack.30.bloch_ref, f32[10]{0:T(128)S(1)} %copy-done.3, f32[2,8,128]{2,1,0:T(8,128)S(1)} %pad_maximum_fusion.hc_ref, f32[2,16,64,128]{3,2,1,0:T(8,128)S(1)} %get-tuple-element.99.c_ref, ...), custom_call_target="tpu_custom_call", output_to_operand_aliasing={{0}: (5, {}), {1}: (6, {})} | custom-call | tf_op jit(solution)/shard_map/pallas_call | solution.py:372
  39.2 1.7 %collective-permute-start.6 = (f32[4,64,128]{2,1,0:T(8,128)S(1)}, f32[4,64,128]{2,1,0:T(8,128)S(1)}, u32[]{:S(2)}, u32[]{:S(2)}) collective-permute-start(f32[4,64,128]{2,1,0:T(8,128)S(1)} %get-tuple-element.131), channel_id=1, source_target_pairs={{0,1},{1,0},{2,3},{3,2},{4,5},{5,4},{6,7},{7,6},{8,9},{9,8},{10,11... | collective-permute-start | bytes 393224 | tf_op jit(solution)/shard_map/ppermute | solution.py:386
  41.3 1.9 %shard_map.126 = (f32[6,16,64,128]{3,2,1,0:T(8,128)S(1)}, f32[6,16,64,128]{3,2,1,0:T(8,128)S(1)}) custom-call(f32[6]{0:T(128)S(1)} %stack.30.bloch_ref, f32[10]{0:T(128)S(1)} %copy-done.3, f32[2,8,128]{2,1,0:T(8,128)S(1)} %pad_maximum_fusion.hc_ref, f32[2,16,64,128]{3,2,1,0:T(8,128)S(1)} %get-tuple-element.99.c_ref, ...), custom_call_target="tpu_custom_call", output_to_operand_aliasing={{0}: (5, {}), {1}: (6, {})} | custom-call | tf_op jit(solution)/shard_map/pallas_call | solution.py:372
  44.9 1.7 %shard_map.128 = (f32[6,16,64,128]{3,2,1,0:T(8,128)S(1)}, f32[6,16,64,128]{3,2,1,0:T(8,128)S(1)}) custom-call(f32[6]{0:T(128)S(1)} %stack.30.bloch_ref, f32[10]{0:T(128)S(1)} %copy-done.3, f32[2,8,128]{2,1,0:T(8,128)S(1)} %pad_maximum_fusion.hc_ref, f32[2,16,64,128]{3,2,1,0:T(8,128)S(1)} %get-tuple-element.99.c_ref, ...), custom_call_target="tpu_custom_call", output_to_operand_aliasing={{0}: (5, {}), {1}: (6, {})} | custom-call | tf_op jit(solution)/shard_map/pallas_call | solution.py:372
  47.3 1.7 %collective-permute-start.8 = (f32[4,64,128]{2,1,0:T(8,128)S(1)}, f32[4,64,128]{2,1,0:T(8,128)S(1)}, u32[]{:S(2)}, u32[]{:S(2)}) collective-permute-start(f32[4,64,128]{2,1,0:T(8,128)S(1)} %get-tuple-element.140), channel_id=1, source_target_pairs={{0,1},{1,0},{2,3},{3,2},{4,5},{5,4},{6,7},{7,6},{8,9},{9,8},{10,11... | collective-permute-start | bytes 393224 | tf_op jit(solution)/shard_map/ppermute | solution.py:386
  49.4 1.9 %shard_map.130 = (f32[6,16,64,128]{3,2,1,0:T(8,128)S(1)}, f32[6,16,64,128]{3,2,1,0:T(8,128)S(1)}) custom-call(f32[6]{0:T(128)S(1)} %stack.30.bloch_ref, f32[10]{0:T(128)S(1)} %copy-done.3, f32[2,8,128]{2,1,0:T(8,128)S(1)} %pad_maximum_fusion.hc_ref, f32[2,16,64,128]{3,2,1,0:T(8,128)S(1)} %get-tuple-element.99.c_ref, ...), custom_call_target="tpu_custom_call", output_to_operand_aliasing={{0}: (5, {}), {1}: (6, {})} | custom-call | tf_op jit(solution)/shard_map/pallas_call | solution.py:372
  53.4 1.7 %shard_map.132 = (f32[6,16,64,128]{3,2,1,0:T(8,128)S(1)}, f32[6,16,64,128]{3,2,1,0:T(8,128)S(1)}) custom-call(f32[6]{0:T(128)S(1)} %stack.30.bloch_ref, f32[10]{0:T(128)S(1)} %copy-done.3, f32[2,8,128]{2,1,0:T(8,128)S(1)} %pad_maximum_fusion.hc_ref, f32[2,16,64,128]{3,2,1,0:T(8,128)S(1)} %get-tuple-element.99.c_ref, ...), custom_call_target="tpu_custom_call", output_to_operand_aliasing={{0}: (5, {}), {1}: (6, {})} | custom-call | tf_op jit(solution)/shard_map/pallas_call | solution.py:372
  55.7 1.7 %collective-permute-start.10 = (f32[4,64,128]{2,1,0:T(8,128)S(1)}, f32[4,64,128]{2,1,0:T(8,128)S(1)}, u32[]{:S(2)}, u32[]{:S(2)}) collective-permute-start(f32[4,64,128]{2,1,0:T(8,128)S(1)} %get-tuple-element.149), channel_id=1, source_target_pairs={{0,1},{1,0},{2,3},{3,2},{4,5},{5,4},{6,7},{7,6},{8,9},{9,8},{10,11... | collective-permute-start | bytes 393224 | tf_op jit(solution)/shard_map/ppermute | solution.py:386
  58.2 1.9 %shard_map.134 = (f32[6,16,64,128]{3,2,1,0:T(8,128)S(1)}, f32[6,16,64,128]{3,2,1,0:T(8,128)S(1)}) custom-call(f32[6]{0:T(128)S(1)} %stack.30.bloch_ref, f32[10]{0:T(128)S(1)} %copy-done.3, f32[2,8,128]{2,1,0:T(8,128)S(1)} %pad_maximum_fusion.hc_ref, f32[2,16,64,128]{3,2,1,0:T(8,128)S(1)} %get-tuple-element.99.c_ref, ...), custom_call_target="tpu_custom_call", output_to_operand_aliasing={{0}: (5, {}), {1}: (6, {})} | custom-call | tf_op jit(solution)/shard_map/pallas_call | solution.py:372
  61.5 1.7 %shard_map.136 = (f32[6,16,64,128]{3,2,1,0:T(8,128)S(1)}, f32[6,16,64,128]{3,2,1,0:T(8,128)S(1)}) custom-call(f32[6]{0:T(128)S(1)} %stack.30.bloch_ref, f32[10]{0:T(128)S(1)} %copy-done.3, f32[2,8,128]{2,1,0:T(8,128)S(1)} %pad_maximum_fusion.hc_ref, f32[2,16,64,128]{3,2,1,0:T(8,128)S(1)} %get-tuple-element.99.c_ref, ...), custom_call_target="tpu_custom_call", output_to_operand_aliasing={{0}: (5, {}), {1}: (6, {})} | custom-call | tf_op jit(solution)/shard_map/pallas_call | solution.py:372
  66.6 1.9 %shard_map.138 = (f32[6,16,64,128]{3,2,1,0:T(8,128)S(1)}, f32[6,16,64,128]{3,2,1,0:T(8,128)S(1)}) custom-call(f32[6]{0:T(128)S(1)} %stack.30.bloch_ref, f32[10]{0:T(128)S(1)} %copy-done.3, f32[2,8,128]{2,1,0:T(8,128)S(1)} %pad_maximum_fusion.hc_ref, f32[2,16,64,128]{3,2,1,0:T(8,128)S(1)} %get-tuple-element.99.c_ref, ...), custom_call_target="tpu_custom_call", output_to_operand_aliasing={{0}: (5, {}), {1}: (6, {})} | custom-call | tf_op jit(solution)/shard_map/pallas_call | solution.py:372
  70.3 1.7 %shard_map.140 = (f32[6,16,64,128]{3,2,1,0:T(8,128)S(1)}, f32[6,16,64,128]{3,2,1,0:T(8,128)S(1)}) custom-call(f32[6]{0:T(128)S(1)} %stack.30.bloch_ref, f32[10]{0:T(128)S(1)} %copy-done.3, f32[2,8,128]{2,1,0:T(8,128)S(1)} %pad_maximum_fusion.hc_ref, f32[2,16,64,128]{3,2,1,0:T(8,128)S(1)} %get-tuple-element.99.c_ref, ...), custom_call_target="tpu_custom_call", output_to_operand_aliasing={{0}: (5, {}), {1}: (6, {})} | custom-call | tf_op jit(solution)/shard_map/pallas_call | solution.py:372
  75.2 1.9 %shard_map.142 = (f32[6,16,64,128]{3,2,1,0:T(8,128)S(1)}, f32[6,16,64,128]{3,2,1,0:T(8,128)S(1)}) custom-call(f32[6]{0:T(128)S(1)} %stack.30.bloch_ref, f32[10]{0:T(128)S(1)} %copy-done.3, f32[2,8,128]{2,1,0:T(8,128)S(1)} %pad_maximum_fusion.hc_ref, f32[2,16,64,128]{3,2,1,0:T(8,128)S(1)} %get-tuple-element.99.c_ref, ...), custom_call_target="tpu_custom_call", output_to_operand_aliasing={{0}: (5, {}), {1}: (6, {})} | custom-call | tf_op jit(solution)/shard_map/pallas_call | solution.py:372
  78.9 1.7 %shard_map.144 = (f32[6,16,64,128]{3,2,1,0:T(8,128)S(1)}, f32[6,16,64,128]{3,2,1,0:T(8,128)S(1)}) custom-call(f32[6]{0:T(128)S(1)} %stack.30.bloch_ref, f32[10]{0:T(128)S(1)} %copy-done.3, f32[2,8,128]{2,1,0:T(8,128)S(1)} %pad_maximum_fusion.hc_ref, f32[2,16,64,128]{3,2,1,0:T(8,128)S(1)} %get-tuple-element.99.c_ref, ...), custom_call_target="tpu_custom_call", output_to_operand_aliasing={{0}: (5, {}), {1}: (6, {})} | custom-call | tf_op jit(solution)/shard_map/pallas_call | solution.py:372
  83.7 1.9 %shard_map.146 = (f32[6,16,64,128]{3,2,1,0:T(8,128)S(1)}, f32[6,16,64,128]{3,2,1,0:T(8,128)S(1)}) custom-call(f32[6]{0:T(128)S(1)} %stack.30.bloch_ref, f32[10]{0:T(128)S(1)} %copy-done.3, f32[2,8,128]{2,1,0:T(8,128)S(1)} %pad_maximum_fusion.hc_ref, f32[2,16,64,128]{3,2,1,0:T(8,128)S(1)} %get-tuple-element.99.c_ref, ...), custom_call_target="tpu_custom_call", output_to_operand_aliasing={{0}: (5, {}), {1}: (6, {})} | custom-call | tf_op jit(solution)/shard_map/pallas_call | solution.py:372
  87.4 1.7 %shard_map.148 = (f32[6,16,64,128]{3,2,1,0:T(8,128)S(1)}, f32[6,16,64,128]{3,2,1,0:T(8,128)S(1)}) custom-call(f32[6]{0:T(128)S(1)} %stack.30.bloch_ref, f32[10]{0:T(128)S(1)} %copy-done.3, f32[2,8,128]{2,1,0:T(8,128)S(1)} %pad_maximum_fusion.hc_ref, f32[2,16,64,128]{3,2,1,0:T(8,128)S(1)} %get-tuple-element.99.c_ref, ...), custom_call_target="tpu_custom_call", output_to_operand_aliasing={{0}: (5, {}), {1}: (6, {})} | custom-call | tf_op jit(solution)/shard_map/pallas_call | solution.py:372
  92.1 1.9 %shard_map.150 = (f32[6,16,64,128]{3,2,1,0:T(8,128)S(1)}, f32[6,16,64,128]{3,2,1,0:T(8,128)S(1)}) custom-call(f32[6]{0:T(128)S(1)} %stack.30.bloch_ref, f32[10]{0:T(128)S(1)} %copy-done.3, f32[2,8,128]{2,1,0:T(8,128)S(1)} %pad_maximum_fusion.hc_ref, f32[2,16,64,128]{3,2,1,0:T(8,128)S(1)} %get-tuple-element.99.c_ref, ...), custom_call_target="tpu_custom_call", output_to_operand_aliasing={{0}: (5, {}), {1}: (6, {})} | custom-call | tf_op jit(solution)/shard_map/pallas_call | solution.py:372
  99.8 2.3 %collective-permute-done.20.refs_1_ = f32[8,128]{1,0:T(8,128)S(1)} collective-permute-done((f32[8,128]{1,0:T(8,128)S(1)}, f32[8,128]{1,0:T(8,128)S(1)}, u32[]{:S(2)}, u32[]{:S(2)}) %collective-permute-start.20) | collective-permute-done | bytes 4128 | tf_op jit(solution)/shard_map/ppermute | solution.py:397
  104.8 2.1 %collective-permute-done.22.refs_1_ = f32[8,128]{1,0:T(8,128)S(1)} collective-permute-done((f32[8,128]{1,0:T(8,128)S(1)}, f32[8,128]{1,0:T(8,128)S(1)}, u32[]{:S(2)}, u32[]{:S(2)}) %collective-permute-start.22) | collective-permute-done | bytes 4128 | tf_op jit(solution)/shard_map/ppermute | solution.py:397
  108.5 2.0 %collective-permute-done.23.refs_1_ = f32[8,128]{1,0:T(8,128)S(1)} collective-permute-done((f32[8,128]{1,0:T(8,128)S(1)}, f32[8,128]{1,0:T(8,128)S(1)}, u32[]{:S(2)}, u32[]{:S(2)}) %collective-permute-start.23) | collective-permute-done | bytes 4128 | tf_op jit(solution)/shard_map/ppermute | solution.py:397
  110.5 2.6 %collective-permute-start.24 = (f32[8,128]{1,0:T(8,128)S(1)}, f32[8,128]{1,0:T(8,128)S(1)}, u32[]{:S(2)}, u32[]{:S(2)}) collective-permute-start(f32[8,128]{1,0:T(8,128)S(1)} %shard_map.161.refs_0_), channel_id=1, source_target_pairs={{0,16},{2,18},{4,20},{6,22},{8,24},{10,26},{12,28},{14,30},{16,0},... | collective-permute-start | bytes 12296 | tf_op jit(solution)/shard_map/ppermute | solution.py:397
  113.1 2.7 %shard_map.153 = (f32[6,16,64,128]{3,2,1,0:T(8,128)}, f32[6,16,64,128]{3,2,1,0:T(8,128)}) custom-call(f32[6,16,64,128]{3,2,1,0:T(8,128)S(1)} %get-tuple-element.191.e_ref, f32[6,16,64,128]{3,2,1,0:T(8,128)S(1)} %get-tuple-element.190.h_in.h_ref), custom_call_target="tpu_custom_call" | custom-call | tf_op jit(solution)/shard_map/pallas_call | solution.py:546
  (96 shorter events, 51.0 us)
Async XLA Ops:
  0.6 12.7 %copy-start.5 = (f32[3]{0:T(128)S(1)}, f32[3]{0:T(128)}, u32[]{:S(2)}) copy-start(f32[3]{0:T(128)} %perm_ref.1) | copy-start | bytes 40
  6.6 1.4 %copy-start = (bf16[1,6,16,64,128]{4,3,2,1,0:T(8,128)(2,1)S(1)}, bf16[1,6,16,64,128]{4,3,2,1,0:T(8,128)(2,1)}, u32[]{:S(2)}) copy-start(bf16[1,6,16,64,128]{4,3,2,1,0:T(8,128)(2,1)} %param.14) | copy-start | bytes 4718596
  8.0 1.4 %copy-start.2 = (bf16[1,6,16,64,128]{4,3,2,1,0:T(8,128)(2,1)S(1)}, bf16[1,6,16,64,128]{4,3,2,1,0:T(8,128)(2,1)}, u32[]{:S(2)}) copy-start(bf16[1,6,16,64,128]{4,3,2,1,0:T(8,128)(2,1)} %param.15) | copy-start | bytes 4718596
  9.4 3.9 %copy-start.1 = (bf16[1,6,16,64,128]{4,3,2,1,0:T(8,128)(2,1)S(1)}, bf16[1,6,16,64,128]{4,3,2,1,0:T(8,128)(2,1)}, u32[]{:S(2)}) copy-start(bf16[1,6,16,64,128]{4,3,2,1,0:T(8,128)(2,1)} %param.14) | copy-start | bytes 4718596
  9.4 3.9 %copy-start.4 = (s32[16,64,128]{2,1,0:T(8,128)S(1)}, s32[16,64,128]{2,1,0:T(8,128)}, u32[]{:S(2)}) copy-start(s32[16,64,128]{2,1,0:T(8,128)} %mat_ref.1) | copy-start | bytes 1572868
  9.4 5.1 %copy-start.6 = (f32[1,2,16,64]{3,2,1,0:T(8,128)S(1)}, f32[1,2,16,64]{3,2,1,0:T(8,128)}, u32[]{:S(2)}) copy-start(f32[1,2,16,64]{3,2,1,0:T(8,128)} %param.12) | copy-start | bytes 24580
  10.2 4.7 %copy-start.3 = (f32[10]{0:T(128)S(1)}, f32[10]{0:T(128)}, u32[]{:S(2)}) copy-start(f32[10]{0:T(128)} %wave_ref.79) | copy-start | bytes 124
  10.2 8.3 %collective-permute-start = (f32[4,64,128]{2,1,0:T(8,128)S(1)}, f32[4,64,128]{2,1,0:T(8,128)S(1)}, u32[]{:S(2)}, u32[]{:S(2)}) collective-permute-start(f32[4,64,128]{2,1,0:T(8,128)S(1)} %get-tuple-element.101), channel_id=1, source_target_pairs={{0,1},{1,0},{2,3},{3,2},{4,5},{5,4},{6,7},{7,6},{8,9},{9,8},{10,11... | collective-permute-start | bytes 393224 | tf_op jit(solution)/shard_map/ppermute | solution.py:386
  13.3 7.6 %collective-permute-start.1 = (f32[4,64,128]{2,1,0:T(8,128)S(1)}, f32[4,64,128]{2,1,0:T(8,128)S(1)}, u32[]{:S(2)}, u32[]{:S(2)}) collective-permute-start(f32[4,64,128]{2,1,0:T(8,128)S(1)} %get-tuple-element.100.s_ref), channel_id=1, source_target_pairs={{0,1},{1,0},{2,3},{3,2},{4,5},{5,4},{6,7},{7,6},{8,9},{9,8},{10,11... | collective-permute-start | bytes 393224 | tf_op jit(solution)/shard_map/ppermute | solution.py:386
  21.6 6.4 %collective-permute-start.2 = (f32[4,64,128]{2,1,0:T(8,128)S(1)}, f32[4,64,128]{2,1,0:T(8,128)S(1)}, u32[]{:S(2)}, u32[]{:S(2)}) collective-permute-start(f32[4,64,128]{2,1,0:T(8,128)S(1)} %get-tuple-element.113), channel_id=1, source_target_pairs={{0,1},{1,0},{2,3},{3,2},{4,5},{5,4},{6,7},{7,6},{8,9},{9,8},{10,11... | collective-permute-start | bytes 393224 | tf_op jit(solution)/shard_map/ppermute | solution.py:386
  23.6 6.8 %collective-permute-start.3 = (f32[4,64,128]{2,1,0:T(8,128)S(1)}, f32[4,64,128]{2,1,0:T(8,128)S(1)}, u32[]{:S(2)}, u32[]{:S(2)}) collective-permute-start(f32[4,64,128]{2,1,0:T(8,128)S(1)} %get-tuple-element.108.s_ref), channel_id=1, source_target_pairs={{0,1},{1,0},{2,3},{3,2},{4,5},{5,4},{6,7},{7,6},{8,9},{9,8},{10,11... | collective-permute-start | bytes 393224 | tf_op jit(solution)/shard_map/ppermute | solution.py:386
  31.1 5.0 %collective-permute-start.4 = (f32[4,64,128]{2,1,0:T(8,128)S(1)}, f32[4,64,128]{2,1,0:T(8,128)S(1)}, u32[]{:S(2)}, u32[]{:S(2)}) collective-permute-start(f32[4,64,128]{2,1,0:T(8,128)S(1)} %get-tuple-element.122), channel_id=1, source_target_pairs={{0,1},{1,0},{2,3},{3,2},{4,5},{5,4},{6,7},{7,6},{8,9},{9,8},{10,11... | collective-permute-start | bytes 393224 | tf_op jit(solution)/shard_map/ppermute | solution.py:386
  32.8 5.7 %collective-permute-start.5 = (f32[4,64,128]{2,1,0:T(8,128)S(1)}, f32[4,64,128]{2,1,0:T(8,128)S(1)}, u32[]{:S(2)}, u32[]{:S(2)}) collective-permute-start(f32[4,64,128]{2,1,0:T(8,128)S(1)} %get-tuple-element.117.s_ref), channel_id=1, source_target_pairs={{0,1},{1,0},{2,3},{3,2},{4,5},{5,4},{6,7},{7,6},{8,9},{9,8},{10,11... | collective-permute-start | bytes 393224 | tf_op jit(solution)/shard_map/ppermute | solution.py:386
  39.2 5.0 %collective-permute-start.6 = (f32[4,64,128]{2,1,0:T(8,128)S(1)}, f32[4,64,128]{2,1,0:T(8,128)S(1)}, u32[]{:S(2)}, u32[]{:S(2)}) collective-permute-start(f32[4,64,128]{2,1,0:T(8,128)S(1)} %get-tuple-element.131), channel_id=1, source_target_pairs={{0,1},{1,0},{2,3},{3,2},{4,5},{5,4},{6,7},{7,6},{8,9},{9,8},{10,11... | collective-permute-start | bytes 393224 | tf_op jit(solution)/shard_map/ppermute | solution.py:386
  40.9 5.7 %collective-permute-start.7 = (f32[4,64,128]{2,1,0:T(8,128)S(1)}, f32[4,64,128]{2,1,0:T(8,128)S(1)}, u32[]{:S(2)}, u32[]{:S(2)}) collective-permute-start(f32[4,64,128]{2,1,0:T(8,128)S(1)} %get-tuple-element.126.s_ref), channel_id=1, source_target_pairs={{0,1},{1,0},{2,3},{3,2},{4,5},{5,4},{6,7},{7,6},{8,9},{9,8},{10,11... | collective-permute-start | bytes 393224 | tf_op jit(solution)/shard_map/ppermute | solution.py:386
  47.3 5.0 %collective-permute-start.8 = (f32[4,64,128]{2,1,0:T(8,128)S(1)}, f32[4,64,128]{2,1,0:T(8,128)S(1)}, u32[]{:S(2)}, u32[]{:S(2)}) collective-permute-start(f32[4,64,128]{2,1,0:T(8,128)S(1)} %get-tuple-element.140), channel_id=1, source_target_pairs={{0,1},{1,0},{2,3},{3,2},{4,5},{5,4},{6,7},{7,6},{8,9},{9,8},{10,11... | collective-permute-start | bytes 393224 | tf_op jit(solution)/shard_map/ppermute | solution.py:386
  49.0 6.0 %collective-permute-start.9 = (f32[4,64,128]{2,1,0:T(8,128)S(1)}, f32[4,64,128]{2,1,0:T(8,128)S(1)}, u32[]{:S(2)}, u32[]{:S(2)}) collective-permute-start(f32[4,64,128]{2,1,0:T(8,128)S(1)} %get-tuple-element.135.s_ref), channel_id=1, source_target_pairs={{0,1},{1,0},{2,3},{3,2},{4,5},{5,4},{6,7},{7,6},{8,9},{9,8},{10,11... | collective-permute-start | bytes 393224 | tf_op jit(solution)/shard_map/ppermute | solution.py:386
  55.7 5.0 %collective-permute-start.10 = (f32[4,64,128]{2,1,0:T(8,128)S(1)}, f32[4,64,128]{2,1,0:T(8,128)S(1)}, u32[]{:S(2)}, u32[]{:S(2)}) collective-permute-start(f32[4,64,128]{2,1,0:T(8,128)S(1)} %get-tuple-element.149), channel_id=1, source_target_pairs={{0,1},{1,0},{2,3},{3,2},{4,5},{5,4},{6,7},{7,6},{8,9},{9,8},{10,11... | collective-permute-start | bytes 393224 | tf_op jit(solution)/shard_map/ppermute | solution.py:386
  57.4 6.4 %collective-permute-start.11 = (f32[4,64,128]{2,1,0:T(8,128)S(1)}, f32[4,64,128]{2,1,0:T(8,128)S(1)}, u32[]{:S(2)}, u32[]{:S(2)}) collective-permute-start(f32[4,64,128]{2,1,0:T(8,128)S(1)} %get-tuple-element.144.s_ref), channel_id=1, source_target_pairs={{0,1},{1,0},{2,3},{3,2},{4,5},{5,4},{6,7},{7,6},{8,9},{9,8},{10,11... | collective-permute-start | bytes 393224 | tf_op jit(solution)/shard_map/ppermute | solution.py:386
  64.5 5.1 %collective-permute-start.12 = (f32[4,64,128]{2,1,0:T(8,128)S(1)}, f32[4,64,128]{2,1,0:T(8,128)S(1)}, u32[]{:S(2)}, u32[]{:S(2)}) collective-permute-start(f32[4,64,128]{2,1,0:T(8,128)S(1)} %get-tuple-element.158), channel_id=1, source_target_pairs={{0,1},{1,0},{2,3},{3,2},{4,5},{5,4},{6,7},{7,6},{8,9},{9,8},{10,11... | collective-permute-start | bytes 393224 | tf_op jit(solution)/shard_map/ppermute | solution.py:386
  66.0 6.4 %collective-permute-start.13 = (f32[4,64,128]{2,1,0:T(8,128)S(1)}, f32[4,64,128]{2,1,0:T(8,128)S(1)}, u32[]{:S(2)}, u32[]{:S(2)}) collective-permute-start(f32[4,64,128]{2,1,0:T(8,128)S(1)} %get-tuple-element.153.s_ref), channel_id=1, source_target_pairs={{0,1},{1,0},{2,3},{3,2},{4,5},{5,4},{6,7},{7,6},{8,9},{9,8},{10,11... | collective-permute-start | bytes 393224 | tf_op jit(solution)/shard_map/ppermute | solution.py:386
  73.1 5.1 %collective-permute-start.14 = (f32[4,64,128]{2,1,0:T(8,128)S(1)}, f32[4,64,128]{2,1,0:T(8,128)S(1)}, u32[]{:S(2)}, u32[]{:S(2)}) collective-permute-start(f32[4,64,128]{2,1,0:T(8,128)S(1)} %get-tuple-element.167), channel_id=1, source_target_pairs={{0,1},{1,0},{2,3},{3,2},{4,5},{5,4},{6,7},{7,6},{8,9},{9,8},{10,11... | collective-permute-start | bytes 393224 | tf_op jit(solution)/shard_map/ppermute | solution.py:386
  74.6 6.4 %collective-permute-start.15 = (f32[4,64,128]{2,1,0:T(8,128)S(1)}, f32[4,64,128]{2,1,0:T(8,128)S(1)}, u32[]{:S(2)}, u32[]{:S(2)}) collective-permute-start(f32[4,64,128]{2,1,0:T(8,128)S(1)} %get-tuple-element.162.s_ref), channel_id=1, source_target_pairs={{0,1},{1,0},{2,3},{3,2},{4,5},{5,4},{6,7},{7,6},{8,9},{9,8},{10,11... | collective-permute-start | bytes 393224 | tf_op jit(solution)/shard_map/ppermute | solution.py:386
  81.6 5.0 %collective-permute-start.16 = (f32[4,64,128]{2,1,0:T(8,128)S(1)}, f32[4,64,128]{2,1,0:T(8,128)S(1)}, u32[]{:S(2)}, u32[]{:S(2)}) collective-permute-start(f32[4,64,128]{2,1,0:T(8,128)S(1)} %get-tuple-element.176), channel_id=1, source_target_pairs={{0,1},{1,0},{2,3},{3,2},{4,5},{5,4},{6,7},{7,6},{8,9},{9,8},{10,11... | collective-permute-start | bytes 393224 | tf_op jit(solution)/shard_map/ppermute | solution.py:386
  83.0 6.4 %collective-permute-start.18 = (f32[4,64,128]{2,1,0:T(8,128)S(1)}, f32[4,64,128]{2,1,0:T(8,128)S(1)}, u32[]{:S(2)}, u32[]{:S(2)}) collective-permute-start(f32[4,64,128]{2,1,0:T(8,128)S(1)} %get-tuple-element.171.s_ref), channel_id=1, source_target_pairs={{0,1},{1,0},{2,3},{3,2},{4,5},{5,4},{6,7},{7,6},{8,9},{9,8},{10,11... | collective-permute-start | bytes 393224 | tf_op jit(solution)/shard_map/ppermute | solution.py:386
  90.0 5.0 %collective-permute-start.19 = (f32[4,64,128]{2,1,0:T(8,128)S(1)}, f32[4,64,128]{2,1,0:T(8,128)S(1)}, u32[]{:S(2)}, u32[]{:S(2)}) collective-permute-start(f32[4,64,128]{2,1,0:T(8,128)S(1)} %get-tuple-element.185), channel_id=1, source_target_pairs={{0,1},{1,0},{2,3},{3,2},{4,5},{5,4},{6,7},{7,6},{8,9},{9,8},{10,11... | collective-permute-start | bytes 393224 | tf_op jit(solution)/shard_map/ppermute | solution.py:386
  91.4 5.4 %collective-permute-start.17 = (f32[4,64,128]{2,1,0:T(8,128)S(1)}, f32[4,64,128]{2,1,0:T(8,128)S(1)}, u32[]{:S(2)}, u32[]{:S(2)}) collective-permute-start(f32[4,64,128]{2,1,0:T(8,128)S(1)} %get-tuple-element.180.s_ref), channel_id=1, source_target_pairs={{0,1},{1,0},{2,3},{3,2},{4,5},{5,4},{6,7},{7,6},{8,9},{9,8},{10,11... | collective-permute-start | bytes 393224 | tf_op jit(solution)/shard_map/ppermute | solution.py:386
  98.5 3.6 %collective-permute-start.20 = (f32[8,128]{1,0:T(8,128)S(1)}, f32[8,128]{1,0:T(8,128)S(1)}, u32[]{:S(2)}, u32[]{:S(2)}) collective-permute-start(f32[8,128]{1,0:T(8,128)S(1)} %shard_map.157.refs_0_), channel_id=1, source_target_pairs={{0,1},{1,0},{2,3},{3,2},{4,5},{5,4},{6,7},{7,6},{8,9},{9,8},{10,11... | collective-permute-start | bytes 12296 | tf_op jit(solution)/shard_map/ppermute | solution.py:397
  102.1 1.2 collective-permute-start.21
  103.3 3.6 %collective-permute-start.22 = (f32[8,128]{1,0:T(8,128)S(1)}, f32[8,128]{1,0:T(8,128)S(1)}, u32[]{:S(2)}, u32[]{:S(2)}) collective-permute-start(f32[8,128]{1,0:T(8,128)S(1)} %shard_map.159.refs_0_), channel_id=1, source_target_pairs={{0,4},{2,6},{4,0},{6,2},{8,12},{10,14},{12,8},{14,10},{16,20},{18,... | collective-permute-start | bytes 12296 | tf_op jit(solution)/shard_map/ppermute | solution.py:397
  106.9 3.6 %collective-permute-start.23 = (f32[8,128]{1,0:T(8,128)S(1)}, f32[8,128]{1,0:T(8,128)S(1)}, u32[]{:S(2)}, u32[]{:S(2)}) collective-permute-start(f32[8,128]{1,0:T(8,128)S(1)} %shard_map.160.refs_0_), channel_id=1, source_target_pairs={{0,8},{2,10},{4,12},{6,14},{8,0},{10,2},{12,4},{14,6},{16,24},{18,... | collective-permute-start | bytes 12296 | tf_op jit(solution)/shard_map/ppermute | solution.py:397
  110.5 5.8 %collective-permute-start.24 = (f32[8,128]{1,0:T(8,128)S(1)}, f32[8,128]{1,0:T(8,128)S(1)}, u32[]{:S(2)}, u32[]{:S(2)}) collective-permute-start(f32[8,128]{1,0:T(8,128)S(1)} %shard_map.161.refs_0_), channel_id=1, source_target_pairs={{0,16},{2,18},{4,20},{6,22},{8,24},{10,26},{12,28},{14,30},{16,0},... | collective-permute-start | bytes 12296 | tf_op jit(solution)/shard_map/ppermute | solution.py:397

commit v2 on v1

v2 whole, which is shorter than its diff:
```python
import functools

import jax
import jax.numpy as jnp
from jax import lax
from jax.experimental import pallas as pl
from jax.experimental.pallas import tpu as pltpu
from jax.sharding import PartitionSpec as P


PML = 16
INTERVAL = 5
NSNAP = 2
MPHASE = 64
NMAT = 3
TIME_STEP = 0.5
SUB = 8

VMEM = pl.BlockSpec(memory_space=pltpu.VMEM)
SMEM = pl.BlockSpec(memory_space=pltpu.SMEM)
HBM = pl.BlockSpec(memory_space=pltpu.HBM)
ANY = pl.BlockSpec(memory_space=pl.ANY)
F32 = jnp.float32

COS, SIN, END, START, KEEP, GAIN, DRIVE = 0, 1, 2, 4, 6, 7, 8


def load(ref, *where):
    tiles = ref.shape[-2] // SUB
    return [ref[(*where, pl.ds(SUB * j, SUB))].astype(F32) for j in range(tiles)]


def load_couple(ref, member, *where):
    return (load(ref, 2 * member, *where), load(ref, 2 * member + 1, *where))


def store(ref, values, *where):
    for j, tile in enumerate(values):
        ref[(*where, pl.ds(SUB * j, SUB))] = tile


def store_couple(ref, couple, member, *where):
    store(ref, couple[0], 2 * member, *where)
    store(ref, couple[1], 2 * member + 1, *where)


def both(fn, *couples):
    return tuple(
        [fn(*tiles) for tiles in zip(*parts)] for parts in zip(*couples)
    )


def scaled(planes, fn, couple, *others):
    out = []
    for part in range(2):
        parts = [couple[part], *(other[part] for other in others)]
        out.append([fn(*tiles) for tiles in zip(*planes, *parts)])
    return tuple(out)


def turn(couple, cosine, sine):
    return (
        [re * cosine - im * sine for re, im in zip(*couple)],
        [re * sine + im * cosine for re, im in zip(*couple)],
    )


def next_y(couple, cosine, sine):
    rows = lax.broadcasted_iota(jnp.int32, couple[0][0].shape, 0)
    wrapped = turn((couple[0][:1], couple[1][:1]), cosine, sine)
    out = []
    for part, edge in zip(couple, wrapped):
        after = part[1:] + edge
        out.append(
            [
                pltpu.roll(jnp.where(rows == 0, there, here), SUB - 1, 0)
                for here, there in zip(part, after)
            ]
        )
    return tuple(out)


def prior_y(couple, cosine, sine):
    rows = lax.broadcasted_iota(jnp.int32, couple[0][0].shape, 0)
    wrapped = turn((couple[0][-1:], couple[1][-1:]), cosine, -sine)
    out = []
    for part, edge in zip(couple, wrapped):
        before = edge + part[:-1]
        out.append(
            [
                pltpu.roll(jnp.where(rows == SUB - 1, there, here), 1, 0)
                for here, there in zip(part, before)
            ]
        )
    return tuple(out)


def next_z(couple):
    depth = couple[0][0].shape[1]
    lanes = lax.broadcasted_iota(jnp.int32, couple[0][0].shape, 1)
    return both(
        lambda tile: jnp.where(lanes == depth - 1, 0.0, pltpu.roll(tile, depth - 1, 1)),
        couple,
    )


def prior_z(couple):
    lanes = lax.broadcasted_iota(jnp.int32, couple[0][0].shape, 1)
    return both(lambda tile: jnp.where(lanes == 0, 0.0, pltpu.roll(tile, 1, 1)), couple)


def new_hx(ey, ez, hx, keep, gain, cosine, sine):
    return both(
        lambda h, z_up, z, y_up, y: keep * h + gain * ((z_up - z) - (y_up - y)),
        hx,
        next_y(ez, cosine, sine),
        ez,
        next_z(ey),
        ey,
    )


def partial_h(ex, ey, ez, hy, hz, keep, gain, cosine, sine):
    part_y = both(
        lambda h, x_up, x, z: keep * h + gain * ((x_up - x) + z), hy, next_z(ex), ex, ez
    )
    part_z = both(
        lambda h, x_up, x, y: keep * h - gain * ((x_up - x) + y),
        hz,
        next_y(ex, cosine, sine),
        ex,
        ey,
    )
    return part_y, part_z


def close_h(part_y, part_z, ey_above, ez_above, gain):
    return (
        both(lambda h, z: h - gain * z, part_y, ez_above),
        both(lambda h, y: h + gain * y, part_z, ey_above),
    )


def h_row(e_ref, h_ref, x, keep, gain, cosine, sine):
    ex, ey, ez = (load_couple(e_ref, m, x) for m in range(3))
    ey_above, ez_above = (load_couple(e_ref, m, x + 1) for m in (1, 2))
    hx, hy, hz = (load_couple(h_ref, m, x) for m in range(3))
    new_x = new_hx(ey, ez, hx, keep, gain, cosine, sine)
    new_y = both(
        lambda h, x_up, x_, z_up, z: keep * h + gain * ((x_up - x_) - (z_up - z)),
        hy,
        next_z(ex),
        ex,
        ez_above,
        ez,
    )
    new_z = both(
        lambda h, y_up, y, x_up, x_: keep * h + gain * ((y_up - y) - (x_up - x_)),
        hz,
        ey_above,
        ey,
        next_y(ex, cosine, sine),
        ex,
    )
    store_couple(h_ref, new_x, 0, x)
    store_couple(h_ref, new_y, 1, x)
    store_couple(h_ref, new_z, 2, x)


def new_e(e, h, hy_below, hz_below, retain, factor, sheet, drive, cosine, sine):
    ex, ey, ez = e
    hx, hy, hz = h
    drive_x = both(lambda s: drive * s, sheet)
    new_x = scaled(
        (retain, factor),
        lambda r, f, e_, z, z_dn, y, y_dn, s: r * e_ + f * ((z - z_dn) - (y - y_dn) - s),
        ex,
        hz,
        prior_y(hz, cosine, sine),
        hy,
        prior_z(hy),
        drive_x,
    )
    new_y = scaled(
        (retain, factor),
        lambda r, f, e_, x, x_dn, z, z_dn: r * e_ + f * ((x - x_dn) - (z - z_dn)),
        ey,
        hx,
        prior_z(hx),
        hz,
        hz_below,
    )
    new_z = scaled(
        (retain, factor),
        lambda r, f, e_, y, y_dn, x, x_dn: r * e_ + f * ((y - y_dn) - (x - x_dn)),
        ez,
        hy,
        hy_below,
        hx,
        prior_y(hx, cosine, sine),
    )
    return new_x, new_y, new_z


def e_row(e_ref, h_ref, c_ref, sheet_ref, x, drive, cosine, sine, below=None):
    e = [load_couple(e_ref, m, x) for m in range(3)]
    h = [load_couple(h_ref, m, x) for m in range(3)]
    if below is None:
        below = [load_couple(h_ref, m, x - 1) for m in (1, 2)]
    retain, factor = load(c_ref, 0, x), load(c_ref, 1, x)
    sheet = (load(sheet_ref, 0, x), load(sheet_ref, 1, x))
    new = new_e(e, h, *below, retain, factor, sheet, drive, cosine, sine)
    for m in range(3):
        store_couple(e_ref, new[m], m, x)
    return new


def is_upper(phase):
    return lax.axis_index("sp") % 2 == phase


def fetch(pairs, sems):
    copies = [
        pltpu.make_async_copy(source, target, sems.at[i])
        for i, (source, target) in enumerate(pairs)
    ]
    for copy in copies:
        copy.start()
    return copies


def first_kernel(
    bloch_hbm, peak_hbm, wave_hbm, e_hbm, h_hbm, p_ref, one_ref, two_ref,
    bloch, peak, wave, low, high, mag, sems,
):
    rows = e_hbm.shape[1]
    copies = fetch(
        [
            (bloch_hbm, bloch),
            (peak_hbm, peak),
            (wave_hbm, wave),
            (e_hbm.at[pl.ds(2, 4), 0], low),
            (e_hbm.at[:, rows - 1], high),
            (h_hbm.at[pl.ds(2, 4), rows - 1], mag),
        ],
        sems,
    )
    for copy in copies[:3]:
        copy.wait()
    shape = p_ref.shape[1:]
    angle_x, angle_y = (
        2.0 * jnp.pi * jnp.full(shape, bloch[0, axis].astype(F32)) / MPHASE
        for axis in range(2)
    )
    cos_x, sin_x = jnp.cos(angle_x), jnp.sin(angle_x)
    slab, slabs = lax.axis_index("sp"), lax.axis_size("sp")
    at_end, at_start = slab == slabs - 1, slab == 0
    half = conductivity(peak[0], shape) * (0.5 * TIME_STEP)
    p_ref[COS] = cosine = jnp.cos(angle_y)
    p_ref[SIN] = sine = jnp.sin(angle_y)
    p_ref[END] = jnp.where(at_end, cos_x, 1.0)
    p_ref[END + 1] = jnp.where(at_end, sin_x, 0.0)
    p_ref[START] = jnp.where(at_start, cos_x, 1.0)
    p_ref[START + 1] = jnp.where(at_start, -sin_x, 0.0)
    p_ref[KEEP] = keep = (1.0 - half) / (1.0 + half)
    p_ref[GAIN] = gain = -TIME_STEP / (1.0 + half)
    for step in range(wave.shape[0]):
        p_ref[DRIVE + step] = jnp.full(shape, wave[step])
    for copy in copies[3:]:
        copy.wait()

    def write(d_ref, s_ref):
        d_ref[...] = low[...].astype(F32)
        ex, ey, ez = (load_couple(high, m) for m in range(3))
        hy, hz = (load_couple(mag, m) for m in range(2))
        part_y, part_z = partial_h(ex, ey, ez, hy, hz, keep, gain, cosine, sine)
        store_couple(s_ref, part_y, 0)
        store_couple(s_ref, part_z, 1)

    @pl.when(is_upper(0))
    def _():
        write(two_ref, one_ref)

    @pl.when(jnp.logical_not(is_upper(0)))
    def _():
        write(one_ref, two_ref)


def widen_kernel(
    peak_hbm, perm_hbm, mat_hbm, e_hbm, h_hbm, e_ref, h_ref, c_ref,
    peak, perm, mat, e_in, h_in, small, sems,
):
    rows, width, depth = mat.shape
    parts = sems.shape[0]
    size = rows // parts
    scalars = fetch([(peak_hbm, peak), (perm_hbm, perm)], small)
    copies = []
    for part in range(parts):
        some = pl.ds(part * size, size)
        copies.append(
            fetch(
                [
                    (mat_hbm.at[some], mat.at[some]),
                    (e_hbm.at[:, some], e_in.at[:, some]),
                    (h_hbm.at[:, some], h_in.at[:, some]),
                ],
                sems.at[part],
            )
        )
    for copy in scalars:
        copy.wait()
    conduct = conductivity(peak[0], (SUB, depth)) * (0.5 * TIME_STEP)
    levels = []
    for index in range(NMAT):
        half = conduct / perm[index]
        levels.append(
            ((1.0 - half) / (1.0 + half), TIME_STEP / perm[index] / (1.0 + half))
        )

    def one_row(x, carry):
        for j in range(width // SUB):
            tile = pl.ds(SUB * j, SUB)
            level = mat[x, tile]
            retain, factor = levels[0]
            for index in range(1, NMAT):
                retain = jnp.where(level == index, levels[index][0], retain)
                factor = jnp.where(level == index, levels[index][1], factor)
            c_ref[0, x, tile] = retain
            c_ref[1, x, tile] = factor
        for m in range(6):
            e_ref[m, x] = e_in[m, x].astype(F32)
            h_ref[m, x] = h_in[m, x].astype(F32)
        return carry

    for part in range(parts):
        for copy in copies[part]:
            copy.wait()
        lax.fori_loop(part * size, (part + 1) * size, one_row, 0)


def conductivity(peak, shape):
    depth = shape[-1]
    height = lax.broadcasted_iota(jnp.int32, shape, len(shape) - 1).astype(F32)
    low = jnp.maximum(PML - height, 0.0) / PML
    high = jnp.maximum(height - (depth - 1 - PML), 0.0) / PML
    return peak * (low * low * low + high * high * high)


def inner_kernel(phase, step, p_ref, c_ref, sheet_ref, e_in, h_in, e_ref, h_ref):
    rows = e_ref.shape[1]
    middle = rows // 2
    cosine, sine, drive = p_ref[COS], p_ref[SIN], p_ref[DRIVE + step]
    keep, gain = p_ref[KEEP], p_ref[GAIN]
    upper = is_upper(phase)
    lo = jnp.where(upper, middle, 0)
    hi = jnp.where(upper, rows - 1, middle)
    skip = 1 if phase == 0 else jnp.where(upper, 0, 1)

    def new_h(x):
        h_row(e_ref, h_ref, x, keep, gain, cosine, sine)

    def new_electric(x):
        e_row(e_ref, h_ref, c_ref, sheet_ref, x, drive, cosine, sine)

    def start_row(x, carry):
        new_h(x)
        return carry

    def one_row(x, carry):
        new_h(x + 1)
        new_electric(x)
        return carry

    lax.fori_loop(lo, lo + skip + 1, start_row, 0)
    lax.fori_loop(lo + skip, hi - 1, one_row, 0)
    new_electric(hi - 1)

    @pl.when(upper)
    def _():
        ey, ez = (load_couple(e_ref, m, rows - 1) for m in (1, 2))
        hx = load_couple(h_ref, 0, rows - 1)
        store_couple(h_ref, new_hx(ey, ez, hx, keep, gain, cosine, sine), 0, rows - 1)

    if phase == 1:

        @pl.when(jnp.logical_not(upper))
        def _():
            new_electric(middle)


def edge_step(
    phase, step, p_ref, c_ref, sheet_ref, mine_ref, their_ref, e_ref, h_ref, out_ref=None
):
    cosine, sine, drive = p_ref[COS], p_ref[SIN], p_ref[DRIVE + step]
    keep, gain = p_ref[KEEP], p_ref[GAIN]
    top = e_ref.shape[1] - 1
    upper = is_upper(phase)

    @pl.when(upper)
    def _():
        part_y, part_z = (load_couple(mine_ref, m) for m in range(2))
        ey_above, ez_above = (
            turn(load_couple(their_ref, m), p_ref[END], p_ref[END + 1]) for m in range(2)
        )
        hy, hz = close_h(part_y, part_z, ey_above, ez_above, gain)
        store_couple(h_ref, hy, 1, top)
        store_couple(h_ref, hz, 2, top)
        ex, ey, ez = e_row(e_ref, h_ref, c_ref, sheet_ref, top, drive, cosine, sine)
        if out_ref is not None:
            part_y, part_z = partial_h(ex, ey, ez, hy, hz, keep, gain, cosine, sine)
            store_couple(out_ref, part_y, 0)
            store_couple(out_ref, part_z, 1)

    @pl.when(jnp.logical_not(upper))
    def _():
        part_y, part_z = (
            turn(load_couple(their_ref, m), p_ref[START], p_ref[START + 1])
            for m in range(2)
        )
        ey, ez = (load_couple(e_ref, m, 0) for m in (1, 2))
        below = close_h(part_y, part_z, ey, ez, gain)
        _, ey, ez = e_row(
            e_ref, h_ref, c_ref, sheet_ref, 0, drive, cosine, sine, below
        )
        if out_ref is not None:
            store_couple(out_ref, ey, 0)
            store_couple(out_ref, ez, 1)


def edge_kernel(
    phase, step, p_ref, c_ref, sheet_ref, mine_ref, their_ref, e_in, h_in,
    e_ref, h_ref, *out_ref,
):
    edge_step(
        phase, step, p_ref, c_ref, sheet_ref, mine_ref, their_ref, e_ref, h_ref, *out_ref
    )


def last_kernel(
    phase, step, slot, scale, p_ref, c_ref, sheet_ref, mine_ref, their_ref, old_ref,
    e_in, h_in, e_ref, h_ref, out_ref,
):
    edge_step(phase, step, p_ref, c_ref, sheet_ref, mine_ref, their_ref, e_ref, h_ref)
    total = jnp.zeros(old_ref.shape, F32)
    for x in (0, e_ref.shape[1] - 1):
        for m in range(4):
            for tile in load(e_ref, m, x):
                total = total + tile * tile
    out_ref[...] = old_ref[...] + monitor(total, slot, scale)


def monitor(total, slot, scale):
    lanes = lax.broadcasted_iota(jnp.int32, total.shape, 1)
    total = jnp.where(lanes == PML + 6, total, 0.0)
    total = jnp.sum(jnp.sum(total, 0, keepdims=True), 1, keepdims=True) * scale
    return jnp.where(lanes == slot, total, 0.0)


def power_kernel(phase, slot, scale, e_ref, old_ref, out_ref):
    rows, _, depth = e_ref.shape[1:]
    lo, hi = 1, rows - 1
    if phase is not None:
        middle, upper = rows // 2, is_upper(phase)
        lo = jnp.where(upper, middle + (1 - phase), 0)
        hi = jnp.where(upper, rows, middle + phase)

    def one_row(x, total):
        for m in range(4):
            for tile in load(e_ref, m, x):
                total = total + tile * tile
        return total

    total = lax.fori_loop(lo, hi, one_row, jnp.zeros((SUB, depth), F32))
    out_ref[...] = old_ref[...] + monitor(total, slot, scale)


def move(pairs, sems):
    for copy in fetch(pairs, sems):
        copy.wait()


def inner_out_kernel(e_ref, h_ref, e_out, h_out, sems):
    rows = e_ref.shape[1]
    some, most = pl.ds(1, rows - 2), pl.ds(0, rows - 1)
    move(
        [(e_ref.at[:, some], e_out.at[:, some]), (h_ref.at[:, most], h_out.at[:, most])],
        sems,
    )


def edge_out_kernel(e_ref, h_ref, e_in, h_in, e_out, h_out, sems):
    end = e_ref.shape[1] - 1
    move(
        [
            (e_ref.at[:, 0], e_out.at[:, 0]),
            (e_ref.at[:, end], e_out.at[:, end]),
            (h_ref.at[:, end], h_out.at[:, end]),
        ],
        sems,
    )


def add_kernel(scale, *refs):
    total = refs[0][...]
    for ref in refs[1:-1]:
        total = total + ref[...]
    refs[-1][...] = total * scale if scale != 1.0 else total


def call(kernel, outs, ins, specs, aliases=None, scratch=(), flops=0, vmem=16):
    return pl.pallas_call(
        kernel,
        out_shape=tuple(pltpu.VMEM(shape, F32) for shape in outs),
        in_specs=specs,
        out_specs=tuple(VMEM for _ in outs),
        input_output_aliases=aliases or {},
        scratch_shapes=scratch,
        cost_estimate=pl.CostEstimate(flops=flops, bytes_accessed=0, transcendentals=0),
        compiler_params=pltpu.CompilerParams(vmem_limit_bytes=vmem * 2**20),
    )(*ins)


def swap(value, phase):
    count = lax.axis_size("sp")
    pairs = [(i, (((i - phase) % count ^ 1) + phase) % count) for i in range(count)]
    return lax.ppermute(value, "sp", pairs)


def shift(value, axis, steps):
    count = lax.axis_size(axis)
    return lax.ppermute(value, axis, [(i, (i + steps) % count) for i in range(count)])


def total_over(value, axis, scale=1.0):
    count = lax.axis_size(axis)
    shape = value.shape
    if count & (count - 1):
        parts = [value] + [shift(value, axis, step) for step in range(1, count)]
        return call(functools.partial(add_kernel, scale), [shape], parts, [VMEM] * count)[0]
    step = 1
    while step < count:
        other = lax.ppermute(value, axis, [(i, i ^ step) for i in range(count)])
        step *= 2
        last = scale if step >= count else 1.0
        value = call(
            functools.partial(add_kernel, last), [shape], [value, other], [VMEM] * 2
        )[0]
    return value


def to_hbm(kernel, shape, ins, specs, copies, aliases=None):
    whole = jax.ShapeDtypeStruct(shape, F32)
    return pl.pallas_call(
        kernel,
        out_shape=(whole, whole),
        in_specs=specs,
        out_specs=(HBM, HBM),
        input_output_aliases=aliases or {},
        scratch_shapes=[pltpu.SemaphoreType.DMA((copies,))],
        compiler_params=pltpu.CompilerParams(vmem_limit_bytes=2**20),
    )(*ins)


def on_device(
    bloch_index,
    material,
    permittivity,
    absorption_peak,
    source_sheet,
    waveform,
    electric_in,
    magnetic_in,
):
    points = bloch_index.shape[0]
    rows, width, depth = material.shape
    total_points = points * lax.axis_size("ka")
    cells_plane = rows * lax.axis_size("sp") * width
    plane = (jnp.arange(depth) == PML + 2).astype(F32)
    sheets = source_sheet[..., None] * plane
    results = [
        one_point(
            bloch_index[point : point + 1], sheets[point], waveform, material, permittivity,
            absorption_peak, electric_in[point], magnetic_in[point], 1.0 / cells_plane,
        )
        for point in range(points)
    ]
    electric, magnetic, powers = zip(*results)
    sums = [total_over(power, "sp") for power in powers]
    local = sums[0]
    for other in sums[1:]:
        local = local + other
    mean = total_over(local, "ka", 1.0 / total_points)
    return (
        jnp.stack(electric),
        jnp.stack(magnetic),
        jnp.stack([total[0, :NSNAP] for total in sums]),
        mean[0, :NSNAP],
    )


def one_point(
    bloch, sheet, waveform, material, permittivity, peak, electric_in, magnetic_in, scale
):
    rows, width, depth = material.shape
    steps = waveform.shape[0]
    edge = (4, width, depth)
    full = (6, rows, width, depth)
    dtype = electric_in.dtype
    electric_in, magnetic_in, material = (
        pltpu.with_memory_space_constraint(value, pltpu.HBM)
        for value in (electric_in, magnetic_in, material)
    )
    p, *mine = call(
        first_kernel,
        [(DRIVE + steps, SUB, depth), edge, edge],
        [bloch, peak, waveform, electric_in, magnetic_in],
        [ANY] * 3 + [HBM] * 2,
        scratch=[
            pltpu.SMEM(bloch.shape, bloch.dtype),
            pltpu.SMEM(peak.shape, F32),
            pltpu.SMEM(waveform.shape, F32),
            pltpu.VMEM((4, width, depth), dtype),
            pltpu.VMEM((6, width, depth), dtype),
            pltpu.VMEM((4, width, depth), dtype),
            pltpu.SemaphoreType.DMA((6,)),
        ],
    )
    their = [swap(mine[phase], phase) for phase in range(2)]
    e, h, c = call(
        widen_kernel,
        [full, full, (2, rows, width, depth)],
        [peak, permittivity, material, electric_in, magnetic_in],
        [ANY] * 2 + [HBM] * 3,
        scratch=[
            pltpu.SMEM(peak.shape, F32),
            pltpu.SMEM(permittivity.shape, F32),
            pltpu.VMEM(material.shape, material.dtype),
            pltpu.VMEM(full, dtype),
            pltpu.VMEM(full, dtype),
            pltpu.SemaphoreType.DMA((2,)),
            pltpu.SemaphoreType.DMA((4, 3)),
        ],
    )
    power = jnp.zeros((SUB, depth), F32)

    def inner(phase, step, e, h):
        return call(
            functools.partial(inner_kernel, phase, step),
            [full, full],
            [p, c, sheet, e, h],
            [VMEM] * 5,
            {3: 0, 4: 1},
        )

    def measured(phase, step, power, e):
        return call(
            functools.partial(power_kernel, phase, step // INTERVAL, scale),
            [(SUB, depth)],
            [e, power],
            [VMEM, VMEM],
        )[0]

    for phase in range(2):
        e, h = inner(phase, 0, e, h)
    for step in range(steps - 1):
        for phase in range(2):
            e, h, mine[phase] = call(
                functools.partial(edge_kernel, phase, step),
                [full, full, edge],
                [p, c, sheet, mine[phase], their[phase], e, h],
                [VMEM] * 7,
                {5: 0, 6: 1},
            )
            if (step + 1) % INTERVAL == 0:
                power = measured(phase, step, power, e)
            their[phase] = swap(mine[phase], phase)
            e, h = inner(phase, step + 1, e, h)
    step = steps - 1
    power = measured(None, step, power, e)
    e_out, h_out = to_hbm(inner_out_kernel, full, [e, h], [VMEM, VMEM], 2)
    e, h = call(
        functools.partial(edge_kernel, 0, step),
        [full, full],
        [p, c, sheet, mine[0], their[0], e, h],
        [VMEM] * 7,
        {5: 0, 6: 1},
    )
    e, h, power = call(
        functools.partial(last_kernel, 1, step, step // INTERVAL, scale),
        [full, full, (SUB, depth)],
        [p, c, sheet, mine[1], their[1], power, e, h],
        [VMEM] * 8,
        {6: 0, 7: 1},
    )
    e_out, h_out = to_hbm(
        edge_out_kernel, full, [e, h, e_out, h_out], [VMEM, VMEM, HBM, HBM], 3, {2: 0, 3: 1}
    )
    return e_out, h_out, power


def solution(mesh):
    in_specs = (
        P("ka", None),
        P("sp", None, None),
        P(),
        P(),
        P("ka", None, "sp", None),
        P(),
        P("ka", None, "sp", None, None),
        P("ka", None, "sp", None, None),
    )
    out_specs = (
        P("ka", None, "sp", None, None),
        P("ka", None, "sp", None, None),
        P("ka", None),
        P(),
    )
    return jax.shard_map(
        on_device, mesh=mesh, in_specs=in_specs, out_specs=out_specs, check_vma=False
    )
```

time: 117 us -> 89 us (0.76)
  Pallas kernels: 56.5 us -> 38.7 us
  waiting for transfers between devices: 20.3 us -> 12.1 us
  starting transfers between devices: 28.9 us -> 33.6 us
  local copies, waits for them, and re-layouts: 5.85 us -> 2.34 us
  between operations: 4.3 us -> 1.7 us
    pallas_call x51 -> x50, Pallas kernels: 53.8 us -> 35.4 us  [call(): pl.pallas_call(kernel, out_shape=tuple((pltpu.VMEM(shape, F32) for shape...]
    ppermute x20, waiting for transfers between devices: 12.6 us -> 4.58 us  [swap(): return lax.ppermute(value, 'sp', pairs)]
    ppermute x20, starting transfers between devices: 22 us -> 25.7 us  [swap(): return lax.ppermute(value, 'sp', pairs)]
    unnamed x14 -> x8, local copies, waits for them, and re-layouts: 2.84 us -> 1.31 us
    another operation x2 -> x0, local copies, waits for them, and re-layouts: 1.38 us -> none  [the longest x1 1.38 us: on_device(): jnp.stack([cos_y, sin_y, jnp.where(at_end, cos_x, 1.0), jnp.where(at_end,...]
    pallas_call x1 -> x2, Pallas kernels: 2.71 us -> 3.35 us  [to_hbm(): pl.pallas_call(kernel, out_shape=(whole, whole), in_specs=specs, out_spec...]
  transfers between devices with their start and end apart: 25 -> 25, of which waited for: 17 -> 16; matrix products, arithmetic and copies ran while one was open for 1% -> 1% of each run, Pallas kernels for 41% -> 42%
where the time goes in v2:
time: 89 us; the launch traced here: 88.8 us
  Pallas kernels  38.7 us (43%)
  starting transfers between devices  33.6 us (38%)
  waiting for transfers between devices  12.1 us (14%)
  local copies, waits for them, and re-layouts  2.34 us (3%)
  between operations  1.7 us (2%)
    pallas_call x50, Pallas kernels, call(): pl.pallas_call(kernel, out_shape=tuple((pltpu.VMEM(shape, F32) for shape...  35.4 us
    ppermute x20, starting transfers between devices, swap(): return lax.ppermute(value, 'sp', pairs)  25.7 us
    ppermute x5, starting transfers between devices, total_over(): other = lax.ppermute(value, axis, [(i, i ^ step) for i in range(count)])  7.88 us
    ppermute x5, waiting for transfers between devices, total_over(): other = lax.ppermute(value, axis, [(i, i ^ step) for i in range(count)])  7.5 us
    ppermute x20, waiting for transfers between devices, swap(): return lax.ppermute(value, 'sp', pairs)  4.58 us
    pallas_call x2, Pallas kernels, to_hbm(): pl.pallas_call(kernel, out_shape=(whole, whole), in_specs=specs, out_spec...  3.35 us
  transfers between devices with their start and end apart: 25, of which 16 were waited for; matrix products, arithmetic and copies ran while one was open for 1% of the time, Pallas kernels for 42%

profile of v2, /device:TPU:0, one launch (start us, length us, event | category | flops | bytes accessed | tf_op | source)
XLA Modules:
  0.0 88.8 jit_solution(12236229181791009960)
XLA Ops:
  3.7 3.1 %collective-permute-start.1 = (f32[4,64,128]{2,1,0:T(8,128)S(1)}, f32[4,64,128]{2,1,0:T(8,128)S(1)}, u32[]{:S(2)}, u32[]{:S(2)}) collective-permute-start(f32[4,64,128]{2,1,0:T(8,128)S(1)} %get-tuple-element.116.mine_ref), channel_id=1, source_target_pairs={{0,1},{1,0},{2,3},{3,2},{4,5},{5,4},{6,7},{7,6},{8,9},{9,8},{10,11... | collective-permute-start | bytes 393224 | tf_op jit(solution)/shard_map/ppermute | solution.py:526
  6.9 2.3 %shard_map.112 = (f32[6,16,64,128]{3,2,1,0:T(8,128)S(1)}, f32[6,16,64,128]{3,2,1,0:T(8,128)S(1)}, f32[2,16,64,128]{3,2,1,0:T(8,128)S(1)}) custom-call(f32[1]{0:T(128)S(6)} %copy.176.peak_hbm, f32[3]{0:T(128)S(1)} %copy-done.2, s32[16,64,128]{2,1,0:T(8,128)} %mat_hbm.1, bf16[6,16,64,128]{3,2,1,0:T(8,128)(2,1)} %bitcast.8, bf16[6,16,64,128]{3,2,1,0:T(8,128)(2,1)} %bitcast.10), custom_call_target="tpu_custom_call" | custom-call | tf_op jit(solution)/shard_map/pallas_call | solution.py:511
  9.5 1.3 %shard_map.113 = (f32[6,16,64,128]{3,2,1,0:T(8,128)S(1)}, f32[6,16,64,128]{3,2,1,0:T(8,128)S(1)}) custom-call(f32[18,8,128]{2,1,0:T(8,128)S(1)} %get-tuple-element.113.p_ref, f32[2,16,64,128]{3,2,1,0:T(8,128)S(1)} %get-tuple-element.114.c_ref, f32[2,16,64,128]{3,2,1,0:T(8,128)S(1)} %broadcast_multiply_fusion.sheet_ref, ...), custom_call_target="tpu_custom_call", output_to_operand_aliasing={{0}: (3, {}), {1}: (4, {})} | custom-call | tf_op jit(solution)/shard_map/pallas_call | solution.py:511
  10.8 1.5 %shard_map.114 = (f32[6,16,64,128]{3,2,1,0:T(8,128)S(1)}, f32[6,16,64,128]{3,2,1,0:T(8,128)S(1)}) custom-call(f32[18,8,128]{2,1,0:T(8,128)S(1)} %get-tuple-element.113.p_ref, f32[2,16,64,128]{3,2,1,0:T(8,128)S(1)} %get-tuple-element.114.c_ref, f32[2,16,64,128]{3,2,1,0:T(8,128)S(1)} %broadcast_multiply_fusion.sheet_ref, ...), custom_call_target="tpu_custom_call", output_to_operand_aliasing={{0}: (3, {}), {1}: (4, {})} | custom-call | tf_op jit(solution)/shard_map/pallas_call | solution.py:511
  12.5 1.9 %collective-permute-start.3 = (f32[4,64,128]{2,1,0:T(8,128)S(1)}, f32[4,64,128]{2,1,0:T(8,128)S(1)}, u32[]{:S(2)}, u32[]{:S(2)}) collective-permute-start(f32[4,64,128]{2,1,0:T(8,128)S(1)} %get-tuple-element.128.mine_ref), channel_id=1, source_target_pairs={{0,1},{1,0},{2,3},{3,2},{4,5},{5,4},{6,7},{7,6},{8,9},{9,8},{10,11... | collective-permute-start | bytes 393224 | tf_op jit(solution)/shard_map/ppermute | solution.py:526
  14.4 1.3 %shard_map.116 = (f32[6,16,64,128]{3,2,1,0:T(8,128)S(1)}, f32[6,16,64,128]{3,2,1,0:T(8,128)S(1)}) custom-call(f32[18,8,128]{2,1,0:T(8,128)S(1)} %get-tuple-element.113.p_ref, f32[2,16,64,128]{3,2,1,0:T(8,128)S(1)} %get-tuple-element.114.c_ref, f32[2,16,64,128]{3,2,1,0:T(8,128)S(1)} %broadcast_multiply_fusion.sheet_ref, ...), custom_call_target="tpu_custom_call", output_to_operand_aliasing={{0}: (3, {}), {1}: (4, {})} | custom-call | tf_op jit(solution)/shard_map/pallas_call | solution.py:511
  16.2 1.5 %shard_map.118 = (f32[6,16,64,128]{3,2,1,0:T(8,128)S(1)}, f32[6,16,64,128]{3,2,1,0:T(8,128)S(1)}) custom-call(f32[18,8,128]{2,1,0:T(8,128)S(1)} %get-tuple-element.113.p_ref, f32[2,16,64,128]{3,2,1,0:T(8,128)S(1)} %get-tuple-element.114.c_ref, f32[2,16,64,128]{3,2,1,0:T(8,128)S(1)} %broadcast_multiply_fusion.sheet_ref, ...), custom_call_target="tpu_custom_call", output_to_operand_aliasing={{0}: (3, {}), {1}: (4, {})} | custom-call | tf_op jit(solution)/shard_map/pallas_call | solution.py:511
  18.3 2.5 %collective-permute-start.5 = (f32[4,64,128]{2,1,0:T(8,128)S(1)}, f32[4,64,128]{2,1,0:T(8,128)S(1)}, u32[]{:S(2)}, u32[]{:S(2)}) collective-permute-start(f32[4,64,128]{2,1,0:T(8,128)S(1)} %get-tuple-element.138.mine_ref), channel_id=1, source_target_pairs={{0,1},{1,0},{2,3},{3,2},{4,5},{5,4},{6,7},{7,6},{8,9},{9,8},{10,11... | collective-permute-start | bytes 393224 | tf_op jit(solution)/shard_map/ppermute | solution.py:526
  20.8 1.3 %shard_map.120 = (f32[6,16,64,128]{3,2,1,0:T(8,128)S(1)}, f32[6,16,64,128]{3,2,1,0:T(8,128)S(1)}) custom-call(f32[18,8,128]{2,1,0:T(8,128)S(1)} %get-tuple-element.113.p_ref, f32[2,16,64,128]{3,2,1,0:T(8,128)S(1)} %get-tuple-element.114.c_ref, f32[2,16,64,128]{3,2,1,0:T(8,128)S(1)} %broadcast_multiply_fusion.sheet_ref, ...), custom_call_target="tpu_custom_call", output_to_operand_aliasing={{0}: (3, {}), {1}: (4, {})} | custom-call | tf_op jit(solution)/shard_map/pallas_call | solution.py:511
  22.3 1.4 %collective-permute-start.4 = (f32[4,64,128]{2,1,0:T(8,128)S(1)}, f32[4,64,128]{2,1,0:T(8,128)S(1)}, u32[]{:S(2)}, u32[]{:S(2)}) collective-permute-start(f32[4,64,128]{2,1,0:T(8,128)S(1)} %get-tuple-element.137.mine_ref), channel_id=1, source_target_pairs={{0,1},{1,0},{2,3},{3,2},{4,5},{5,4},{6,7},{7,6},{8,9},{9,8},{10,11... | collective-permute-start | bytes 393224 | tf_op jit(solution)/shard_map/ppermute | solution.py:526
  23.7 1.5 %shard_map.122 = (f32[6,16,64,128]{3,2,1,0:T(8,128)S(1)}, f32[6,16,64,128]{3,2,1,0:T(8,128)S(1)}) custom-call(f32[18,8,128]{2,1,0:T(8,128)S(1)} %get-tuple-element.113.p_ref, f32[2,16,64,128]{3,2,1,0:T(8,128)S(1)} %get-tuple-element.114.c_ref, f32[2,16,64,128]{3,2,1,0:T(8,128)S(1)} %broadcast_multiply_fusion.sheet_ref, ...), custom_call_target="tpu_custom_call", output_to_operand_aliasing={{0}: (3, {}), {1}: (4, {})} | custom-call | tf_op jit(solution)/shard_map/pallas_call | solution.py:511
  25.4 1.7 %collective-permute-start.7 = (f32[4,64,128]{2,1,0:T(8,128)S(1)}, f32[4,64,128]{2,1,0:T(8,128)S(1)}, u32[]{:S(2)}, u32[]{:S(2)}) collective-permute-start(f32[4,64,128]{2,1,0:T(8,128)S(1)} %get-tuple-element.148.mine_ref), channel_id=1, source_target_pairs={{0,1},{1,0},{2,3},{3,2},{4,5},{5,4},{6,7},{7,6},{8,9},{9,8},{10,11... | collective-permute-start | bytes 393224 | tf_op jit(solution)/shard_map/ppermute | solution.py:526
  27.1 1.3 %shard_map.124 = (f32[6,16,64,128]{3,2,1,0:T(8,128)S(1)}, f32[6,16,64,128]{3,2,1,0:T(8,128)S(1)}) custom-call(f32[18,8,128]{2,1,0:T(8,128)S(1)} %get-tuple-element.113.p_ref, f32[2,16,64,128]{3,2,1,0:T(8,128)S(1)} %get-tuple-element.114.c_ref, f32[2,16,64,128]{3,2,1,0:T(8,128)S(1)} %broadcast_multiply_fusion.sheet_ref, ...), custom_call_target="tpu_custom_call", output_to_operand_aliasing={{0}: (3, {}), {1}: (4, {})} | custom-call | tf_op jit(solution)/shard_map/pallas_call | solution.py:511
  28.5 1.6 %collective-permute-start.6 = (f32[4,64,128]{2,1,0:T(8,128)S(1)}, f32[4,64,128]{2,1,0:T(8,128)S(1)}, u32[]{:S(2)}, u32[]{:S(2)}) collective-permute-start(f32[4,64,128]{2,1,0:T(8,128)S(1)} %get-tuple-element.147.mine_ref), channel_id=1, source_target_pairs={{0,1},{1,0},{2,3},{3,2},{4,5},{5,4},{6,7},{7,6},{8,9},{9,8},{10,11... | collective-permute-start | bytes 393224 | tf_op jit(solution)/shard_map/ppermute | solution.py:526
  30.1 1.5 %shard_map.126 = (f32[6,16,64,128]{3,2,1,0:T(8,128)S(1)}, f32[6,16,64,128]{3,2,1,0:T(8,128)S(1)}) custom-call(f32[18,8,128]{2,1,0:T(8,128)S(1)} %get-tuple-element.113.p_ref, f32[2,16,64,128]{3,2,1,0:T(8,128)S(1)} %get-tuple-element.114.c_ref, f32[2,16,64,128]{3,2,1,0:T(8,128)S(1)} %broadcast_multiply_fusion.sheet_ref, ...), custom_call_target="tpu_custom_call", output_to_operand_aliasing={{0}: (3, {}), {1}: (4, {})} | custom-call | tf_op jit(solution)/shard_map/pallas_call | solution.py:511
  33.0 1.3 %shard_map.128 = (f32[6,16,64,128]{3,2,1,0:T(8,128)S(1)}, f32[6,16,64,128]{3,2,1,0:T(8,128)S(1)}) custom-call(f32[18,8,128]{2,1,0:T(8,128)S(1)} %get-tuple-element.113.p_ref, f32[2,16,64,128]{3,2,1,0:T(8,128)S(1)} %get-tuple-element.114.c_ref, f32[2,16,64,128]{3,2,1,0:T(8,128)S(1)} %broadcast_multiply_fusion.sheet_ref, ...), custom_call_target="tpu_custom_call", output_to_operand_aliasing={{0}: (3, {}), {1}: (4, {})} | custom-call | tf_op jit(solution)/shard_map/pallas_call | solution.py:511
  34.6 1.8 %collective-permute-start.8 = (f32[4,64,128]{2,1,0:T(8,128)S(1)}, f32[4,64,128]{2,1,0:T(8,128)S(1)}, u32[]{:S(2)}, u32[]{:S(2)}) collective-permute-start(f32[4,64,128]{2,1,0:T(8,128)S(1)} %get-tuple-element.157.mine_ref), channel_id=1, source_target_pairs={{0,1},{1,0},{2,3},{3,2},{4,5},{5,4},{6,7},{7,6},{8,9},{9,8},{10,11... | collective-permute-start | bytes 393224 | tf_op jit(solution)/shard_map/ppermute | solution.py:526
  36.4 1.5 %shard_map.130 = (f32[6,16,64,128]{3,2,1,0:T(8,128)S(1)}, f32[6,16,64,128]{3,2,1,0:T(8,128)S(1)}) custom-call(f32[18,8,128]{2,1,0:T(8,128)S(1)} %get-tuple-element.113.p_ref, f32[2,16,64,128]{3,2,1,0:T(8,128)S(1)} %get-tuple-element.114.c_ref, f32[2,16,64,128]{3,2,1,0:T(8,128)S(1)} %broadcast_multiply_fusion.sheet_ref, ...), custom_call_target="tpu_custom_call", output_to_operand_aliasing={{0}: (3, {}), {1}: (4, {})} | custom-call | tf_op jit(solution)/shard_map/pallas_call | solution.py:511
  39.9 1.3 %shard_map.132 = (f32[6,16,64,128]{3,2,1,0:T(8,128)S(1)}, f32[6,16,64,128]{3,2,1,0:T(8,128)S(1)}) custom-call(f32[18,8,128]{2,1,0:T(8,128)S(1)} %get-tuple-element.113.p_ref, f32[2,16,64,128]{3,2,1,0:T(8,128)S(1)} %get-tuple-element.114.c_ref, f32[2,16,64,128]{3,2,1,0:T(8,128)S(1)} %broadcast_multiply_fusion.sheet_ref, ...), custom_call_target="tpu_custom_call", output_to_operand_aliasing={{0}: (3, {}), {1}: (4, {})} | custom-call | tf_op jit(solution)/shard_map/pallas_call | solution.py:511
  42.9 1.5 %shard_map.134 = (f32[6,16,64,128]{3,2,1,0:T(8,128)S(1)}, f32[6,16,64,128]{3,2,1,0:T(8,128)S(1)}) custom-call(f32[18,8,128]{2,1,0:T(8,128)S(1)} %get-tuple-element.113.p_ref, f32[2,16,64,128]{3,2,1,0:T(8,128)S(1)} %get-tuple-element.114.c_ref, f32[2,16,64,128]{3,2,1,0:T(8,128)S(1)} %broadcast_multiply_fusion.sheet_ref, ...), custom_call_target="tpu_custom_call", output_to_operand_aliasing={{0}: (3, {}), {1}: (4, {})} | custom-call | tf_op jit(solution)/shard_map/pallas_call | solution.py:511
  48.5 1.5 %shard_map.138 = (f32[6,16,64,128]{3,2,1,0:T(8,128)S(1)}, f32[6,16,64,128]{3,2,1,0:T(8,128)S(1)}) custom-call(f32[18,8,128]{2,1,0:T(8,128)S(1)} %get-tuple-element.113.p_ref, f32[2,16,64,128]{3,2,1,0:T(8,128)S(1)} %get-tuple-element.114.c_ref, f32[2,16,64,128]{3,2,1,0:T(8,128)S(1)} %broadcast_multiply_fusion.sheet_ref, ...), custom_call_target="tpu_custom_call", output_to_operand_aliasing={{0}: (3, {}), {1}: (4, {})} | custom-call | tf_op jit(solution)/shard_map/pallas_call | solution.py:511
  55.2 1.5 %shard_map.142 = (f32[6,16,64,128]{3,2,1,0:T(8,128)S(1)}, f32[6,16,64,128]{3,2,1,0:T(8,128)S(1)}) custom-call(f32[18,8,128]{2,1,0:T(8,128)S(1)} %get-tuple-element.113.p_ref, f32[2,16,64,128]{3,2,1,0:T(8,128)S(1)} %get-tuple-element.114.c_ref, f32[2,16,64,128]{3,2,1,0:T(8,128)S(1)} %broadcast_multiply_fusion.sheet_ref, ...), custom_call_target="tpu_custom_call", output_to_operand_aliasing={{0}: (3, {}), {1}: (4, {})} | custom-call | tf_op jit(solution)/shard_map/pallas_call | solution.py:511
  60.8 1.5 %shard_map.146 = (f32[6,16,64,128]{3,2,1,0:T(8,128)S(1)}, f32[6,16,64,128]{3,2,1,0:T(8,128)S(1)}) custom-call(f32[18,8,128]{2,1,0:T(8,128)S(1)} %get-tuple-element.113.p_ref, f32[2,16,64,128]{3,2,1,0:T(8,128)S(1)} %get-tuple-element.114.c_ref, f32[2,16,64,128]{3,2,1,0:T(8,128)S(1)} %broadcast_multiply_fusion.sheet_ref, ...), custom_call_target="tpu_custom_call", output_to_operand_aliasing={{0}: (3, {}), {1}: (4, {})} | custom-call | tf_op jit(solution)/shard_map/pallas_call | solution.py:511
  65.2 1.3 %collective-permute-start.18 = (f32[4,64,128]{2,1,0:T(8,128)S(1)}, f32[4,64,128]{2,1,0:T(8,128)S(1)}, u32[]{:S(2)}, u32[]{:S(2)}) collective-permute-start(f32[4,64,128]{2,1,0:T(8,128)S(1)} %get-tuple-element.207.mine_ref), channel_id=1, source_target_pairs={{0,1},{1,0},{2,3},{3,2},{4,5},{5,4},{6,7},{7,6},{8,9},{9,8},{10,11... | collective-permute-start | bytes 393224 | tf_op jit(solution)/shard_map/ppermute | solution.py:526
  66.5 1.5 %shard_map.150 = (f32[6,16,64,128]{3,2,1,0:T(8,128)S(1)}, f32[6,16,64,128]{3,2,1,0:T(8,128)S(1)}) custom-call(f32[18,8,128]{2,1,0:T(8,128)S(1)} %get-tuple-element.113.p_ref, f32[2,16,64,128]{3,2,1,0:T(8,128)S(1)} %get-tuple-element.114.c_ref, f32[2,16,64,128]{3,2,1,0:T(8,128)S(1)} %broadcast_multiply_fusion.sheet_ref, ...), custom_call_target="tpu_custom_call", output_to_operand_aliasing={{0}: (3, {}), {1}: (4, {})} | custom-call | tf_op jit(solution)/shard_map/pallas_call | solution.py:511
  68.5 2.5 %shard_map.156 = (f32[6,16,64,128]{3,2,1,0:T(8,128)}, f32[6,16,64,128]{3,2,1,0:T(8,128)}) custom-call(f32[6,16,64,128]{3,2,1,0:T(8,128)S(1)} %get-tuple-element.210.e_ref.e_in, f32[6,16,64,128]{3,2,1,0:T(8,128)S(1)} %get-tuple-element.212.h_in.h_ref), custom_call_target="tpu_custom_call" | custom-call | tf_op jit(solution)/shard_map/pallas_call | solution.py:553
  72.2 2.9 %collective-permute-done.20.refs_1_ = f32[8,128]{1,0:T(8,128)S(1)} collective-permute-done((f32[8,128]{1,0:T(8,128)S(1)}, f32[8,128]{1,0:T(8,128)S(1)}, u32[]{:S(2)}, u32[]{:S(2)}) %collective-permute-start.20) | collective-permute-done | bytes 4128 | tf_op jit(solution)/shard_map/ppermute | solution.py:542
  76.3 2.1 %collective-permute-start.22 = (f32[8,128]{1,0:T(8,128)S(1)}, f32[8,128]{1,0:T(8,128)S(1)}, u32[]{:S(2)}, u32[]{:S(2)}) collective-permute-start(f32[8,128]{1,0:T(8,128)S(1)} %shard_map.159.refs_0_), channel_id=1, source_target_pairs={{0,4},{2,6},{4,0},{6,2},{8,12},{10,14},{12,8},{14,10},{16,20},{18,... | collective-permute-start | bytes 12296 | tf_op jit(solution)/shard_map/ppermute | solution.py:542
  78.4 1.6 %collective-permute-done.22.refs_1_ = f32[8,128]{1,0:T(8,128)S(1)} collective-permute-done((f32[8,128]{1,0:T(8,128)S(1)}, f32[8,128]{1,0:T(8,128)S(1)}, u32[]{:S(2)}, u32[]{:S(2)}) %collective-permute-start.22) | collective-permute-done | bytes 4128 | tf_op jit(solution)/shard_map/ppermute | solution.py:542
  80.0 2.1 %collective-permute-start.23 = (f32[8,128]{1,0:T(8,128)S(1)}, f32[8,128]{1,0:T(8,128)S(1)}, u32[]{:S(2)}, u32[]{:S(2)}) collective-permute-start(f32[8,128]{1,0:T(8,128)S(1)} %shard_map.160.refs_0_), channel_id=1, source_target_pairs={{0,8},{2,10},{4,12},{6,14},{8,0},{10,2},{12,4},{14,6},{16,24},{18,... | collective-permute-start | bytes 12296 | tf_op jit(solution)/shard_map/ppermute | solution.py:542
  82.1 1.6 %collective-permute-done.23.refs_1_ = f32[8,128]{1,0:T(8,128)S(1)} collective-permute-done((f32[8,128]{1,0:T(8,128)S(1)}, f32[8,128]{1,0:T(8,128)S(1)}, u32[]{:S(2)}, u32[]{:S(2)}) %collective-permute-start.23) | collective-permute-done | bytes 4128 | tf_op jit(solution)/shard_map/ppermute | solution.py:542
  83.7 3.0 %collective-permute-start.24 = (f32[8,128]{1,0:T(8,128)S(1)}, f32[8,128]{1,0:T(8,128)S(1)}, u32[]{:S(2)}, u32[]{:S(2)}) collective-permute-start(f32[8,128]{1,0:T(8,128)S(1)} %shard_map.161.refs_0_), channel_id=1, source_target_pairs={{0,16},{2,18},{4,20},{6,22},{8,24},{10,26},{12,28},{14,30},{16,0},... | collective-permute-start | bytes 12296 | tf_op jit(solution)/shard_map/ppermute | solution.py:542
  (83 shorter events, 31.5 us)
Async XLA Ops:
  0.6 6.2 %copy-start.2 = (f32[3]{0:T(128)S(1)}, f32[3]{0:T(128)}, u32[]{:S(2)}) copy-start(f32[3]{0:T(128)} %perm_hbm.1) | copy-start | bytes 40
  1.3 0.7 copy-start
  2.0 0.7 copy-start.1
  2.6 6.5 %copy-start.3 = (f32[1,2,16,64]{3,2,1,0:T(8,128)S(1)}, f32[1,2,16,64]{3,2,1,0:T(8,128)}, u32[]{:S(2)}) copy-start(f32[1,2,16,64]{3,2,1,0:T(8,128)} %param.12) | copy-start | bytes 24580
  3.7 8.5 %collective-permute-start.1 = (f32[4,64,128]{2,1,0:T(8,128)S(1)}, f32[4,64,128]{2,1,0:T(8,128)S(1)}, u32[]{:S(2)}, u32[]{:S(2)}) collective-permute-start(f32[4,64,128]{2,1,0:T(8,128)S(1)} %get-tuple-element.116.mine_ref), channel_id=1, source_target_pairs={{0,1},{1,0},{2,3},{3,2},{4,5},{5,4},{6,7},{7,6},{8,9},{9,8},{10,11... | collective-permute-start | bytes 393224 | tf_op jit(solution)/shard_map/ppermute | solution.py:526
  6.8 8.9 %collective-permute-start = (f32[4,64,128]{2,1,0:T(8,128)S(1)}, f32[4,64,128]{2,1,0:T(8,128)S(1)}, u32[]{:S(2)}, u32[]{:S(2)}) collective-permute-start(f32[4,64,128]{2,1,0:T(8,128)S(1)} %get-tuple-element.115.mine_ref), channel_id=1, source_target_pairs={{0,1},{1,0},{2,3},{3,2},{4,5},{5,4},{6,7},{7,6},{8,9},{9,8},{10,11... | collective-permute-start | bytes 393224 | tf_op jit(solution)/shard_map/ppermute | solution.py:526
  12.5 5.7 %collective-permute-start.3 = (f32[4,64,128]{2,1,0:T(8,128)S(1)}, f32[4,64,128]{2,1,0:T(8,128)S(1)}, u32[]{:S(2)}, u32[]{:S(2)}) collective-permute-start(f32[4,64,128]{2,1,0:T(8,128)S(1)} %get-tuple-element.128.mine_ref), channel_id=1, source_target_pairs={{0,1},{1,0},{2,3},{3,2},{4,5},{5,4},{6,7},{7,6},{8,9},{9,8},{10,11... | collective-permute-start | bytes 393224 | tf_op jit(solution)/shard_map/ppermute | solution.py:526
  15.8 6.3 %collective-permute-start.2 = (f32[4,64,128]{2,1,0:T(8,128)S(1)}, f32[4,64,128]{2,1,0:T(8,128)S(1)}, u32[]{:S(2)}, u32[]{:S(2)}) collective-permute-start(f32[4,64,128]{2,1,0:T(8,128)S(1)} %get-tuple-element.127.mine_ref), channel_id=1, source_target_pairs={{0,1},{1,0},{2,3},{3,2},{4,5},{5,4},{6,7},{7,6},{8,9},{9,8},{10,11... | collective-permute-start | bytes 393224 | tf_op jit(solution)/shard_map/ppermute | solution.py:526
  18.3 6.8 %collective-permute-start.5 = (f32[4,64,128]{2,1,0:T(8,128)S(1)}, f32[4,64,128]{2,1,0:T(8,128)S(1)}, u32[]{:S(2)}, u32[]{:S(2)}) collective-permute-start(f32[4,64,128]{2,1,0:T(8,128)S(1)} %get-tuple-element.138.mine_ref), channel_id=1, source_target_pairs={{0,1},{1,0},{2,3},{3,2},{4,5},{5,4},{6,7},{7,6},{8,9},{9,8},{10,11... | collective-permute-start | bytes 393224 | tf_op jit(solution)/shard_map/ppermute | solution.py:526
  22.3 6.1 %collective-permute-start.4 = (f32[4,64,128]{2,1,0:T(8,128)S(1)}, f32[4,64,128]{2,1,0:T(8,128)S(1)}, u32[]{:S(2)}, u32[]{:S(2)}) collective-permute-start(f32[4,64,128]{2,1,0:T(8,128)S(1)} %get-tuple-element.137.mine_ref), channel_id=1, source_target_pairs={{0,1},{1,0},{2,3},{3,2},{4,5},{5,4},{6,7},{7,6},{8,9},{9,8},{10,11... | collective-permute-start | bytes 393224 | tf_op jit(solution)/shard_map/ppermute | solution.py:526
  25.4 6.2 %collective-permute-start.7 = (f32[4,64,128]{2,1,0:T(8,128)S(1)}, f32[4,64,128]{2,1,0:T(8,128)S(1)}, u32[]{:S(2)}, u32[]{:S(2)}) collective-permute-start(f32[4,64,128]{2,1,0:T(8,128)S(1)} %get-tuple-element.148.mine_ref), channel_id=1, source_target_pairs={{0,1},{1,0},{2,3},{3,2},{4,5},{5,4},{6,7},{7,6},{8,9},{9,8},{10,11... | collective-permute-start | bytes 393224 | tf_op jit(solution)/shard_map/ppermute | solution.py:526
  28.5 6.0 %collective-permute-start.6 = (f32[4,64,128]{2,1,0:T(8,128)S(1)}, f32[4,64,128]{2,1,0:T(8,128)S(1)}, u32[]{:S(2)}, u32[]{:S(2)}) collective-permute-start(f32[4,64,128]{2,1,0:T(8,128)S(1)} %get-tuple-element.147.mine_ref), channel_id=1, source_target_pairs={{0,1},{1,0},{2,3},{3,2},{4,5},{5,4},{6,7},{7,6},{8,9},{9,8},{10,11... | collective-permute-start | bytes 393224 | tf_op jit(solution)/shard_map/ppermute | solution.py:526
  31.8 6.4 %collective-permute-start.9 = (f32[4,64,128]{2,1,0:T(8,128)S(1)}, f32[4,64,128]{2,1,0:T(8,128)S(1)}, u32[]{:S(2)}, u32[]{:S(2)}) collective-permute-start(f32[4,64,128]{2,1,0:T(8,128)S(1)} %get-tuple-element.158.mine_ref), channel_id=1, source_target_pairs={{0,1},{1,0},{2,3},{3,2},{4,5},{5,4},{6,7},{7,6},{8,9},{9,8},{10,11... | collective-permute-start | bytes 393224 | tf_op jit(solution)/shard_map/ppermute | solution.py:526
  34.6 6.5 %collective-permute-start.8 = (f32[4,64,128]{2,1,0:T(8,128)S(1)}, f32[4,64,128]{2,1,0:T(8,128)S(1)}, u32[]{:S(2)}, u32[]{:S(2)}) collective-permute-start(f32[4,64,128]{2,1,0:T(8,128)S(1)} %get-tuple-element.157.mine_ref), channel_id=1, source_target_pairs={{0,1},{1,0},{2,3},{3,2},{4,5},{5,4},{6,7},{7,6},{8,9},{9,8},{10,11... | collective-permute-start | bytes 393224 | tf_op jit(solution)/shard_map/ppermute | solution.py:526
  38.4 6.0 %collective-permute-start.11 = (f32[4,64,128]{2,1,0:T(8,128)S(1)}, f32[4,64,128]{2,1,0:T(8,128)S(1)}, u32[]{:S(2)}, u32[]{:S(2)}) collective-permute-start(f32[4,64,128]{2,1,0:T(8,128)S(1)} %get-tuple-element.168.mine_ref), channel_id=1, source_target_pairs={{0,1},{1,0},{2,3},{3,2},{4,5},{5,4},{6,7},{7,6},{8,9},{9,8},{10,11... | collective-permute-start | bytes 393224 | tf_op jit(solution)/shard_map/ppermute | solution.py:526
  41.3 6.2 %collective-permute-start.10 = (f32[4,64,128]{2,1,0:T(8,128)S(1)}, f32[4,64,128]{2,1,0:T(8,128)S(1)}, u32[]{:S(2)}, u32[]{:S(2)}) collective-permute-start(f32[4,64,128]{2,1,0:T(8,128)S(1)} %get-tuple-element.167.mine_ref), channel_id=1, source_target_pairs={{0,1},{1,0},{2,3},{3,2},{4,5},{5,4},{6,7},{7,6},{8,9},{9,8},{10,11... | collective-permute-start | bytes 393224 | tf_op jit(solution)/shard_map/ppermute | solution.py:526
  44.5 5.8 %collective-permute-start.13 = (f32[4,64,128]{2,1,0:T(8,128)S(1)}, f32[4,64,128]{2,1,0:T(8,128)S(1)}, u32[]{:S(2)}, u32[]{:S(2)}) collective-permute-start(f32[4,64,128]{2,1,0:T(8,128)S(1)} %get-tuple-element.178.mine_ref), channel_id=1, source_target_pairs={{0,1},{1,0},{2,3},{3,2},{4,5},{5,4},{6,7},{7,6},{8,9},{9,8},{10,11... | collective-permute-start | bytes 393224 | tf_op jit(solution)/shard_map/ppermute | solution.py:526
  47.6 6.4 %collective-permute-start.12 = (f32[4,64,128]{2,1,0:T(8,128)S(1)}, f32[4,64,128]{2,1,0:T(8,128)S(1)}, u32[]{:S(2)}, u32[]{:S(2)}) collective-permute-start(f32[4,64,128]{2,1,0:T(8,128)S(1)} %get-tuple-element.177.mine_ref), channel_id=1, source_target_pairs={{0,1},{1,0},{2,3},{3,2},{4,5},{5,4},{6,7},{7,6},{8,9},{9,8},{10,11... | collective-permute-start | bytes 393224 | tf_op jit(solution)/shard_map/ppermute | solution.py:526
  50.5 6.3 %collective-permute-start.15 = (f32[4,64,128]{2,1,0:T(8,128)S(1)}, f32[4,64,128]{2,1,0:T(8,128)S(1)}, u32[]{:S(2)}, u32[]{:S(2)}) collective-permute-start(f32[4,64,128]{2,1,0:T(8,128)S(1)} %get-tuple-element.188.mine_ref), channel_id=1, source_target_pairs={{0,1},{1,0},{2,3},{3,2},{4,5},{5,4},{6,7},{7,6},{8,9},{9,8},{10,11... | collective-permute-start | bytes 393224 | tf_op jit(solution)/shard_map/ppermute | solution.py:526
  54.3 5.6 %collective-permute-start.14 = (f32[4,64,128]{2,1,0:T(8,128)S(1)}, f32[4,64,128]{2,1,0:T(8,128)S(1)}, u32[]{:S(2)}, u32[]{:S(2)}) collective-permute-start(f32[4,64,128]{2,1,0:T(8,128)S(1)} %get-tuple-element.187.mine_ref), channel_id=1, source_target_pairs={{0,1},{1,0},{2,3},{3,2},{4,5},{5,4},{6,7},{7,6},{8,9},{9,8},{10,11... | collective-permute-start | bytes 393224 | tf_op jit(solution)/shard_map/ppermute | solution.py:526
  57.0 5.6 %collective-permute-start.17 = (f32[4,64,128]{2,1,0:T(8,128)S(1)}, f32[4,64,128]{2,1,0:T(8,128)S(1)}, u32[]{:S(2)}, u32[]{:S(2)}) collective-permute-start(f32[4,64,128]{2,1,0:T(8,128)S(1)} %get-tuple-element.198.mine_ref), channel_id=1, source_target_pairs={{0,1},{1,0},{2,3},{3,2},{4,5},{5,4},{6,7},{7,6},{8,9},{9,8},{10,11... | collective-permute-start | bytes 393224 | tf_op jit(solution)/shard_map/ppermute | solution.py:526
  60.0 5.0 %collective-permute-start.16 = (f32[4,64,128]{2,1,0:T(8,128)S(1)}, f32[4,64,128]{2,1,0:T(8,128)S(1)}, u32[]{:S(2)}, u32[]{:S(2)}) collective-permute-start(f32[4,64,128]{2,1,0:T(8,128)S(1)} %get-tuple-element.197.mine_ref), channel_id=1, source_target_pairs={{0,1},{1,0},{2,3},{3,2},{4,5},{5,4},{6,7},{7,6},{8,9},{9,8},{10,11... | collective-permute-start | bytes 393224 | tf_op jit(solution)/shard_map/ppermute | solution.py:526
  62.8 8.3 %collective-permute-start.19 = (f32[4,64,128]{2,1,0:T(8,128)S(1)}, f32[4,64,128]{2,1,0:T(8,128)S(1)}, u32[]{:S(2)}, u32[]{:S(2)}) collective-permute-start(f32[4,64,128]{2,1,0:T(8,128)S(1)} %get-tuple-element.211.mine_ref), channel_id=1, source_target_pairs={{0,1},{1,0},{2,3},{3,2},{4,5},{5,4},{6,7},{7,6},{8,9},{9,8},{10,11... | collective-permute-start | bytes 393224 | tf_op jit(solution)/shard_map/ppermute | solution.py:526
  65.2 6.0 %collective-permute-start.18 = (f32[4,64,128]{2,1,0:T(8,128)S(1)}, f32[4,64,128]{2,1,0:T(8,128)S(1)}, u32[]{:S(2)}, u32[]{:S(2)}) collective-permute-start(f32[4,64,128]{2,1,0:T(8,128)S(1)} %get-tuple-element.207.mine_ref), channel_id=1, source_target_pairs={{0,1},{1,0},{2,3},{3,2},{4,5},{5,4},{6,7},{7,6},{8,9},{9,8},{10,11... | collective-permute-start | bytes 393224 | tf_op jit(solution)/shard_map/ppermute | solution.py:526
  71.5 3.6 %collective-permute-start.20 = (f32[8,128]{1,0:T(8,128)S(1)}, f32[8,128]{1,0:T(8,128)S(1)}, u32[]{:S(2)}, u32[]{:S(2)}) collective-permute-start(f32[8,128]{1,0:T(8,128)S(1)} %get-tuple-element.221.refs_0_), channel_id=1, source_target_pairs={{0,1},{1,0},{2,3},{3,2},{4,5},{5,4},{6,7},{7,6},{8,9},{9,8},{10,11... | collective-permute-start | bytes 12296 | tf_op jit(solution)/shard_map/ppermute | solution.py:542
  75.1 1.2 %collective-permute-start.21 = (f32[8,128]{1,0:T(8,128)S(1)}, f32[8,128]{1,0:T(8,128)S(1)}, u32[]{:S(2)}, u32[]{:S(2)}) collective-permute-start(f32[8,128]{1,0:T(8,128)S(1)} %shard_map.158.refs_0_), channel_id=1, source_target_pairs={{0,2},{2,0},{4,6},{6,4},{8,10},{10,8},{12,14},{14,12},{16,18},{18,... | collective-permute-start | bytes 12296 | tf_op jit(solution)/shard_map/ppermute | solution.py:542
  76.3 3.7 %collective-permute-start.22 = (f32[8,128]{1,0:T(8,128)S(1)}, f32[8,128]{1,0:T(8,128)S(1)}, u32[]{:S(2)}, u32[]{:S(2)}) collective-permute-start(f32[8,128]{1,0:T(8,128)S(1)} %shard_map.159.refs_0_), channel_id=1, source_target_pairs={{0,4},{2,6},{4,0},{6,2},{8,12},{10,14},{12,8},{14,10},{16,20},{18,... | collective-permute-start | bytes 12296 | tf_op jit(solution)/shard_map/ppermute | solution.py:542
  80.0 3.7 %collective-permute-start.23 = (f32[8,128]{1,0:T(8,128)S(1)}, f32[8,128]{1,0:T(8,128)S(1)}, u32[]{:S(2)}, u32[]{:S(2)}) collective-permute-start(f32[8,128]{1,0:T(8,128)S(1)} %shard_map.160.refs_0_), channel_id=1, source_target_pairs={{0,8},{2,10},{4,12},{6,14},{8,0},{10,2},{12,4},{14,6},{16,24},{18,... | collective-permute-start | bytes 12296 | tf_op jit(solution)/shard_map/ppermute | solution.py:542
  83.7 4.6 %collective-permute-start.24 = (f32[8,128]{1,0:T(8,128)S(1)}, f32[8,128]{1,0:T(8,128)S(1)}, u32[]{:S(2)}, u32[]{:S(2)}) collective-permute-start(f32[8,128]{1,0:T(8,128)S(1)} %shard_map.161.refs_0_), channel_id=1, source_target_pairs={{0,16},{2,18},{4,20},{6,22},{8,24},{10,26},{12,28},{14,30},{16,0},... | collective-permute-start | bytes 12296 | tf_op jit(solution)/shard_map/ppermute | solution.py:542

commit v3 on v2

--- a/solution.py
+++ b/solution.py
@@ -474,30 +474,9 @@
     out_ref[...] = old_ref[...] + monitor(total, slot, scale)
 
 
-def move(pairs, sems):
-    for copy in fetch(pairs, sems):
+def out_kernel(in_ref, out_ref, sems):
+    for copy in fetch([(in_ref, out_ref)], sems):
         copy.wait()
-
-
-def inner_out_kernel(e_ref, h_ref, e_out, h_out, sems):
-    rows = e_ref.shape[1]
-    some, most = pl.ds(1, rows - 2), pl.ds(0, rows - 1)
-    move(
-        [(e_ref.at[:, some], e_out.at[:, some]), (h_ref.at[:, most], h_out.at[:, most])],
-        sems,
-    )
-
-
-def edge_out_kernel(e_ref, h_ref, e_in, h_in, e_out, h_out, sems):
-    end = e_ref.shape[1] - 1
-    move(
-        [
-            (e_ref.at[:, 0], e_out.at[:, 0]),
-            (e_ref.at[:, end], e_out.at[:, end]),
-            (h_ref.at[:, end], h_out.at[:, end]),
-        ],
-        sems,
-    )
 
 
 def add_kernel(scale, *refs):
@@ -548,17 +527,15 @@
     return value
 
 
-def to_hbm(kernel, shape, ins, specs, copies, aliases=None):
-    whole = jax.ShapeDtypeStruct(shape, F32)
+def to_hbm(value):
     return pl.pallas_call(
-        kernel,
-        out_shape=(whole, whole),
-        in_specs=specs,
-        out_specs=(HBM, HBM),
-        input_output_aliases=aliases or {},
-        scratch_shapes=[pltpu.SemaphoreType.DMA((copies,))],
+        out_kernel,
+        out_shape=jax.ShapeDtypeStruct(value.shape, F32),
+        in_specs=[VMEM],
+        out_specs=HBM,
+        scratch_shapes=[pltpu.SemaphoreType.DMA((1,))],
         compiler_params=pltpu.CompilerParams(vmem_limit_bytes=2**20),
-    )(*ins)
+    )(value)
 
 
 def on_device(
@@ -586,10 +563,12 @@
     ]
     electric, magnetic, powers = zip(*results)
     sums = [total_over(power, "sp") for power in powers]
+    electric = [to_hbm(value) for value in electric]
     local = sums[0]
     for other in sums[1:]:
         local = local + other
     mean = total_over(local, "ka", 1.0 / total_points)
+    magnetic = [to_hbm(value) for value in magnetic]
     return (
         jnp.stack(electric),
         jnp.stack(magnetic),
@@ -606,15 +585,15 @@
     edge = (4, width, depth)
     full = (6, rows, width, depth)
     dtype = electric_in.dtype
-    electric_in, magnetic_in, material = (
+    bloch, waveform, permittivity, electric_in, magnetic_in, material = (
         pltpu.with_memory_space_constraint(value, pltpu.HBM)
-        for value in (electric_in, magnetic_in, material)
+        for value in (bloch, waveform, permittivity, electric_in, magnetic_in, material)
     )
     p, *mine = call(
         first_kernel,
         [(DRIVE + steps, SUB, depth), edge, edge],
         [bloch, peak, waveform, electric_in, magnetic_in],
-        [ANY] * 3 + [HBM] * 2,
+        [HBM, ANY] + [HBM] * 3,
         scratch=[
             pltpu.SMEM(bloch.shape, bloch.dtype),
             pltpu.SMEM(peak.shape, F32),
@@ -630,7 +609,7 @@
         widen_kernel,
         [full, full, (2, rows, width, depth)],
         [peak, permittivity, material, electric_in, magnetic_in],
-        [ANY] * 2 + [HBM] * 3,
+        [ANY] + [HBM] * 4,
         scratch=[
             pltpu.SMEM(peak.shape, F32),
             pltpu.SMEM(permittivity.shape, F32),
@@ -677,7 +656,6 @@
             e, h = inner(phase, step + 1, e, h)
     step = steps - 1
     power = measured(None, step, power, e)
-    e_out, h_out = to_hbm(inner_out_kernel, full, [e, h], [VMEM, VMEM], 2)
     e, h = call(
         functools.partial(edge_kernel, 0, step),
         [full, full],
@@ -692,10 +670,7 @@
         [VMEM] * 8,
         {6: 0, 7: 1},
     )
-    e_out, h_out = to_hbm(
-        edge_out_kernel, full, [e, h, e_out, h_out], [VMEM, VMEM, HBM, HBM], 3, {2: 0, 3: 1}
-    )
-    return e_out, h_out, power
+    return e, h, power
 
 
 def solution(mesh):

time: 89 us -> 88.6 us (level)
  local copies, waits for them, and re-layouts: 2.34 us -> 1.03 us
  waiting for transfers between devices: 12.1 us -> 13.4 us
    ppermute x20, waiting for transfers between devices: 4.58 us -> 6.23 us  [swap(): return lax.ppermute(value, 'sp', pairs)]
    unnamed x8 -> x2, local copies, waits for them, and re-layouts: 1.31 us -> 0.01 us
where the time goes in v3:
time: 88.6 us; the launch traced here: 88.5 us
  Pallas kernels  38.7 us (44%)
  starting transfers between devices  33.3 us (38%)
  waiting for transfers between devices  13.4 us (15%)
  between operations  1.66 us (2%)
  local copies, waits for them, and re-layouts  1.03 us (1%)
    pallas_call x50, Pallas kernels, call(): pl.pallas_call(kernel, out_shape=tuple((pltpu.VMEM(shape, F32) for shape...  35.3 us
    ppermute x20, starting transfers between devices, swap(): return lax.ppermute(value, 'sp', pairs)  25.7 us
    ppermute x5, starting transfers between devices, total_over(): other = lax.ppermute(value, axis, [(i, i ^ step) for i in range(count)])  7.62 us
    ppermute x5, waiting for transfers between devices, total_over(): other = lax.ppermute(value, axis, [(i, i ^ step) for i in range(count)])  7.22 us
    ppermute x20, waiting for transfers between devices, swap(): return lax.ppermute(value, 'sp', pairs)  6.23 us
    pallas_call x2, Pallas kernels, to_hbm(): pl.pallas_call(out_kernel, out_shape=jax.ShapeDtypeStruct(value.shape, F3...  3.35 us
  transfers between devices with their start and end apart: 25, of which 16 were waited for; matrix products, arithmetic and copies ran while one was open for 1% of the time, Pallas kernels for 42%

profile of v3, /device:TPU:0, one launch (start us, length us, event | category | flops | bytes accessed | tf_op | source)
XLA Modules:
  0.0 88.5 jit_solution(7729732460477821691)
XLA Ops:
  2.4 3.1 %collective-permute-start.1 = (f32[4,64,128]{2,1,0:T(8,128)S(1)}, f32[4,64,128]{2,1,0:T(8,128)S(1)}, u32[]{:S(2)}, u32[]{:S(2)}) collective-permute-start(f32[4,64,128]{2,1,0:T(8,128)S(1)} %get-tuple-element.112.mine_ref), channel_id=1, source_target_pairs={{0,1},{1,0},{2,3},{3,2},{4,5},{5,4},{6,7},{7,6},{8,9},{9,8},{10,11... | collective-permute-start | bytes 393224 | tf_op jit(solution)/shard_map/ppermute | solution.py:505
  5.5 2.3 %shard_map.112 = (f32[6,16,64,128]{3,2,1,0:T(8,128)S(1)}, f32[6,16,64,128]{3,2,1,0:T(8,128)S(1)}, f32[2,16,64,128]{3,2,1,0:T(8,128)S(1)}) custom-call(f32[1]{0:T(128)S(6)} %copy.172.peak_hbm, f32[3]{0:T(128)} %perm_hbm.1, s32[16,64,128]{2,1,0:T(8,128)} %mat_hbm.1, bf16[6,16,64,128]{3,2,1,0:T(8,128)(2,1)} %bitcast.8, bf16[6,16,64,128]{3,2,1,0:T(8,128)(2,1)} %bitcast.10), custom_call_target="tpu_custom_call" | custom-call | tf_op jit(solution)/shard_map/pallas_call | solution.py:490
  8.2 1.3 %shard_map.113 = (f32[6,16,64,128]{3,2,1,0:T(8,128)S(1)}, f32[6,16,64,128]{3,2,1,0:T(8,128)S(1)}) custom-call(f32[18,8,128]{2,1,0:T(8,128)S(1)} %get-tuple-element.109.p_ref, f32[2,16,64,128]{3,2,1,0:T(8,128)S(1)} %get-tuple-element.110.c_ref, f32[2,16,64,128]{3,2,1,0:T(8,128)S(1)} %broadcast_multiply_fusion.sheet_ref, ...), custom_call_target="tpu_custom_call", output_to_operand_aliasing={{0}: (3, {}), {1}: (4, {})} | custom-call | tf_op jit(solution)/shard_map/pallas_call | solution.py:490
  9.4 1.5 %shard_map.114 = (f32[6,16,64,128]{3,2,1,0:T(8,128)S(1)}, f32[6,16,64,128]{3,2,1,0:T(8,128)S(1)}) custom-call(f32[18,8,128]{2,1,0:T(8,128)S(1)} %get-tuple-element.109.p_ref, f32[2,16,64,128]{3,2,1,0:T(8,128)S(1)} %get-tuple-element.110.c_ref, f32[2,16,64,128]{3,2,1,0:T(8,128)S(1)} %broadcast_multiply_fusion.sheet_ref, ...), custom_call_target="tpu_custom_call", output_to_operand_aliasing={{0}: (3, {}), {1}: (4, {})} | custom-call | tf_op jit(solution)/shard_map/pallas_call | solution.py:490
  11.1 1.9 %collective-permute-start.3 = (f32[4,64,128]{2,1,0:T(8,128)S(1)}, f32[4,64,128]{2,1,0:T(8,128)S(1)}, u32[]{:S(2)}, u32[]{:S(2)}) collective-permute-start(f32[4,64,128]{2,1,0:T(8,128)S(1)} %get-tuple-element.124.mine_ref), channel_id=1, source_target_pairs={{0,1},{1,0},{2,3},{3,2},{4,5},{5,4},{6,7},{7,6},{8,9},{9,8},{10,11... | collective-permute-start | bytes 393224 | tf_op jit(solution)/shard_map/ppermute | solution.py:505
  13.0 1.3 %shard_map.116 = (f32[6,16,64,128]{3,2,1,0:T(8,128)S(1)}, f32[6,16,64,128]{3,2,1,0:T(8,128)S(1)}) custom-call(f32[18,8,128]{2,1,0:T(8,128)S(1)} %get-tuple-element.109.p_ref, f32[2,16,64,128]{3,2,1,0:T(8,128)S(1)} %get-tuple-element.110.c_ref, f32[2,16,64,128]{3,2,1,0:T(8,128)S(1)} %broadcast_multiply_fusion.sheet_ref, ...), custom_call_target="tpu_custom_call", output_to_operand_aliasing={{0}: (3, {}), {1}: (4, {})} | custom-call | tf_op jit(solution)/shard_map/pallas_call | solution.py:490
  14.8 1.5 %shard_map.118 = (f32[6,16,64,128]{3,2,1,0:T(8,128)S(1)}, f32[6,16,64,128]{3,2,1,0:T(8,128)S(1)}) custom-call(f32[18,8,128]{2,1,0:T(8,128)S(1)} %get-tuple-element.109.p_ref, f32[2,16,64,128]{3,2,1,0:T(8,128)S(1)} %get-tuple-element.110.c_ref, f32[2,16,64,128]{3,2,1,0:T(8,128)S(1)} %broadcast_multiply_fusion.sheet_ref, ...), custom_call_target="tpu_custom_call", output_to_operand_aliasing={{0}: (3, {}), {1}: (4, {})} | custom-call | tf_op jit(solution)/shard_map/pallas_call | solution.py:490
  17.0 2.5 %collective-permute-start.5 = (f32[4,64,128]{2,1,0:T(8,128)S(1)}, f32[4,64,128]{2,1,0:T(8,128)S(1)}, u32[]{:S(2)}, u32[]{:S(2)}) collective-permute-start(f32[4,64,128]{2,1,0:T(8,128)S(1)} %get-tuple-element.134.mine_ref), channel_id=1, source_target_pairs={{0,1},{1,0},{2,3},{3,2},{4,5},{5,4},{6,7},{7,6},{8,9},{9,8},{10,11... | collective-permute-start | bytes 393224 | tf_op jit(solution)/shard_map/ppermute | solution.py:505
  19.5 1.3 %shard_map.120 = (f32[6,16,64,128]{3,2,1,0:T(8,128)S(1)}, f32[6,16,64,128]{3,2,1,0:T(8,128)S(1)}) custom-call(f32[18,8,128]{2,1,0:T(8,128)S(1)} %get-tuple-element.109.p_ref, f32[2,16,64,128]{3,2,1,0:T(8,128)S(1)} %get-tuple-element.110.c_ref, f32[2,16,64,128]{3,2,1,0:T(8,128)S(1)} %broadcast_multiply_fusion.sheet_ref, ...), custom_call_target="tpu_custom_call", output_to_operand_aliasing={{0}: (3, {}), {1}: (4, {})} | custom-call | tf_op jit(solution)/shard_map/pallas_call | solution.py:490
  20.9 1.4 %collective-permute-start.4 = (f32[4,64,128]{2,1,0:T(8,128)S(1)}, f32[4,64,128]{2,1,0:T(8,128)S(1)}, u32[]{:S(2)}, u32[]{:S(2)}) collective-permute-start(f32[4,64,128]{2,1,0:T(8,128)S(1)} %get-tuple-element.133.mine_ref), channel_id=1, source_target_pairs={{0,1},{1,0},{2,3},{3,2},{4,5},{5,4},{6,7},{7,6},{8,9},{9,8},{10,11... | collective-permute-start | bytes 393224 | tf_op jit(solution)/shard_map/ppermute | solution.py:505
  22.4 1.5 %shard_map.122 = (f32[6,16,64,128]{3,2,1,0:T(8,128)S(1)}, f32[6,16,64,128]{3,2,1,0:T(8,128)S(1)}) custom-call(f32[18,8,128]{2,1,0:T(8,128)S(1)} %get-tuple-element.109.p_ref, f32[2,16,64,128]{3,2,1,0:T(8,128)S(1)} %get-tuple-element.110.c_ref, f32[2,16,64,128]{3,2,1,0:T(8,128)S(1)} %broadcast_multiply_fusion.sheet_ref, ...), custom_call_target="tpu_custom_call", output_to_operand_aliasing={{0}: (3, {}), {1}: (4, {})} | custom-call | tf_op jit(solution)/shard_map/pallas_call | solution.py:490
  24.0 1.7 %collective-permute-start.7 = (f32[4,64,128]{2,1,0:T(8,128)S(1)}, f32[4,64,128]{2,1,0:T(8,128)S(1)}, u32[]{:S(2)}, u32[]{:S(2)}) collective-permute-start(f32[4,64,128]{2,1,0:T(8,128)S(1)} %get-tuple-element.144.mine_ref), channel_id=1, source_target_pairs={{0,1},{1,0},{2,3},{3,2},{4,5},{5,4},{6,7},{7,6},{8,9},{9,8},{10,11... | collective-permute-start | bytes 393224 | tf_op jit(solution)/shard_map/ppermute | solution.py:505
  25.8 1.3 %shard_map.124 = (f32[6,16,64,128]{3,2,1,0:T(8,128)S(1)}, f32[6,16,64,128]{3,2,1,0:T(8,128)S(1)}) custom-call(f32[18,8,128]{2,1,0:T(8,128)S(1)} %get-tuple-element.109.p_ref, f32[2,16,64,128]{3,2,1,0:T(8,128)S(1)} %get-tuple-element.110.c_ref, f32[2,16,64,128]{3,2,1,0:T(8,128)S(1)} %broadcast_multiply_fusion.sheet_ref, ...), custom_call_target="tpu_custom_call", output_to_operand_aliasing={{0}: (3, {}), {1}: (4, {})} | custom-call | tf_op jit(solution)/shard_map/pallas_call | solution.py:490
  27.2 1.6 %collective-permute-start.6 = (f32[4,64,128]{2,1,0:T(8,128)S(1)}, f32[4,64,128]{2,1,0:T(8,128)S(1)}, u32[]{:S(2)}, u32[]{:S(2)}) collective-permute-start(f32[4,64,128]{2,1,0:T(8,128)S(1)} %get-tuple-element.143.mine_ref), channel_id=1, source_target_pairs={{0,1},{1,0},{2,3},{3,2},{4,5},{5,4},{6,7},{7,6},{8,9},{9,8},{10,11... | collective-permute-start | bytes 393224 | tf_op jit(solution)/shard_map/ppermute | solution.py:505
  28.8 1.5 %shard_map.126 = (f32[6,16,64,128]{3,2,1,0:T(8,128)S(1)}, f32[6,16,64,128]{3,2,1,0:T(8,128)S(1)}) custom-call(f32[18,8,128]{2,1,0:T(8,128)S(1)} %get-tuple-element.109.p_ref, f32[2,16,64,128]{3,2,1,0:T(8,128)S(1)} %get-tuple-element.110.c_ref, f32[2,16,64,128]{3,2,1,0:T(8,128)S(1)} %broadcast_multiply_fusion.sheet_ref, ...), custom_call_target="tpu_custom_call", output_to_operand_aliasing={{0}: (3, {}), {1}: (4, {})} | custom-call | tf_op jit(solution)/shard_map/pallas_call | solution.py:490
  31.6 1.3 %shard_map.128 = (f32[6,16,64,128]{3,2,1,0:T(8,128)S(1)}, f32[6,16,64,128]{3,2,1,0:T(8,128)S(1)}) custom-call(f32[18,8,128]{2,1,0:T(8,128)S(1)} %get-tuple-element.109.p_ref, f32[2,16,64,128]{3,2,1,0:T(8,128)S(1)} %get-tuple-element.110.c_ref, f32[2,16,64,128]{3,2,1,0:T(8,128)S(1)} %broadcast_multiply_fusion.sheet_ref, ...), custom_call_target="tpu_custom_call", output_to_operand_aliasing={{0}: (3, {}), {1}: (4, {})} | custom-call | tf_op jit(solution)/shard_map/pallas_call | solution.py:490
  33.3 1.8 %collective-permute-start.8 = (f32[4,64,128]{2,1,0:T(8,128)S(1)}, f32[4,64,128]{2,1,0:T(8,128)S(1)}, u32[]{:S(2)}, u32[]{:S(2)}) collective-permute-start(f32[4,64,128]{2,1,0:T(8,128)S(1)} %get-tuple-element.153.mine_ref), channel_id=1, source_target_pairs={{0,1},{1,0},{2,3},{3,2},{4,5},{5,4},{6,7},{7,6},{8,9},{9,8},{10,11... | collective-permute-start | bytes 393224 | tf_op jit(solution)/shard_map/ppermute | solution.py:505
  35.1 1.5 %shard_map.130 = (f32[6,16,64,128]{3,2,1,0:T(8,128)S(1)}, f32[6,16,64,128]{3,2,1,0:T(8,128)S(1)}) custom-call(f32[18,8,128]{2,1,0:T(8,128)S(1)} %get-tuple-element.109.p_ref, f32[2,16,64,128]{3,2,1,0:T(8,128)S(1)} %get-tuple-element.110.c_ref, f32[2,16,64,128]{3,2,1,0:T(8,128)S(1)} %broadcast_multiply_fusion.sheet_ref, ...), custom_call_target="tpu_custom_call", output_to_operand_aliasing={{0}: (3, {}), {1}: (4, {})} | custom-call | tf_op jit(solution)/shard_map/pallas_call | solution.py:490
  41.5 1.5 %shard_map.134 = (f32[6,16,64,128]{3,2,1,0:T(8,128)S(1)}, f32[6,16,64,128]{3,2,1,0:T(8,128)S(1)}) custom-call(f32[18,8,128]{2,1,0:T(8,128)S(1)} %get-tuple-element.109.p_ref, f32[2,16,64,128]{3,2,1,0:T(8,128)S(1)} %get-tuple-element.110.c_ref, f32[2,16,64,128]{3,2,1,0:T(8,128)S(1)} %broadcast_multiply_fusion.sheet_ref, ...), custom_call_target="tpu_custom_call", output_to_operand_aliasing={{0}: (3, {}), {1}: (4, {})} | custom-call | tf_op jit(solution)/shard_map/pallas_call | solution.py:490
  47.2 1.5 %shard_map.138 = (f32[6,16,64,128]{3,2,1,0:T(8,128)S(1)}, f32[6,16,64,128]{3,2,1,0:T(8,128)S(1)}) custom-call(f32[18,8,128]{2,1,0:T(8,128)S(1)} %get-tuple-element.109.p_ref, f32[2,16,64,128]{3,2,1,0:T(8,128)S(1)} %get-tuple-element.110.c_ref, f32[2,16,64,128]{3,2,1,0:T(8,128)S(1)} %broadcast_multiply_fusion.sheet_ref, ...), custom_call_target="tpu_custom_call", output_to_operand_aliasing={{0}: (3, {}), {1}: (4, {})} | custom-call | tf_op jit(solution)/shard_map/pallas_call | solution.py:490
  53.9 1.5 %shard_map.142 = (f32[6,16,64,128]{3,2,1,0:T(8,128)S(1)}, f32[6,16,64,128]{3,2,1,0:T(8,128)S(1)}) custom-call(f32[18,8,128]{2,1,0:T(8,128)S(1)} %get-tuple-element.109.p_ref, f32[2,16,64,128]{3,2,1,0:T(8,128)S(1)} %get-tuple-element.110.c_ref, f32[2,16,64,128]{3,2,1,0:T(8,128)S(1)} %broadcast_multiply_fusion.sheet_ref, ...), custom_call_target="tpu_custom_call", output_to_operand_aliasing={{0}: (3, {}), {1}: (4, {})} | custom-call | tf_op jit(solution)/shard_map/pallas_call | solution.py:490
  59.5 1.5 %shard_map.146 = (f32[6,16,64,128]{3,2,1,0:T(8,128)S(1)}, f32[6,16,64,128]{3,2,1,0:T(8,128)S(1)}) custom-call(f32[18,8,128]{2,1,0:T(8,128)S(1)} %get-tuple-element.109.p_ref, f32[2,16,64,128]{3,2,1,0:T(8,128)S(1)} %get-tuple-element.110.c_ref, f32[2,16,64,128]{3,2,1,0:T(8,128)S(1)} %broadcast_multiply_fusion.sheet_ref, ...), custom_call_target="tpu_custom_call", output_to_operand_aliasing={{0}: (3, {}), {1}: (4, {})} | custom-call | tf_op jit(solution)/shard_map/pallas_call | solution.py:490
  65.2 1.5 %shard_map.150 = (f32[6,16,64,128]{3,2,1,0:T(8,128)S(1)}, f32[6,16,64,128]{3,2,1,0:T(8,128)S(1)}) custom-call(f32[18,8,128]{2,1,0:T(8,128)S(1)} %get-tuple-element.109.p_ref, f32[2,16,64,128]{3,2,1,0:T(8,128)S(1)} %get-tuple-element.110.c_ref, f32[2,16,64,128]{3,2,1,0:T(8,128)S(1)} %broadcast_multiply_fusion.sheet_ref, ...), custom_call_target="tpu_custom_call", output_to_operand_aliasing={{0}: (3, {}), {1}: (4, {})} | custom-call | tf_op jit(solution)/shard_map/pallas_call | solution.py:490
  67.3 1.6 %collective-permute-done.18.their_ref = f32[4,64,128]{2,1,0:T(8,128)S(1)} collective-permute-done((f32[4,64,128]{2,1,0:T(8,128)S(1)}, f32[4,64,128]{2,1,0:T(8,128)S(1)}, u32[]{:S(2)}, u32[]{:S(2)}) %collective-permute-start.18) | collective-permute-done | bytes 131104 | tf_op jit(solution)/shard_map/ppermute | solution.py:505
  70.4 2.4 %collective-permute-done.20.refs_1_ = f32[8,128]{1,0:T(8,128)S(1)} collective-permute-done((f32[8,128]{1,0:T(8,128)S(1)}, f32[8,128]{1,0:T(8,128)S(1)}, u32[]{:S(2)}, u32[]{:S(2)}) %collective-permute-start.20) | collective-permute-done | bytes 4128 | tf_op jit(solution)/shard_map/ppermute | solution.py:521
  74.0 1.8 %collective-permute-start.22 = (f32[8,128]{1,0:T(8,128)S(1)}, f32[8,128]{1,0:T(8,128)S(1)}, u32[]{:S(2)}, u32[]{:S(2)}) collective-permute-start(f32[8,128]{1,0:T(8,128)S(1)} %shard_map.159.refs_0_), channel_id=1, source_target_pairs={{0,4},{2,6},{4,0},{6,2},{8,12},{10,14},{12,8},{14,10},{16,20},{18,... | collective-permute-start | bytes 12296 | tf_op jit(solution)/shard_map/ppermute | solution.py:521
  75.8 1.9 %collective-permute-done.22.refs_1_ = f32[8,128]{1,0:T(8,128)S(1)} collective-permute-done((f32[8,128]{1,0:T(8,128)S(1)}, f32[8,128]{1,0:T(8,128)S(1)}, u32[]{:S(2)}, u32[]{:S(2)}) %collective-permute-start.22) | collective-permute-done | bytes 4128 | tf_op jit(solution)/shard_map/ppermute | solution.py:521
  77.6 1.8 %collective-permute-start.23 = (f32[8,128]{1,0:T(8,128)S(1)}, f32[8,128]{1,0:T(8,128)S(1)}, u32[]{:S(2)}, u32[]{:S(2)}) collective-permute-start(f32[8,128]{1,0:T(8,128)S(1)} %shard_map.160.refs_0_), channel_id=1, source_target_pairs={{0,8},{2,10},{4,12},{6,14},{8,0},{10,2},{12,4},{14,6},{16,24},{18,... | collective-permute-start | bytes 12296 | tf_op jit(solution)/shard_map/ppermute | solution.py:521
  79.4 1.8 %collective-permute-done.23.refs_1_ = f32[8,128]{1,0:T(8,128)S(1)} collective-permute-done((f32[8,128]{1,0:T(8,128)S(1)}, f32[8,128]{1,0:T(8,128)S(1)}, u32[]{:S(2)}, u32[]{:S(2)}) %collective-permute-start.23) | collective-permute-done | bytes 4128 | tf_op jit(solution)/shard_map/ppermute | solution.py:521
  81.2 2.9 %collective-permute-start.24 = (f32[8,128]{1,0:T(8,128)S(1)}, f32[8,128]{1,0:T(8,128)S(1)}, u32[]{:S(2)}, u32[]{:S(2)}) collective-permute-start(f32[8,128]{1,0:T(8,128)S(1)} %shard_map.161.refs_0_), channel_id=1, source_target_pairs={{0,16},{2,18},{4,20},{6,22},{8,24},{10,26},{12,28},{14,30},{16,0},... | collective-permute-start | bytes 12296 | tf_op jit(solution)/shard_map/ppermute | solution.py:521
  84.1 1.7 %shard_map.156 = f32[6,16,64,128]{3,2,1,0:T(8,128)} custom-call(f32[6,16,64,128]{3,2,1,0:T(8,128)S(1)} %get-tuple-element.211.in_ref), custom_call_target="tpu_custom_call" | custom-call | tf_op jit(solution)/shard_map/pallas_call | solution.py:531
  85.8 1.7 %shard_map.157 = f32[6,16,64,128]{3,2,1,0:T(8,128)} custom-call(f32[6,16,64,128]{3,2,1,0:T(8,128)S(1)} %get-tuple-element.212.in_ref), custom_call_target="tpu_custom_call" | custom-call | tf_op jit(solution)/shard_map/pallas_call | solution.py:531
  (77 shorter events, 32.2 us)
Async XLA Ops:
  1.3 6.5 %copy-start = (f32[1,2,16,64]{3,2,1,0:T(8,128)S(1)}, f32[1,2,16,64]{3,2,1,0:T(8,128)}, u32[]{:S(2)}) copy-start(f32[1,2,16,64]{3,2,1,0:T(8,128)} %param.12) | copy-start | bytes 24580
  2.4 8.5 %collective-permute-start.1 = (f32[4,64,128]{2,1,0:T(8,128)S(1)}, f32[4,64,128]{2,1,0:T(8,128)S(1)}, u32[]{:S(2)}, u32[]{:S(2)}) collective-permute-start(f32[4,64,128]{2,1,0:T(8,128)S(1)} %get-tuple-element.112.mine_ref), channel_id=1, source_target_pairs={{0,1},{1,0},{2,3},{3,2},{4,5},{5,4},{6,7},{7,6},{8,9},{9,8},{10,11... | collective-permute-start | bytes 393224 | tf_op jit(solution)/shard_map/ppermute | solution.py:505
  5.4 8.9 %collective-permute-start = (f32[4,64,128]{2,1,0:T(8,128)S(1)}, f32[4,64,128]{2,1,0:T(8,128)S(1)}, u32[]{:S(2)}, u32[]{:S(2)}) collective-permute-start(f32[4,64,128]{2,1,0:T(8,128)S(1)} %get-tuple-element.111.mine_ref), channel_id=1, source_target_pairs={{0,1},{1,0},{2,3},{3,2},{4,5},{5,4},{6,7},{7,6},{8,9},{9,8},{10,11... | collective-permute-start | bytes 393224 | tf_op jit(solution)/shard_map/ppermute | solution.py:505
  11.1 5.7 %collective-permute-start.3 = (f32[4,64,128]{2,1,0:T(8,128)S(1)}, f32[4,64,128]{2,1,0:T(8,128)S(1)}, u32[]{:S(2)}, u32[]{:S(2)}) collective-permute-start(f32[4,64,128]{2,1,0:T(8,128)S(1)} %get-tuple-element.124.mine_ref), channel_id=1, source_target_pairs={{0,1},{1,0},{2,3},{3,2},{4,5},{5,4},{6,7},{7,6},{8,9},{9,8},{10,11... | collective-permute-start | bytes 393224 | tf_op jit(solution)/shard_map/ppermute | solution.py:505
  14.5 6.3 %collective-permute-start.2 = (f32[4,64,128]{2,1,0:T(8,128)S(1)}, f32[4,64,128]{2,1,0:T(8,128)S(1)}, u32[]{:S(2)}, u32[]{:S(2)}) collective-permute-start(f32[4,64,128]{2,1,0:T(8,128)S(1)} %get-tuple-element.123.mine_ref), channel_id=1, source_target_pairs={{0,1},{1,0},{2,3},{3,2},{4,5},{5,4},{6,7},{7,6},{8,9},{9,8},{10,11... | collective-permute-start | bytes 393224 | tf_op jit(solution)/shard_map/ppermute | solution.py:505
  17.0 6.8 %collective-permute-start.5 = (f32[4,64,128]{2,1,0:T(8,128)S(1)}, f32[4,64,128]{2,1,0:T(8,128)S(1)}, u32[]{:S(2)}, u32[]{:S(2)}) collective-permute-start(f32[4,64,128]{2,1,0:T(8,128)S(1)} %get-tuple-element.134.mine_ref), channel_id=1, source_target_pairs={{0,1},{1,0},{2,3},{3,2},{4,5},{5,4},{6,7},{7,6},{8,9},{9,8},{10,11... | collective-permute-start | bytes 393224 | tf_op jit(solution)/shard_map/ppermute | solution.py:505
  20.9 6.1 %collective-permute-start.4 = (f32[4,64,128]{2,1,0:T(8,128)S(1)}, f32[4,64,128]{2,1,0:T(8,128)S(1)}, u32[]{:S(2)}, u32[]{:S(2)}) collective-permute-start(f32[4,64,128]{2,1,0:T(8,128)S(1)} %get-tuple-element.133.mine_ref), channel_id=1, source_target_pairs={{0,1},{1,0},{2,3},{3,2},{4,5},{5,4},{6,7},{7,6},{8,9},{9,8},{10,11... | collective-permute-start | bytes 393224 | tf_op jit(solution)/shard_map/ppermute | solution.py:505
  24.0 6.2 %collective-permute-start.7 = (f32[4,64,128]{2,1,0:T(8,128)S(1)}, f32[4,64,128]{2,1,0:T(8,128)S(1)}, u32[]{:S(2)}, u32[]{:S(2)}) collective-permute-start(f32[4,64,128]{2,1,0:T(8,128)S(1)} %get-tuple-element.144.mine_ref), channel_id=1, source_target_pairs={{0,1},{1,0},{2,3},{3,2},{4,5},{5,4},{6,7},{7,6},{8,9},{9,8},{10,11... | collective-permute-start | bytes 393224 | tf_op jit(solution)/shard_map/ppermute | solution.py:505
  27.2 6.0 %collective-permute-start.6 = (f32[4,64,128]{2,1,0:T(8,128)S(1)}, f32[4,64,128]{2,1,0:T(8,128)S(1)}, u32[]{:S(2)}, u32[]{:S(2)}) collective-permute-start(f32[4,64,128]{2,1,0:T(8,128)S(1)} %get-tuple-element.143.mine_ref), channel_id=1, source_target_pairs={{0,1},{1,0},{2,3},{3,2},{4,5},{5,4},{6,7},{7,6},{8,9},{9,8},{10,11... | collective-permute-start | bytes 393224 | tf_op jit(solution)/shard_map/ppermute | solution.py:505
  30.4 6.4 %collective-permute-start.9 = (f32[4,64,128]{2,1,0:T(8,128)S(1)}, f32[4,64,128]{2,1,0:T(8,128)S(1)}, u32[]{:S(2)}, u32[]{:S(2)}) collective-permute-start(f32[4,64,128]{2,1,0:T(8,128)S(1)} %get-tuple-element.154.mine_ref), channel_id=1, source_target_pairs={{0,1},{1,0},{2,3},{3,2},{4,5},{5,4},{6,7},{7,6},{8,9},{9,8},{10,11... | collective-permute-start | bytes 393224 | tf_op jit(solution)/shard_map/ppermute | solution.py:505
  33.3 6.5 %collective-permute-start.8 = (f32[4,64,128]{2,1,0:T(8,128)S(1)}, f32[4,64,128]{2,1,0:T(8,128)S(1)}, u32[]{:S(2)}, u32[]{:S(2)}) collective-permute-start(f32[4,64,128]{2,1,0:T(8,128)S(1)} %get-tuple-element.153.mine_ref), channel_id=1, source_target_pairs={{0,1},{1,0},{2,3},{3,2},{4,5},{5,4},{6,7},{7,6},{8,9},{9,8},{10,11... | collective-permute-start | bytes 393224 | tf_op jit(solution)/shard_map/ppermute | solution.py:505
  37.0 6.0 %collective-permute-start.11 = (f32[4,64,128]{2,1,0:T(8,128)S(1)}, f32[4,64,128]{2,1,0:T(8,128)S(1)}, u32[]{:S(2)}, u32[]{:S(2)}) collective-permute-start(f32[4,64,128]{2,1,0:T(8,128)S(1)} %get-tuple-element.164.mine_ref), channel_id=1, source_target_pairs={{0,1},{1,0},{2,3},{3,2},{4,5},{5,4},{6,7},{7,6},{8,9},{9,8},{10,11... | collective-permute-start | bytes 393224 | tf_op jit(solution)/shard_map/ppermute | solution.py:505
  40.0 6.2 %collective-permute-start.10 = (f32[4,64,128]{2,1,0:T(8,128)S(1)}, f32[4,64,128]{2,1,0:T(8,128)S(1)}, u32[]{:S(2)}, u32[]{:S(2)}) collective-permute-start(f32[4,64,128]{2,1,0:T(8,128)S(1)} %get-tuple-element.163.mine_ref), channel_id=1, source_target_pairs={{0,1},{1,0},{2,3},{3,2},{4,5},{5,4},{6,7},{7,6},{8,9},{9,8},{10,11... | collective-permute-start | bytes 393224 | tf_op jit(solution)/shard_map/ppermute | solution.py:505
  43.2 5.8 %collective-permute-start.13 = (f32[4,64,128]{2,1,0:T(8,128)S(1)}, f32[4,64,128]{2,1,0:T(8,128)S(1)}, u32[]{:S(2)}, u32[]{:S(2)}) collective-permute-start(f32[4,64,128]{2,1,0:T(8,128)S(1)} %get-tuple-element.174.mine_ref), channel_id=1, source_target_pairs={{0,1},{1,0},{2,3},{3,2},{4,5},{5,4},{6,7},{7,6},{8,9},{9,8},{10,11... | collective-permute-start | bytes 393224 | tf_op jit(solution)/shard_map/ppermute | solution.py:505
  46.2 6.4 %collective-permute-start.12 = (f32[4,64,128]{2,1,0:T(8,128)S(1)}, f32[4,64,128]{2,1,0:T(8,128)S(1)}, u32[]{:S(2)}, u32[]{:S(2)}) collective-permute-start(f32[4,64,128]{2,1,0:T(8,128)S(1)} %get-tuple-element.173.mine_ref), channel_id=1, source_target_pairs={{0,1},{1,0},{2,3},{3,2},{4,5},{5,4},{6,7},{7,6},{8,9},{9,8},{10,11... | collective-permute-start | bytes 393224 | tf_op jit(solution)/shard_map/ppermute | solution.py:505
  49.1 6.3 %collective-permute-start.15 = (f32[4,64,128]{2,1,0:T(8,128)S(1)}, f32[4,64,128]{2,1,0:T(8,128)S(1)}, u32[]{:S(2)}, u32[]{:S(2)}) collective-permute-start(f32[4,64,128]{2,1,0:T(8,128)S(1)} %get-tuple-element.184.mine_ref), channel_id=1, source_target_pairs={{0,1},{1,0},{2,3},{3,2},{4,5},{5,4},{6,7},{7,6},{8,9},{9,8},{10,11... | collective-permute-start | bytes 393224 | tf_op jit(solution)/shard_map/ppermute | solution.py:505
  53.0 5.6 %collective-permute-start.14 = (f32[4,64,128]{2,1,0:T(8,128)S(1)}, f32[4,64,128]{2,1,0:T(8,128)S(1)}, u32[]{:S(2)}, u32[]{:S(2)}) collective-permute-start(f32[4,64,128]{2,1,0:T(8,128)S(1)} %get-tuple-element.183.mine_ref), channel_id=1, source_target_pairs={{0,1},{1,0},{2,3},{3,2},{4,5},{5,4},{6,7},{7,6},{8,9},{9,8},{10,11... | collective-permute-start | bytes 393224 | tf_op jit(solution)/shard_map/ppermute | solution.py:505
  55.7 5.6 %collective-permute-start.17 = (f32[4,64,128]{2,1,0:T(8,128)S(1)}, f32[4,64,128]{2,1,0:T(8,128)S(1)}, u32[]{:S(2)}, u32[]{:S(2)}) collective-permute-start(f32[4,64,128]{2,1,0:T(8,128)S(1)} %get-tuple-element.194.mine_ref), channel_id=1, source_target_pairs={{0,1},{1,0},{2,3},{3,2},{4,5},{5,4},{6,7},{7,6},{8,9},{9,8},{10,11... | collective-permute-start | bytes 393224 | tf_op jit(solution)/shard_map/ppermute | solution.py:505
  58.7 5.1 %collective-permute-start.16 = (f32[4,64,128]{2,1,0:T(8,128)S(1)}, f32[4,64,128]{2,1,0:T(8,128)S(1)}, u32[]{:S(2)}, u32[]{:S(2)}) collective-permute-start(f32[4,64,128]{2,1,0:T(8,128)S(1)} %get-tuple-element.193.mine_ref), channel_id=1, source_target_pairs={{0,1},{1,0},{2,3},{3,2},{4,5},{5,4},{6,7},{7,6},{8,9},{9,8},{10,11... | collective-permute-start | bytes 393224 | tf_op jit(solution)/shard_map/ppermute | solution.py:505
  61.4 5.8 %collective-permute-start.19 = (f32[4,64,128]{2,1,0:T(8,128)S(1)}, f32[4,64,128]{2,1,0:T(8,128)S(1)}, u32[]{:S(2)}, u32[]{:S(2)}) collective-permute-start(f32[4,64,128]{2,1,0:T(8,128)S(1)} %get-tuple-element.207.mine_ref), channel_id=1, source_target_pairs={{0,1},{1,0},{2,3},{3,2},{4,5},{5,4},{6,7},{7,6},{8,9},{9,8},{10,11... | collective-permute-start | bytes 393224 | tf_op jit(solution)/shard_map/ppermute | solution.py:505
  63.9 5.0 %collective-permute-start.18 = (f32[4,64,128]{2,1,0:T(8,128)S(1)}, f32[4,64,128]{2,1,0:T(8,128)S(1)}, u32[]{:S(2)}, u32[]{:S(2)}) collective-permute-start(f32[4,64,128]{2,1,0:T(8,128)S(1)} %get-tuple-element.203.mine_ref), channel_id=1, source_target_pairs={{0,1},{1,0},{2,3},{3,2},{4,5},{5,4},{6,7},{7,6},{8,9},{9,8},{10,11... | collective-permute-start | bytes 393224 | tf_op jit(solution)/shard_map/ppermute | solution.py:505
  69.2 3.6 %collective-permute-start.20 = (f32[8,128]{1,0:T(8,128)S(1)}, f32[8,128]{1,0:T(8,128)S(1)}, u32[]{:S(2)}, u32[]{:S(2)}) collective-permute-start(f32[8,128]{1,0:T(8,128)S(1)} %get-tuple-element.213.refs_0_), channel_id=1, source_target_pairs={{0,1},{1,0},{2,3},{3,2},{4,5},{5,4},{6,7},{7,6},{8,9},{9,8},{10,11... | collective-permute-start | bytes 12296 | tf_op jit(solution)/shard_map/ppermute | solution.py:521
  72.8 1.2 %collective-permute-start.21 = (f32[8,128]{1,0:T(8,128)S(1)}, f32[8,128]{1,0:T(8,128)S(1)}, u32[]{:S(2)}, u32[]{:S(2)}) collective-permute-start(f32[8,128]{1,0:T(8,128)S(1)} %shard_map.158.refs_0_), channel_id=1, source_target_pairs={{0,2},{2,0},{4,6},{6,4},{8,10},{10,8},{12,14},{14,12},{16,18},{18,... | collective-permute-start | bytes 12296 | tf_op jit(solution)/shard_map/ppermute | solution.py:521
  74.0 3.6 %collective-permute-start.22 = (f32[8,128]{1,0:T(8,128)S(1)}, f32[8,128]{1,0:T(8,128)S(1)}, u32[]{:S(2)}, u32[]{:S(2)}) collective-permute-start(f32[8,128]{1,0:T(8,128)S(1)} %shard_map.159.refs_0_), channel_id=1, source_target_pairs={{0,4},{2,6},{4,0},{6,2},{8,12},{10,14},{12,8},{14,10},{16,20},{18,... | collective-permute-start | bytes 12296 | tf_op jit(solution)/shard_map/ppermute | solution.py:521
  77.6 3.6 %collective-permute-start.23 = (f32[8,128]{1,0:T(8,128)S(1)}, f32[8,128]{1,0:T(8,128)S(1)}, u32[]{:S(2)}, u32[]{:S(2)}) collective-permute-start(f32[8,128]{1,0:T(8,128)S(1)} %shard_map.160.refs_0_), channel_id=1, source_target_pairs={{0,8},{2,10},{4,12},{6,14},{8,0},{10,2},{12,4},{14,6},{16,24},{18,... | collective-permute-start | bytes 12296 | tf_op jit(solution)/shard_map/ppermute | solution.py:521
  81.2 6.7 %collective-permute-start.24 = (f32[8,128]{1,0:T(8,128)S(1)}, f32[8,128]{1,0:T(8,128)S(1)}, u32[]{:S(2)}, u32[]{:S(2)}) collective-permute-start(f32[8,128]{1,0:T(8,128)S(1)} %shard_map.161.refs_0_), channel_id=1, source_target_pairs={{0,16},{2,18},{4,20},{6,22},{8,24},{10,26},{12,28},{14,30},{16,0},... | collective-permute-start | bytes 12296 | tf_op jit(solution)/shard_map/ppermute | solution.py:521

commit v4 on v3

--- a/solution.py
+++ b/solution.py
@@ -372,7 +372,15 @@
         return carry
 
     lax.fori_loop(lo, lo + skip + 1, start_row, 0)
-    lax.fori_loop(lo + skip, hi - 1, one_row, 0)
+    begin = lo + skip
+    pairs = (hi - 1 - begin) // 2
+
+    def two_rows(pair, carry):
+        one_row(begin + 2 * pair, carry)
+        return one_row(begin + 2 * pair + 1, carry)
+
+    lax.fori_loop(0, pairs, two_rows, 0)
+    lax.fori_loop(begin + 2 * pairs, hi - 1, one_row, 0)
     new_electric(hi - 1)
 
     @pl.when(upper)
@@ -442,10 +450,9 @@
 ):
     edge_step(phase, step, p_ref, c_ref, sheet_ref, mine_ref, their_ref, e_ref, h_ref)
     total = jnp.zeros(old_ref.shape, F32)
-    for x in (0, e_ref.shape[1] - 1):
-        for m in range(4):
-            for tile in load(e_ref, m, x):
-                total = total + tile * tile
+    ends = [load(e_ref, m, x) for x in (0, e_ref.shape[1] - 1) for m in range(4)]
+    for tiles in zip(*ends):
+        total = total + sum(tile * tile for tile in tiles)
     out_ref[...] = old_ref[...] + monitor(total, slot, scale)
 
 
@@ -464,13 +471,15 @@
         lo = jnp.where(upper, middle + (1 - phase), 0)
         hi = jnp.where(upper, rows, middle + phase)
 
-    def one_row(x, total):
-        for m in range(4):
-            for tile in load(e_ref, m, x):
-                total = total + tile * tile
-        return total
-
-    total = lax.fori_loop(lo, hi, one_row, jnp.zeros((SUB, depth), F32))
+    def one_row(x, sums):
+        parts = [load(e_ref, m, x) for m in range(4)]
+        return tuple(
+            total + ((a * a + b * b) + (c * c + d * d))
+            for total, a, b, c, d in zip(sums, *parts)
+        )
+
+    zeros = (jnp.zeros((SUB, depth), F32),) * (e_ref.shape[-2] // SUB)
+    total = sum(lax.fori_loop(lo, hi, one_row, zeros))
     out_ref[...] = old_ref[...] + monitor(total, slot, scale)
 
 
@@ -639,8 +648,7 @@
             [VMEM, VMEM],
         )[0]
 
-    for phase in range(2):
-        e, h = inner(phase, 0, e, h)
+    e, h = inner(0, 0, e, h)
     for step in range(steps - 1):
         for phase in range(2):
             e, h, mine[phase] = call(
@@ -653,6 +661,8 @@
             if (step + 1) % INTERVAL == 0:
                 power = measured(phase, step, power, e)
             their[phase] = swap(mine[phase], phase)
+            if step == phase == 0:
+                e, h = inner(1, 0, e, h)
             e, h = inner(phase, step + 1, e, h)
     step = steps - 1
     power = measured(None, step, power, e)

time: 88.6 us -> 88 us (level)
  waiting for transfers between devices: 13.4 us -> 22.9 us
  starting transfers between devices: 33.3 us -> 25.9 us
  Pallas kernels: 38.7 us -> 36.1 us
    ppermute x20, waiting for transfers between devices: 6.23 us -> 15.8 us  [swap(): return lax.ppermute(value, 'sp', pairs)]
    ppermute x20, starting transfers between devices: 25.7 us -> 18 us  [swap(): return lax.ppermute(value, 'sp', pairs)]
    pallas_call x50, Pallas kernels: 35.3 us -> 32.7 us  [call(): pl.pallas_call(kernel, out_shape=tuple((pltpu.VMEM(shape, F32) for shape...]
  transfers between devices with their start and end apart: 25 -> 25, of which waited for: 16 -> 20; matrix products, arithmetic and copies ran while one was open for 1% -> 1% of each run, Pallas kernels for 42% -> 40%
where the time goes in v4:
time: 88 us; the launch traced here: 87.8 us
  Pallas kernels  36.1 us (41%)
  starting transfers between devices  25.9 us (29%)
  waiting for transfers between devices  22.9 us (26%)
  between operations  1.63 us (2%)
  local copies, waits for them, and re-layouts  1.04 us (1%)
    pallas_call x50, Pallas kernels, call(): pl.pallas_call(kernel, out_shape=tuple((pltpu.VMEM(shape, F32) for shape...  32.7 us
    ppermute x20, starting transfers between devices, swap(): return lax.ppermute(value, 'sp', pairs)  18 us
    ppermute x20, waiting for transfers between devices, swap(): return lax.ppermute(value, 'sp', pairs)  15.8 us
    ppermute x5, starting transfers between devices, total_over(): other = lax.ppermute(value, axis, [(i, i ^ step) for i in range(count)])  7.87 us
    ppermute x5, waiting for transfers between devices, total_over(): other = lax.ppermute(value, axis, [(i, i ^ step) for i in range(count)])  7.06 us
    pallas_call x2, Pallas kernels, to_hbm(): pl.pallas_call(out_kernel, out_shape=jax.ShapeDtypeStruct(value.shape, F3...  3.35 us
  transfers between devices with their start and end apart: 25, of which 20 were waited for; matrix products, arithmetic and copies ran while one was open for 1% of the time, Pallas kernels for 40%

profile of v4, /device:TPU:0, one launch (start us, length us, event | category | flops | bytes accessed | tf_op | source)
XLA Modules:
  0.0 87.8 jit_solution(9450469504275819593)
XLA Ops:
  2.4 3.1 %collective-permute-start.1 = (f32[4,64,128]{2,1,0:T(8,128)S(1)}, f32[4,64,128]{2,1,0:T(8,128)S(1)}, u32[]{:S(2)}, u32[]{:S(2)}) collective-permute-start(f32[4,64,128]{2,1,0:T(8,128)S(1)} %get-tuple-element.112.mine_ref), channel_id=1, source_target_pairs={{0,1},{1,0},{2,3},{3,2},{4,5},{5,4},{6,7},{7,6},{8,9},{9,8},{10,11... | collective-permute-start | bytes 393224 | tf_op jit(solution)/shard_map/ppermute | solution.py:514
  5.5 2.3 %shard_map.112 = (f32[6,16,64,128]{3,2,1,0:T(8,128)S(1)}, f32[6,16,64,128]{3,2,1,0:T(8,128)S(1)}, f32[2,16,64,128]{3,2,1,0:T(8,128)S(1)}) custom-call(f32[1]{0:T(128)S(6)} %copy.172.peak_hbm, f32[3]{0:T(128)} %perm_hbm.1, s32[16,64,128]{2,1,0:T(8,128)} %mat_hbm.1, bf16[6,16,64,128]{3,2,1,0:T(8,128)(2,1)} %bitcast.8, bf16[6,16,64,128]{3,2,1,0:T(8,128)(2,1)} %bitcast.10), custom_call_target="tpu_custom_call" | custom-call | tf_op jit(solution)/shard_map/pallas_call | solution.py:499
  8.2 1.2 %shard_map.113 = (f32[6,16,64,128]{3,2,1,0:T(8,128)S(1)}, f32[6,16,64,128]{3,2,1,0:T(8,128)S(1)}) custom-call(f32[18,8,128]{2,1,0:T(8,128)S(1)} %get-tuple-element.109.p_ref, f32[2,16,64,128]{3,2,1,0:T(8,128)S(1)} %get-tuple-element.110.c_ref, f32[2,16,64,128]{3,2,1,0:T(8,128)S(1)} %broadcast_multiply_fusion.sheet_ref, ...), custom_call_target="tpu_custom_call", output_to_operand_aliasing={{0}: (3, {}), {1}: (4, {})} | custom-call | tf_op jit(solution)/shard_map/pallas_call | solution.py:499
  10.0 2.0 %collective-permute-start.3 = (f32[4,64,128]{2,1,0:T(8,128)S(1)}, f32[4,64,128]{2,1,0:T(8,128)S(1)}, u32[]{:S(2)}, u32[]{:S(2)}) collective-permute-start(f32[4,64,128]{2,1,0:T(8,128)S(1)} %get-tuple-element.124.mine_ref), channel_id=1, source_target_pairs={{0,1},{1,0},{2,3},{3,2},{4,5},{5,4},{6,7},{7,6},{8,9},{9,8},{10,11... | collective-permute-start | bytes 393224 | tf_op jit(solution)/shard_map/ppermute | solution.py:514
  12.0 1.4 %shard_map.115 = (f32[6,16,64,128]{3,2,1,0:T(8,128)S(1)}, f32[6,16,64,128]{3,2,1,0:T(8,128)S(1)}) custom-call(f32[18,8,128]{2,1,0:T(8,128)S(1)} %get-tuple-element.109.p_ref, f32[2,16,64,128]{3,2,1,0:T(8,128)S(1)} %get-tuple-element.110.c_ref, f32[2,16,64,128]{3,2,1,0:T(8,128)S(1)} %broadcast_multiply_fusion.sheet_ref, ...), custom_call_target="tpu_custom_call", output_to_operand_aliasing={{0}: (3, {}), {1}: (4, {})} | custom-call | tf_op jit(solution)/shard_map/pallas_call | solution.py:499
  13.4 1.2 %shard_map.116 = (f32[6,16,64,128]{3,2,1,0:T(8,128)S(1)}, f32[6,16,64,128]{3,2,1,0:T(8,128)S(1)}) custom-call(f32[18,8,128]{2,1,0:T(8,128)S(1)} %get-tuple-element.109.p_ref, f32[2,16,64,128]{3,2,1,0:T(8,128)S(1)} %get-tuple-element.110.c_ref, f32[2,16,64,128]{3,2,1,0:T(8,128)S(1)} %broadcast_multiply_fusion.sheet_ref, ...), custom_call_target="tpu_custom_call", output_to_operand_aliasing={{0}: (3, {}), {1}: (4, {})} | custom-call | tf_op jit(solution)/shard_map/pallas_call | solution.py:499
  14.8 1.4 %shard_map.118 = (f32[6,16,64,128]{3,2,1,0:T(8,128)S(1)}, f32[6,16,64,128]{3,2,1,0:T(8,128)S(1)}) custom-call(f32[18,8,128]{2,1,0:T(8,128)S(1)} %get-tuple-element.109.p_ref, f32[2,16,64,128]{3,2,1,0:T(8,128)S(1)} %get-tuple-element.110.c_ref, f32[2,16,64,128]{3,2,1,0:T(8,128)S(1)} %broadcast_multiply_fusion.sheet_ref, ...), custom_call_target="tpu_custom_call", output_to_operand_aliasing={{0}: (3, {}), {1}: (4, {})} | custom-call | tf_op jit(solution)/shard_map/pallas_call | solution.py:499
  16.4 1.9 %collective-permute-start.5 = (f32[4,64,128]{2,1,0:T(8,128)S(1)}, f32[4,64,128]{2,1,0:T(8,128)S(1)}, u32[]{:S(2)}, u32[]{:S(2)}) collective-permute-start(f32[4,64,128]{2,1,0:T(8,128)S(1)} %get-tuple-element.134.mine_ref), channel_id=1, source_target_pairs={{0,1},{1,0},{2,3},{3,2},{4,5},{5,4},{6,7},{7,6},{8,9},{9,8},{10,11... | collective-permute-start | bytes 393224 | tf_op jit(solution)/shard_map/ppermute | solution.py:514
  20.8 1.4 %shard_map.122 = (f32[6,16,64,128]{3,2,1,0:T(8,128)S(1)}, f32[6,16,64,128]{3,2,1,0:T(8,128)S(1)}) custom-call(f32[18,8,128]{2,1,0:T(8,128)S(1)} %get-tuple-element.109.p_ref, f32[2,16,64,128]{3,2,1,0:T(8,128)S(1)} %get-tuple-element.110.c_ref, f32[2,16,64,128]{3,2,1,0:T(8,128)S(1)} %broadcast_multiply_fusion.sheet_ref, ...), custom_call_target="tpu_custom_call", output_to_operand_aliasing={{0}: (3, {}), {1}: (4, {})} | custom-call | tf_op jit(solution)/shard_map/pallas_call | solution.py:499
  22.2 1.2 %collective-permute-done.5.their_ref = f32[4,64,128]{2,1,0:T(8,128)S(1)} collective-permute-done((f32[4,64,128]{2,1,0:T(8,128)S(1)}, f32[4,64,128]{2,1,0:T(8,128)S(1)}, u32[]{:S(2)}, u32[]{:S(2)}) %collective-permute-start.5) | collective-permute-done | bytes 131104 | tf_op jit(solution)/shard_map/ppermute | solution.py:514
  27.5 1.4 %shard_map.126 = (f32[6,16,64,128]{3,2,1,0:T(8,128)S(1)}, f32[6,16,64,128]{3,2,1,0:T(8,128)S(1)}) custom-call(f32[18,8,128]{2,1,0:T(8,128)S(1)} %get-tuple-element.109.p_ref, f32[2,16,64,128]{3,2,1,0:T(8,128)S(1)} %get-tuple-element.110.c_ref, f32[2,16,64,128]{3,2,1,0:T(8,128)S(1)} %broadcast_multiply_fusion.sheet_ref, ...), custom_call_target="tpu_custom_call", output_to_operand_aliasing={{0}: (3, {}), {1}: (4, {})} | custom-call | tf_op jit(solution)/shard_map/pallas_call | solution.py:499
  31.3 1.4 %collective-permute-done.6.their_ref = f32[4,64,128]{2,1,0:T(8,128)S(1)} collective-permute-done((f32[4,64,128]{2,1,0:T(8,128)S(1)}, f32[4,64,128]{2,1,0:T(8,128)S(1)}, u32[]{:S(2)}, u32[]{:S(2)}) %collective-permute-start.6) | collective-permute-done | bytes 131104 | tf_op jit(solution)/shard_map/ppermute | solution.py:514
  33.7 1.4 %shard_map.130 = (f32[6,16,64,128]{3,2,1,0:T(8,128)S(1)}, f32[6,16,64,128]{3,2,1,0:T(8,128)S(1)}) custom-call(f32[18,8,128]{2,1,0:T(8,128)S(1)} %get-tuple-element.109.p_ref, f32[2,16,64,128]{3,2,1,0:T(8,128)S(1)} %get-tuple-element.110.c_ref, f32[2,16,64,128]{3,2,1,0:T(8,128)S(1)} %broadcast_multiply_fusion.sheet_ref, ...), custom_call_target="tpu_custom_call", output_to_operand_aliasing={{0}: (3, {}), {1}: (4, {})} | custom-call | tf_op jit(solution)/shard_map/pallas_call | solution.py:499
  35.1 1.4 %collective-permute-done.9.their_ref = f32[4,64,128]{2,1,0:T(8,128)S(1)} collective-permute-done((f32[4,64,128]{2,1,0:T(8,128)S(1)}, f32[4,64,128]{2,1,0:T(8,128)S(1)}, u32[]{:S(2)}, u32[]{:S(2)}) %collective-permute-start.9) | collective-permute-done | bytes 131104 | tf_op jit(solution)/shard_map/ppermute | solution.py:514
  39.4 1.3 %collective-permute-start.10 = (f32[4,64,128]{2,1,0:T(8,128)S(1)}, f32[4,64,128]{2,1,0:T(8,128)S(1)}, u32[]{:S(2)}, u32[]{:S(2)}) collective-permute-start(f32[4,64,128]{2,1,0:T(8,128)S(1)} %get-tuple-element.163.mine_ref), channel_id=1, source_target_pairs={{0,1},{1,0},{2,3},{3,2},{4,5},{5,4},{6,7},{7,6},{8,9},{9,8},{10,11... | collective-permute-start | bytes 393224 | tf_op jit(solution)/shard_map/ppermute | solution.py:514
  40.9 1.4 %shard_map.134 = (f32[6,16,64,128]{3,2,1,0:T(8,128)S(1)}, f32[6,16,64,128]{3,2,1,0:T(8,128)S(1)}) custom-call(f32[18,8,128]{2,1,0:T(8,128)S(1)} %get-tuple-element.109.p_ref, f32[2,16,64,128]{3,2,1,0:T(8,128)S(1)} %get-tuple-element.110.c_ref, f32[2,16,64,128]{3,2,1,0:T(8,128)S(1)} %broadcast_multiply_fusion.sheet_ref, ...), custom_call_target="tpu_custom_call", output_to_operand_aliasing={{0}: (3, {}), {1}: (4, {})} | custom-call | tf_op jit(solution)/shard_map/pallas_call | solution.py:499
  44.3 1.3 %collective-permute-done.10.their_ref = f32[4,64,128]{2,1,0:T(8,128)S(1)} collective-permute-done((f32[4,64,128]{2,1,0:T(8,128)S(1)}, f32[4,64,128]{2,1,0:T(8,128)S(1)}, u32[]{:S(2)}, u32[]{:S(2)}) %collective-permute-start.10) | collective-permute-done | bytes 131104 | tf_op jit(solution)/shard_map/ppermute | solution.py:514
  46.3 1.4 %shard_map.138 = (f32[6,16,64,128]{3,2,1,0:T(8,128)S(1)}, f32[6,16,64,128]{3,2,1,0:T(8,128)S(1)}) custom-call(f32[18,8,128]{2,1,0:T(8,128)S(1)} %get-tuple-element.109.p_ref, f32[2,16,64,128]{3,2,1,0:T(8,128)S(1)} %get-tuple-element.110.c_ref, f32[2,16,64,128]{3,2,1,0:T(8,128)S(1)} %broadcast_multiply_fusion.sheet_ref, ...), custom_call_target="tpu_custom_call", output_to_operand_aliasing={{0}: (3, {}), {1}: (4, {})} | custom-call | tf_op jit(solution)/shard_map/pallas_call | solution.py:499
  52.5 1.4 %shard_map.142 = (f32[6,16,64,128]{3,2,1,0:T(8,128)S(1)}, f32[6,16,64,128]{3,2,1,0:T(8,128)S(1)}) custom-call(f32[18,8,128]{2,1,0:T(8,128)S(1)} %get-tuple-element.109.p_ref, f32[2,16,64,128]{3,2,1,0:T(8,128)S(1)} %get-tuple-element.110.c_ref, f32[2,16,64,128]{3,2,1,0:T(8,128)S(1)} %broadcast_multiply_fusion.sheet_ref, ...), custom_call_target="tpu_custom_call", output_to_operand_aliasing={{0}: (3, {}), {1}: (4, {})} | custom-call | tf_op jit(solution)/shard_map/pallas_call | solution.py:499
  53.8 1.3 %collective-permute-done.15.their_ref = f32[4,64,128]{2,1,0:T(8,128)S(1)} collective-permute-done((f32[4,64,128]{2,1,0:T(8,128)S(1)}, f32[4,64,128]{2,1,0:T(8,128)S(1)}, u32[]{:S(2)}, u32[]{:S(2)}) %collective-permute-start.15) | collective-permute-done | bytes 131104 | tf_op jit(solution)/shard_map/ppermute | solution.py:514
  59.0 1.4 %shard_map.146 = (f32[6,16,64,128]{3,2,1,0:T(8,128)S(1)}, f32[6,16,64,128]{3,2,1,0:T(8,128)S(1)}) custom-call(f32[18,8,128]{2,1,0:T(8,128)S(1)} %get-tuple-element.109.p_ref, f32[2,16,64,128]{3,2,1,0:T(8,128)S(1)} %get-tuple-element.110.c_ref, f32[2,16,64,128]{3,2,1,0:T(8,128)S(1)} %broadcast_multiply_fusion.sheet_ref, ...), custom_call_target="tpu_custom_call", output_to_operand_aliasing={{0}: (3, {}), {1}: (4, {})} | custom-call | tf_op jit(solution)/shard_map/pallas_call | solution.py:499
  63.2 1.2 %collective-permute-start.18 = (f32[4,64,128]{2,1,0:T(8,128)S(1)}, f32[4,64,128]{2,1,0:T(8,128)S(1)}, u32[]{:S(2)}, u32[]{:S(2)}) collective-permute-start(f32[4,64,128]{2,1,0:T(8,128)S(1)} %get-tuple-element.203.mine_ref), channel_id=1, source_target_pairs={{0,1},{1,0},{2,3},{3,2},{4,5},{5,4},{6,7},{7,6},{8,9},{9,8},{10,11... | collective-permute-start | bytes 393224 | tf_op jit(solution)/shard_map/ppermute | solution.py:514
  64.4 1.4 %shard_map.150 = (f32[6,16,64,128]{3,2,1,0:T(8,128)S(1)}, f32[6,16,64,128]{3,2,1,0:T(8,128)S(1)}) custom-call(f32[18,8,128]{2,1,0:T(8,128)S(1)} %get-tuple-element.109.p_ref, f32[2,16,64,128]{3,2,1,0:T(8,128)S(1)} %get-tuple-element.110.c_ref, f32[2,16,64,128]{3,2,1,0:T(8,128)S(1)} %broadcast_multiply_fusion.sheet_ref, ...), custom_call_target="tpu_custom_call", output_to_operand_aliasing={{0}: (3, {}), {1}: (4, {})} | custom-call | tf_op jit(solution)/shard_map/pallas_call | solution.py:499
  66.2 2.0 %collective-permute-done.18.their_ref = f32[4,64,128]{2,1,0:T(8,128)S(1)} collective-permute-done((f32[4,64,128]{2,1,0:T(8,128)S(1)}, f32[4,64,128]{2,1,0:T(8,128)S(1)}, u32[]{:S(2)}, u32[]{:S(2)}) %collective-permute-start.18) | collective-permute-done | bytes 131104 | tf_op jit(solution)/shard_map/ppermute | solution.py:514
  69.6 2.5 %collective-permute-done.20.refs_1_ = f32[8,128]{1,0:T(8,128)S(1)} collective-permute-done((f32[8,128]{1,0:T(8,128)S(1)}, f32[8,128]{1,0:T(8,128)S(1)}, u32[]{:S(2)}, u32[]{:S(2)}) %collective-permute-start.20) | collective-permute-done | bytes 4128 | tf_op jit(solution)/shard_map/ppermute | solution.py:530
  73.3 1.8 %collective-permute-start.22 = (f32[8,128]{1,0:T(8,128)S(1)}, f32[8,128]{1,0:T(8,128)S(1)}, u32[]{:S(2)}, u32[]{:S(2)}) collective-permute-start(f32[8,128]{1,0:T(8,128)S(1)} %shard_map.159.refs_0_), channel_id=1, source_target_pairs={{0,4},{2,6},{4,0},{6,2},{8,12},{10,14},{12,8},{14,10},{16,20},{18,... | collective-permute-start | bytes 12296 | tf_op jit(solution)/shard_map/ppermute | solution.py:530
  75.1 1.8 %collective-permute-done.22.refs_1_ = f32[8,128]{1,0:T(8,128)S(1)} collective-permute-done((f32[8,128]{1,0:T(8,128)S(1)}, f32[8,128]{1,0:T(8,128)S(1)}, u32[]{:S(2)}, u32[]{:S(2)}) %collective-permute-start.22) | collective-permute-done | bytes 4128 | tf_op jit(solution)/shard_map/ppermute | solution.py:530
  76.9 1.9 %collective-permute-start.23 = (f32[8,128]{1,0:T(8,128)S(1)}, f32[8,128]{1,0:T(8,128)S(1)}, u32[]{:S(2)}, u32[]{:S(2)}) collective-permute-start(f32[8,128]{1,0:T(8,128)S(1)} %shard_map.160.refs_0_), channel_id=1, source_target_pairs={{0,8},{2,10},{4,12},{6,14},{8,0},{10,2},{12,4},{14,6},{16,24},{18,... | collective-permute-start | bytes 12296 | tf_op jit(solution)/shard_map/ppermute | solution.py:530
  78.8 1.7 %collective-permute-done.23.refs_1_ = f32[8,128]{1,0:T(8,128)S(1)} collective-permute-done((f32[8,128]{1,0:T(8,128)S(1)}, f32[8,128]{1,0:T(8,128)S(1)}, u32[]{:S(2)}, u32[]{:S(2)}) %collective-permute-start.23) | collective-permute-done | bytes 4128 | tf_op jit(solution)/shard_map/ppermute | solution.py:530
  80.5 2.9 %collective-permute-start.24 = (f32[8,128]{1,0:T(8,128)S(1)}, f32[8,128]{1,0:T(8,128)S(1)}, u32[]{:S(2)}, u32[]{:S(2)}) collective-permute-start(f32[8,128]{1,0:T(8,128)S(1)} %shard_map.161.refs_0_), channel_id=1, source_target_pairs={{0,16},{2,18},{4,20},{6,22},{8,24},{10,26},{12,28},{14,30},{16,0},... | collective-permute-start | bytes 12296 | tf_op jit(solution)/shard_map/ppermute | solution.py:530
  83.4 1.7 %shard_map.156 = f32[6,16,64,128]{3,2,1,0:T(8,128)} custom-call(f32[6,16,64,128]{3,2,1,0:T(8,128)S(1)} %get-tuple-element.211.in_ref), custom_call_target="tpu_custom_call" | custom-call | tf_op jit(solution)/shard_map/pallas_call | solution.py:540
  85.1 1.7 %shard_map.157 = f32[6,16,64,128]{3,2,1,0:T(8,128)} custom-call(f32[6,16,64,128]{3,2,1,0:T(8,128)S(1)} %get-tuple-element.212.in_ref), custom_call_target="tpu_custom_call" | custom-call | tf_op jit(solution)/shard_map/pallas_call | solution.py:540
  (77 shorter events, 33.8 us)
Async XLA Ops:
  1.3 6.5 %copy-start = (f32[1,2,16,64]{3,2,1,0:T(8,128)S(1)}, f32[1,2,16,64]{3,2,1,0:T(8,128)}, u32[]{:S(2)}) copy-start(f32[1,2,16,64]{3,2,1,0:T(8,128)} %param.12) | copy-start | bytes 24580
  2.4 7.4 %collective-permute-start.1 = (f32[4,64,128]{2,1,0:T(8,128)S(1)}, f32[4,64,128]{2,1,0:T(8,128)S(1)}, u32[]{:S(2)}, u32[]{:S(2)}) collective-permute-start(f32[4,64,128]{2,1,0:T(8,128)S(1)} %get-tuple-element.112.mine_ref), channel_id=1, source_target_pairs={{0,1},{1,0},{2,3},{3,2},{4,5},{5,4},{6,7},{7,6},{8,9},{9,8},{10,11... | collective-permute-start | bytes 393224 | tf_op jit(solution)/shard_map/ppermute | solution.py:514
  5.4 9.1 %collective-permute-start = (f32[4,64,128]{2,1,0:T(8,128)S(1)}, f32[4,64,128]{2,1,0:T(8,128)S(1)}, u32[]{:S(2)}, u32[]{:S(2)}) collective-permute-start(f32[4,64,128]{2,1,0:T(8,128)S(1)} %get-tuple-element.111.mine_ref), channel_id=1, source_target_pairs={{0,1},{1,0},{2,3},{3,2},{4,5},{5,4},{6,7},{7,6},{8,9},{9,8},{10,11... | collective-permute-start | bytes 393224 | tf_op jit(solution)/shard_map/ppermute | solution.py:514
  10.0 6.2 %collective-permute-start.3 = (f32[4,64,128]{2,1,0:T(8,128)S(1)}, f32[4,64,128]{2,1,0:T(8,128)S(1)}, u32[]{:S(2)}, u32[]{:S(2)}) collective-permute-start(f32[4,64,128]{2,1,0:T(8,128)S(1)} %get-tuple-element.124.mine_ref), channel_id=1, source_target_pairs={{0,1},{1,0},{2,3},{3,2},{4,5},{5,4},{6,7},{7,6},{8,9},{9,8},{10,11... | collective-permute-start | bytes 393224 | tf_op jit(solution)/shard_map/ppermute | solution.py:514
  14.7 5.9 %collective-permute-start.2 = (f32[4,64,128]{2,1,0:T(8,128)S(1)}, f32[4,64,128]{2,1,0:T(8,128)S(1)}, u32[]{:S(2)}, u32[]{:S(2)}) collective-permute-start(f32[4,64,128]{2,1,0:T(8,128)S(1)} %get-tuple-element.123.mine_ref), channel_id=1, source_target_pairs={{0,1},{1,0},{2,3},{3,2},{4,5},{5,4},{6,7},{7,6},{8,9},{9,8},{10,11... | collective-permute-start | bytes 393224 | tf_op jit(solution)/shard_map/ppermute | solution.py:514
  16.4 7.0 %collective-permute-start.5 = (f32[4,64,128]{2,1,0:T(8,128)S(1)}, f32[4,64,128]{2,1,0:T(8,128)S(1)}, u32[]{:S(2)}, u32[]{:S(2)}) collective-permute-start(f32[4,64,128]{2,1,0:T(8,128)S(1)} %get-tuple-element.134.mine_ref), channel_id=1, source_target_pairs={{0,1},{1,0},{2,3},{3,2},{4,5},{5,4},{6,7},{7,6},{8,9},{9,8},{10,11... | collective-permute-start | bytes 393224 | tf_op jit(solution)/shard_map/ppermute | solution.py:514
  20.8 5.4 %collective-permute-start.4 = (f32[4,64,128]{2,1,0:T(8,128)S(1)}, f32[4,64,128]{2,1,0:T(8,128)S(1)}, u32[]{:S(2)}, u32[]{:S(2)}) collective-permute-start(f32[4,64,128]{2,1,0:T(8,128)S(1)} %get-tuple-element.133.mine_ref), channel_id=1, source_target_pairs={{0,1},{1,0},{2,3},{3,2},{4,5},{5,4},{6,7},{7,6},{8,9},{9,8},{10,11... | collective-permute-start | bytes 393224 | tf_op jit(solution)/shard_map/ppermute | solution.py:514
  23.6 6.2 %collective-permute-start.7 = (f32[4,64,128]{2,1,0:T(8,128)S(1)}, f32[4,64,128]{2,1,0:T(8,128)S(1)}, u32[]{:S(2)}, u32[]{:S(2)}) collective-permute-start(f32[4,64,128]{2,1,0:T(8,128)S(1)} %get-tuple-element.144.mine_ref), channel_id=1, source_target_pairs={{0,1},{1,0},{2,3},{3,2},{4,5},{5,4},{6,7},{7,6},{8,9},{9,8},{10,11... | collective-permute-start | bytes 393224 | tf_op jit(solution)/shard_map/ppermute | solution.py:514
  26.3 6.4 %collective-permute-start.6 = (f32[4,64,128]{2,1,0:T(8,128)S(1)}, f32[4,64,128]{2,1,0:T(8,128)S(1)}, u32[]{:S(2)}, u32[]{:S(2)}) collective-permute-start(f32[4,64,128]{2,1,0:T(8,128)S(1)} %get-tuple-element.143.mine_ref), channel_id=1, source_target_pairs={{0,1},{1,0},{2,3},{3,2},{4,5},{5,4},{6,7},{7,6},{8,9},{9,8},{10,11... | collective-permute-start | bytes 393224 | tf_op jit(solution)/shard_map/ppermute | solution.py:514
  30.0 6.4 %collective-permute-start.9 = (f32[4,64,128]{2,1,0:T(8,128)S(1)}, f32[4,64,128]{2,1,0:T(8,128)S(1)}, u32[]{:S(2)}, u32[]{:S(2)}) collective-permute-start(f32[4,64,128]{2,1,0:T(8,128)S(1)} %get-tuple-element.154.mine_ref), channel_id=1, source_target_pairs={{0,1},{1,0},{2,3},{3,2},{4,5},{5,4},{6,7},{7,6},{8,9},{9,8},{10,11... | collective-permute-start | bytes 393224 | tf_op jit(solution)/shard_map/ppermute | solution.py:514
  32.9 6.4 %collective-permute-start.8 = (f32[4,64,128]{2,1,0:T(8,128)S(1)}, f32[4,64,128]{2,1,0:T(8,128)S(1)}, u32[]{:S(2)}, u32[]{:S(2)}) collective-permute-start(f32[4,64,128]{2,1,0:T(8,128)S(1)} %get-tuple-element.153.mine_ref), channel_id=1, source_target_pairs={{0,1},{1,0},{2,3},{3,2},{4,5},{5,4},{6,7},{7,6},{8,9},{9,8},{10,11... | collective-permute-start | bytes 393224 | tf_op jit(solution)/shard_map/ppermute | solution.py:514
  36.7 5.6 %collective-permute-start.11 = (f32[4,64,128]{2,1,0:T(8,128)S(1)}, f32[4,64,128]{2,1,0:T(8,128)S(1)}, u32[]{:S(2)}, u32[]{:S(2)}) collective-permute-start(f32[4,64,128]{2,1,0:T(8,128)S(1)} %get-tuple-element.164.mine_ref), channel_id=1, source_target_pairs={{0,1},{1,0},{2,3},{3,2},{4,5},{5,4},{6,7},{7,6},{8,9},{9,8},{10,11... | collective-permute-start | bytes 393224 | tf_op jit(solution)/shard_map/ppermute | solution.py:514
  39.4 6.3 %collective-permute-start.10 = (f32[4,64,128]{2,1,0:T(8,128)S(1)}, f32[4,64,128]{2,1,0:T(8,128)S(1)}, u32[]{:S(2)}, u32[]{:S(2)}) collective-permute-start(f32[4,64,128]{2,1,0:T(8,128)S(1)} %get-tuple-element.163.mine_ref), channel_id=1, source_target_pairs={{0,1},{1,0},{2,3},{3,2},{4,5},{5,4},{6,7},{7,6},{8,9},{9,8},{10,11... | collective-permute-start | bytes 393224 | tf_op jit(solution)/shard_map/ppermute | solution.py:514
  42.5 6.1 %collective-permute-start.13 = (f32[4,64,128]{2,1,0:T(8,128)S(1)}, f32[4,64,128]{2,1,0:T(8,128)S(1)}, u32[]{:S(2)}, u32[]{:S(2)}) collective-permute-start(f32[4,64,128]{2,1,0:T(8,128)S(1)} %get-tuple-element.174.mine_ref), channel_id=1, source_target_pairs={{0,1},{1,0},{2,3},{3,2},{4,5},{5,4},{6,7},{7,6},{8,9},{9,8},{10,11... | collective-permute-start | bytes 393224 | tf_op jit(solution)/shard_map/ppermute | solution.py:514
  45.8 6.2 %collective-permute-start.12 = (f32[4,64,128]{2,1,0:T(8,128)S(1)}, f32[4,64,128]{2,1,0:T(8,128)S(1)}, u32[]{:S(2)}, u32[]{:S(2)}) collective-permute-start(f32[4,64,128]{2,1,0:T(8,128)S(1)} %get-tuple-element.173.mine_ref), channel_id=1, source_target_pairs={{0,1},{1,0},{2,3},{3,2},{4,5},{5,4},{6,7},{7,6},{8,9},{9,8},{10,11... | collective-permute-start | bytes 393224 | tf_op jit(solution)/shard_map/ppermute | solution.py:514
  48.7 6.4 %collective-permute-start.15 = (f32[4,64,128]{2,1,0:T(8,128)S(1)}, f32[4,64,128]{2,1,0:T(8,128)S(1)}, u32[]{:S(2)}, u32[]{:S(2)}) collective-permute-start(f32[4,64,128]{2,1,0:T(8,128)S(1)} %get-tuple-element.184.mine_ref), channel_id=1, source_target_pairs={{0,1},{1,0},{2,3},{3,2},{4,5},{5,4},{6,7},{7,6},{8,9},{9,8},{10,11... | collective-permute-start | bytes 393224 | tf_op jit(solution)/shard_map/ppermute | solution.py:514
  52.1 5.8 %collective-permute-start.14 = (f32[4,64,128]{2,1,0:T(8,128)S(1)}, f32[4,64,128]{2,1,0:T(8,128)S(1)}, u32[]{:S(2)}, u32[]{:S(2)}) collective-permute-start(f32[4,64,128]{2,1,0:T(8,128)S(1)} %get-tuple-element.183.mine_ref), channel_id=1, source_target_pairs={{0,1},{1,0},{2,3},{3,2},{4,5},{5,4},{6,7},{7,6},{8,9},{9,8},{10,11... | collective-permute-start | bytes 393224 | tf_op jit(solution)/shard_map/ppermute | solution.py:514
  55.3 5.3 %collective-permute-start.17 = (f32[4,64,128]{2,1,0:T(8,128)S(1)}, f32[4,64,128]{2,1,0:T(8,128)S(1)}, u32[]{:S(2)}, u32[]{:S(2)}) collective-permute-start(f32[4,64,128]{2,1,0:T(8,128)S(1)} %get-tuple-element.194.mine_ref), channel_id=1, source_target_pairs={{0,1},{1,0},{2,3},{3,2},{4,5},{5,4},{6,7},{7,6},{8,9},{9,8},{10,11... | collective-permute-start | bytes 393224 | tf_op jit(solution)/shard_map/ppermute | solution.py:514
  58.0 5.1 %collective-permute-start.16 = (f32[4,64,128]{2,1,0:T(8,128)S(1)}, f32[4,64,128]{2,1,0:T(8,128)S(1)}, u32[]{:S(2)}, u32[]{:S(2)}) collective-permute-start(f32[4,64,128]{2,1,0:T(8,128)S(1)} %get-tuple-element.193.mine_ref), channel_id=1, source_target_pairs={{0,1},{1,0},{2,3},{3,2},{4,5},{5,4},{6,7},{7,6},{8,9},{9,8},{10,11... | collective-permute-start | bytes 393224 | tf_op jit(solution)/shard_map/ppermute | solution.py:514
  60.8 5.3 %collective-permute-start.19 = (f32[4,64,128]{2,1,0:T(8,128)S(1)}, f32[4,64,128]{2,1,0:T(8,128)S(1)}, u32[]{:S(2)}, u32[]{:S(2)}) collective-permute-start(f32[4,64,128]{2,1,0:T(8,128)S(1)} %get-tuple-element.207.mine_ref), channel_id=1, source_target_pairs={{0,1},{1,0},{2,3},{3,2},{4,5},{5,4},{6,7},{7,6},{8,9},{9,8},{10,11... | collective-permute-start | bytes 393224 | tf_op jit(solution)/shard_map/ppermute | solution.py:514
  63.2 5.0 %collective-permute-start.18 = (f32[4,64,128]{2,1,0:T(8,128)S(1)}, f32[4,64,128]{2,1,0:T(8,128)S(1)}, u32[]{:S(2)}, u32[]{:S(2)}) collective-permute-start(f32[4,64,128]{2,1,0:T(8,128)S(1)} %get-tuple-element.203.mine_ref), channel_id=1, source_target_pairs={{0,1},{1,0},{2,3},{3,2},{4,5},{5,4},{6,7},{7,6},{8,9},{9,8},{10,11... | collective-permute-start | bytes 393224 | tf_op jit(solution)/shard_map/ppermute | solution.py:514
  68.5 3.6 %collective-permute-start.20 = (f32[8,128]{1,0:T(8,128)S(1)}, f32[8,128]{1,0:T(8,128)S(1)}, u32[]{:S(2)}, u32[]{:S(2)}) collective-permute-start(f32[8,128]{1,0:T(8,128)S(1)} %get-tuple-element.213.refs_0_), channel_id=1, source_target_pairs={{0,1},{1,0},{2,3},{3,2},{4,5},{5,4},{6,7},{7,6},{8,9},{9,8},{10,11... | collective-permute-start | bytes 12296 | tf_op jit(solution)/shard_map/ppermute | solution.py:530
  72.1 1.2 %collective-permute-start.21 = (f32[8,128]{1,0:T(8,128)S(1)}, f32[8,128]{1,0:T(8,128)S(1)}, u32[]{:S(2)}, u32[]{:S(2)}) collective-permute-start(f32[8,128]{1,0:T(8,128)S(1)} %shard_map.158.refs_0_), channel_id=1, source_target_pairs={{0,2},{2,0},{4,6},{6,4},{8,10},{10,8},{12,14},{14,12},{16,18},{18,... | collective-permute-start | bytes 12296 | tf_op jit(solution)/shard_map/ppermute | solution.py:530
  73.3 3.6 %collective-permute-start.22 = (f32[8,128]{1,0:T(8,128)S(1)}, f32[8,128]{1,0:T(8,128)S(1)}, u32[]{:S(2)}, u32[]{:S(2)}) collective-permute-start(f32[8,128]{1,0:T(8,128)S(1)} %shard_map.159.refs_0_), channel_id=1, source_target_pairs={{0,4},{2,6},{4,0},{6,2},{8,12},{10,14},{12,8},{14,10},{16,20},{18,... | collective-permute-start | bytes 12296 | tf_op jit(solution)/shard_map/ppermute | solution.py:530
  76.9 3.6 %collective-permute-start.23 = (f32[8,128]{1,0:T(8,128)S(1)}, f32[8,128]{1,0:T(8,128)S(1)}, u32[]{:S(2)}, u32[]{:S(2)}) collective-permute-start(f32[8,128]{1,0:T(8,128)S(1)} %shard_map.160.refs_0_), channel_id=1, source_target_pairs={{0,8},{2,10},{4,12},{6,14},{8,0},{10,2},{12,4},{14,6},{16,24},{18,... | collective-permute-start | bytes 12296 | tf_op jit(solution)/shard_map/ppermute | solution.py:530
  80.5 6.8 %collective-permute-start.24 = (f32[8,128]{1,0:T(8,128)S(1)}, f32[8,128]{1,0:T(8,128)S(1)}, u32[]{:S(2)}, u32[]{:S(2)}) collective-permute-start(f32[8,128]{1,0:T(8,128)S(1)} %shard_map.161.refs_0_), channel_id=1, source_target_pairs={{0,16},{2,18},{4,20},{6,22},{8,24},{10,26},{12,28},{14,30},{16,0},... | collective-permute-start | bytes 12296 | tf_op jit(solution)/shard_map/ppermute | solution.py:530
